TPU v7x, 32 devices: a whole 2x2x4 slice. The times are simulated.
32 devices in a mesh: section: 2 (over x), replica: 2 (over core), shard: 8 (over z, y).
Axes of the slice: x: 2, y: 2, z: 4, core: 2. Of those that a mesh axis runs over, the one named last changes fastest.
Arguments:
- tokens: int32 [32, 320], P('replica'), may hold values from 0 to 31999
- parents: int32 [32, 10], P('replica'), may hold values from 0 to 8, as said below
- loss_positions: int32 [32, 16], P('replica'), may hold values from 0 to 319
- targets: int32 [32, 16], P('replica'), may hold values from 0 to 31999
- teacher_index: int32 [32, 16, 64], P('replica'), may hold values from 0 to 31999
- teacher_probability: float32 [32, 16, 64], P('replica'), may hold values from 0.001 to 0.05
- step_count: int32 [], replicated, may hold values from 1 to 20
- embed_table: float32 [32000, 768], P(('replica', 'shard')), may hold values from -0.4330127 to 0.4330127
- table_first: float32 [32000, 768], P(('replica', 'shard')), may hold values from -9.1552734e-05 to 9.1552734e-05
- table_second: float32 [32000, 768], P(('replica', 'shard')), may hold values from 3.2273243e-13 to 3.2273243e-11
- attention_in: float32 [2, 768, 2304], P('section', 'shard'), may hold values from -0.21875 to 0.21875
- attention_in_first: float32 [2, 768, 2304], P('section', 'shard'), may hold values from -9.1552734e-05 to 9.1552734e-05
- attention_in_second: float32 [2, 768, 2304], P('section', 'shard'), may hold values from 3.2273243e-13 to 3.2273243e-11
- attention_out: float32 [2, 768, 768], P('section', 'shard'), may hold values from -0.4375 to 0.4375
- attention_out_first: float32 [2, 768, 768], P('section', 'shard'), may hold values from -9.1552734e-05 to 9.1552734e-05
- attention_out_second: float32 [2, 768, 768], P('section', 'shard'), may hold values from 3.2273243e-13 to 3.2273243e-11
- feedforward_in: float32 [2, 768, 4096], P('section', 'shard'), may hold values from -0.21875 to 0.21875
- feedforward_in_first: float32 [2, 768, 4096], P('section', 'shard'), may hold values from -9.1552734e-05 to 9.1552734e-05
- feedforward_in_second: float32 [2, 768, 4096], P('section', 'shard'), may hold values from 3.2273243e-13 to 3.2273243e-11
- feedforward_out: float32 [2, 2048, 768], P('section', 'shard'), may hold values from -0.125 to 0.125
- feedforward_out_first: float32 [2, 2048, 768], P('section', 'shard'), may hold values from -9.1552734e-05 to 9.1552734e-05
- feedforward_out_second: float32 [2, 2048, 768], P('section', 'shard'), may hold values from 3.2273243e-13 to 3.2273243e-11
- forget_gate: float32 [2, 769, 12], replicated
- forget_first: float32 [2, 769, 12], replicated, may hold values from -9.1552734e-05 to 9.1552734e-05
- forget_second: float32 [2, 769, 12], replicated, may hold values from 3.2273243e-13 to 3.2273243e-11
- norm_gains: float32 [5, 768], replicated, may hold values from 0.5 to 1.5
- gains_first: float32 [5, 768], replicated, may hold values from -9.1552734e-05 to 9.1552734e-05
- gains_second: float32 [5, 768], replicated, may hold values from 3.2273243e-13 to 3.2273243e-11
Outputs:
- new_table: float32 [32000, 768], P(('replica', 'shard'))
- new_table_first: float32 [32000, 768], P(('replica', 'shard'))
- new_table_second: float32 [32000, 768], P(('replica', 'shard'))
- new_attention_in: float32 [2, 768, 2304], P('section', 'shard')
- new_attention_in_first: float32 [2, 768, 2304], P('section', 'shard')
- new_attention_in_second: float32 [2, 768, 2304], P('section', 'shard')
- new_attention_out: float32 [2, 768, 768], P('section', 'shard')
- new_attention_out_first: float32 [2, 768, 768], P('section', 'shard')
- new_attention_out_second: float32 [2, 768, 768], P('section', 'shard')
- new_feedforward_in: float32 [2, 768, 4096], P('section', 'shard')
- new_feedforward_in_first: float32 [2, 768, 4096], P('section', 'shard')
- new_feedforward_in_second: float32 [2, 768, 4096], P('section', 'shard')
- new_feedforward_out: float32 [2, 2048, 768], P('section', 'shard')
- new_feedforward_out_first: float32 [2, 2048, 768], P('section', 'shard')
- new_feedforward_out_second: float32 [2, 2048, 768], P('section', 'shard')
- new_forget_gate: float32 [2, 769, 12], replicated
- new_forget_first: float32 [2, 769, 12], replicated
- new_forget_second: float32 [2, 769, 12], replicated
- new_gains: float32 [5, 768], replicated
- new_gains_first: float32 [5, 768], replicated
- new_gains_second: float32 [5, 768], replicated
- tensor_norms: float32 [16, 2], replicated
- grad_norm: float32 [], replicated
- loss: float32 [], replicated
Inputs may be any that keep to these rules, and one draw needn't show every extreme that they name: parents[t, 0] = 0 marks the root; for s >= 1, parents[t, s] < s; parents[t, 9] = 8.
All inputs are finite; a program needn't handle non-finite values.
Results may differ from a plain program's by a relative error of at most 0.028.
Values may be sent and summed in bfloat16 or wider, within the bound.
A program may use at most 320 MiB of HBM per device.

v0:
```python
from functools import partial

import jax
import jax.numpy as jnp
from jax import lax
from jax.sharding import PartitionSpec as P

eps_norm = 1e-06
beta_first = 0.9
beta_second = 0.999
adam_eps = 1e-10
decay_rate = 0.01
learn_rate = 0.2
clip_factor = 8.0
highest = lax.Precision.HIGHEST
masked_score = -1e30


def passed_along(value, axis, steps):
    count = lax.axis_size(axis)
    initial, last = (max(0, -steps), min(count, count - steps))
    return lax.ppermute(value, axis, [(source, source + steps) for source in range(initial, last)])


def combined_all(part, axis, combine):
    gathered = jax.tree.map(lambda a: lax.all_gather(a, axis), part)

    def take(source):
        return jax.tree.map(lambda a: lax.dynamic_index_in_dim(a, source, 0, False), gathered)

    return lax.fori_loop(
        1, lax.axis_size(axis), lambda source, state: combine(state, take(source)), take(0)
    )


def lower(values):
    return values.astype(jnp.bfloat16)


def product(left, right):
    return jnp.dot(left, right, preferred_element_type=jnp.float32)


def product_left(left, right):
    return lax.dot_general(
        left, right, (((0,), (0,)), ((), ())), preferred_element_type=jnp.float32
    )


def product_right(left, right):
    return lax.dot_general(
        left, right, (((1,), (1,)), ((), ())), preferred_element_type=jnp.float32
    )


def rms_forward(values, gain):
    inverse = lax.rsqrt(jnp.mean(values * values, axis=-1, keepdims=True) + eps_norm)
    normed = values * inverse
    return (normed * gain, normed, inverse)


def rms_backward(grad_out, normed, inverse, gain):
    grad_normed = grad_out * gain
    grad_in = inverse * (
        grad_normed - normed * jnp.mean(grad_normed * normed, axis=-1, keepdims=True)
    )
    return (grad_in, jnp.sum(grad_out * normed, axis=0))


def path_mask(parent_row, tree_len):
    seg_count = parent_row.shape[0]
    seglen = tree_len // seg_count
    seg_order = jnp.arange(seg_count, dtype=jnp.int32)
    parent_hot = ((parent_row[:, None] == seg_order[None, :]) & (seg_order[:, None] >= 1)).astype(
        jnp.float32
    )
    identity = jnp.eye(seg_count, dtype=jnp.float32)

    def extend(step_index, reached):
        return jnp.minimum(1.0, identity + jnp.dot(parent_hot, reached, precision=highest))

    reached = lax.fori_loop(0, seg_count, extend, identity)
    strict = reached - identity
    seg_of = jnp.arange(tree_len, dtype=jnp.int32) // seglen
    seg_hot = (seg_of[:, None] == seg_order[None, :]).astype(jnp.float32)
    ancestor = jnp.dot(jnp.dot(seg_hot, strict, precision=highest), seg_hot.T, precision=highest)
    places = jnp.arange(tree_len, dtype=jnp.int32)
    inside = (seg_of[:, None] == seg_of[None, :]) & (places[None, :] <= places[:, None])
    return ancestor + inside.astype(jnp.float32)


def attention_scores(queries, keys_all, cumul):
    scale = queries.shape[-1] ** (-0.5)
    scores = (
        jnp.einsum("ihd,jhd->hij", queries, keys_all, preferred_element_type=jnp.float32) * scale
    )
    cumul_heads = cumul.T
    return scores + cumul_heads[:, :, None] - cumul_heads[:, None, :]


def layer_forward(values, allowed, weights):
    (
        weight_in,
        weight_out,
        weight_up,
        weight_down,
        forget_proj,
        forget_bias,
        gain_attention,
        gain_feedforward,
    ) = weights
    tree_len, width = values.shape
    head_count = forget_proj.shape[1]
    normed_out_a, normed_a, inverse_a = rms_forward(values, gain_attention)
    act_a = lower(normed_out_a)
    mixed = lower(product(act_a, weight_in))
    forget_logit = product(act_a, forget_proj) + forget_bias
    cumul = jnp.dot(allowed, jax.nn.log_sigmoid(forget_logit), precision=highest)
    parts = mixed.reshape(tree_len, 3, head_count, width // head_count)
    scores = attention_scores(parts[:, 0], parts[:, 1], cumul)
    scores = jnp.where(allowed[None] > 0, scores, masked_score)
    score_max = jnp.max(scores, axis=-1, keepdims=True)
    exp_scores = jnp.exp(scores - score_max)
    score_sum = jnp.sum(exp_scores, axis=-1, keepdims=True)
    probs = lower(exp_scores / score_sum)
    log_total = score_max + jnp.log(score_sum)
    attended = jnp.einsum("hij,jhd->ihd", probs, parts[:, 2], preferred_element_type=jnp.float32)
    attended = lower(attended.reshape(tree_len, width))
    middle = values + product(attended, weight_out)
    normed_out_b, normed_b, inverse_b = rms_forward(middle, gain_feedforward)
    act_b = lower(normed_out_b)
    gate_up = product(act_b, weight_up)
    half_width = gate_up.shape[1] // 2
    hidden = lower(jax.nn.silu(gate_up[:, :half_width]) * gate_up[:, half_width:])
    output = middle + product(hidden, weight_down)
    return (output, (values, mixed, forget_logit, log_total, attended, middle, gate_up))


def layer_backward(grad_out, allowed, saved, weights):
    (
        weight_in,
        weight_out,
        weight_up,
        weight_down,
        forget_proj,
        forget_bias,
        gain_attention,
        gain_feedforward,
    ) = weights
    values, mixed, forget_logit, log_total, attended, middle, gate_up = saved
    tree_len, width = values.shape
    head_count = forget_proj.shape[1]
    head_width = width // head_count
    half_width = gate_up.shape[1] // 2
    gate = gate_up[:, :half_width]
    upper = gate_up[:, half_width:]
    sigma = jax.nn.sigmoid(gate)
    silu_gate = gate * sigma
    hidden = lower(silu_gate * upper)
    normed_out_b, normed_b, inverse_b = rms_forward(middle, gain_feedforward)
    act_b = lower(normed_out_b)
    grad_branch = lower(grad_out)
    grad_down = product_left(hidden, grad_branch)
    grad_hidden = product_right(grad_branch, weight_down)
    grad_gate = grad_hidden * upper * sigma * (1.0 + gate * (1.0 - sigma))
    grad_upper = grad_hidden * silu_gate
    grad_gate_up = lower(jnp.concatenate([grad_gate, grad_upper], axis=1))
    grad_up = product_left(act_b, grad_gate_up)
    grad_norm_b, grad_gain_b = rms_backward(
        product_right(grad_gate_up, weight_up), normed_b, inverse_b, gain_feedforward
    )
    grad_middle = grad_out + grad_norm_b
    grad_attn_branch = lower(grad_middle)
    grad_out_weight = product_left(attended, grad_attn_branch)
    grad_attended = lower(product_right(grad_attn_branch, weight_out)).reshape(
        tree_len, head_count, head_width
    )
    normed_out_a, normed_a, inverse_a = rms_forward(values, gain_attention)
    act_a = lower(normed_out_a)
    cumul = jnp.dot(allowed, jax.nn.log_sigmoid(forget_logit), precision=highest)
    parts = mixed.reshape(tree_len, 3, head_count, head_width)
    scale = head_width ** (-0.5)
    scores = attention_scores(parts[:, 0], parts[:, 1], cumul)
    scores = jnp.where(allowed[None] > 0, scores, masked_score)
    probs = jnp.exp(scores - log_total)
    grad_probs = jnp.einsum(
        "ihd,jhd->hij", grad_attended, parts[:, 2], preferred_element_type=jnp.float32
    )
    grad_values = jnp.einsum(
        "hij,ihd->jhd", lower(probs), grad_attended, preferred_element_type=jnp.float32
    )
    grad_scores = lower(probs * (grad_probs - jnp.sum(probs * grad_probs, axis=-1, keepdims=True)))
    grad_queries = (
        jnp.einsum("hij,jhd->ihd", grad_scores, parts[:, 1], preferred_element_type=jnp.float32)
        * scale
    )
    grad_keys = (
        jnp.einsum("hij,ihd->jhd", grad_scores, parts[:, 0], preferred_element_type=jnp.float32)
        * scale
    )
    grad_cumul = (
        jnp.sum(grad_scores, axis=2, dtype=jnp.float32)
        - jnp.sum(grad_scores, axis=1, dtype=jnp.float32)
    ).T
    grad_logit = lower(
        jnp.dot(allowed.T, grad_cumul, precision=highest) * jax.nn.sigmoid(-forget_logit)
    )
    grad_mixed = lower(
        jnp.stack([grad_queries, grad_keys, grad_values], axis=1).reshape(tree_len, 3 * width)
    )
    grad_in_weight = product_left(act_a, grad_mixed)
    grad_forget = jnp.concatenate(
        [product_left(act_a, grad_logit), jnp.sum(grad_logit, axis=0, dtype=jnp.float32)[None]],
        axis=0,
    )
    grad_act_a = product_right(grad_mixed, weight_in) + product_right(grad_logit, forget_proj)
    grad_norm_a, grad_gain_a = rms_backward(grad_act_a, normed_a, inverse_a, gain_attention)
    grad_in = grad_middle + grad_norm_a
    return (
        grad_in,
        (grad_in_weight, grad_out_weight, grad_up, grad_down),
        grad_forget,
        jnp.stack([grad_gain_a, grad_gain_b]),
    )


def local_columns(vocab_ids, rows_each, shard_count, shard_id):
    block_id = vocab_ids // rows_each
    owned = block_id % shard_count == shard_id
    column = block_id // shard_count * rows_each + vocab_ids % rows_each
    return (owned, column)


def combine_stats(first, second):
    row_peak = jnp.maximum(first[0], second[0])
    row_total = first[1] * jnp.exp(first[0] - row_peak) + second[1] * jnp.exp(second[0] - row_peak)
    return (row_peak, row_total)


def place_rows(grad_rows, spot_index, tree_len):
    return jnp.zeros((tree_len, grad_rows.shape[1]), jnp.float32).at[spot_index].add(grad_rows)


def reduce_shards(grads):
    return (
        lax.psum_scatter(
            grads[0][None].astype(jnp.bfloat16), "shard", scatter_dimension=1, tiled=True
        ).astype(jnp.float32),
        lax.psum_scatter(
            grads[1][None].astype(jnp.bfloat16), "shard", scatter_dimension=1, tiled=True
        ).astype(jnp.float32),
        lax.psum_scatter(
            grads[2][None].astype(jnp.bfloat16), "shard", scatter_dimension=1, tiled=True
        ).astype(jnp.float32),
        lax.psum_scatter(
            grads[3][None].astype(jnp.bfloat16), "shard", scatter_dimension=1, tiled=True
        ).astype(jnp.float32),
    )


def adam_step(weight, grad, first, second, clip_scale, correct_first, correct_second):
    scaled = clip_scale * grad
    first_new = beta_first * first + (1.0 - beta_first) * scaled
    second_new = beta_second * second + (1.0 - beta_second) * scaled * scaled
    direction = (
        first_new / correct_first / (jnp.sqrt(second_new / correct_second) + adam_eps)
        + decay_rate * weight
    )
    return (first_new, second_new, direction)


def local(
    tokens,
    parents,
    loss_positions,
    targets,
    teacher_index,
    teacher_probability,
    step_count,
    embed_table,
    table_first,
    table_second,
    attention_in,
    attention_in_first,
    attention_in_second,
    attention_out,
    attention_out_first,
    attention_out_second,
    feedforward_in,
    feedforward_in_first,
    feedforward_in_second,
    feedforward_out,
    feedforward_out_first,
    feedforward_out_second,
    forget_gate,
    forget_first,
    forget_second,
    norm_gains,
    gains_first,
    gains_second,
):
    section_id = lax.axis_index("section")
    replica_id = lax.axis_index("replica")
    shard_id = lax.axis_index("shard")
    section_count = lax.axis_size("section")
    replica_count = lax.axis_size("replica")
    shard_count = lax.axis_size("shard")
    group_trees, tree_len = tokens.shape
    micro = group_trees // shard_count
    rows_each, width = embed_table.shape
    pos_count = loss_positions.shape[1]
    pos_all = group_trees * replica_count * pos_count
    own_start = shard_id * micro
    first_section = section_id == 0
    last_section = section_id == section_count - 1
    table_low = lax.all_gather(lower(embed_table), "replica", axis=0, tiled=True)
    gathered = (
        lax.all_gather(lower(attention_in), "shard", axis=1, tiled=True),
        lax.all_gather(lower(attention_out), "shard", axis=1, tiled=True),
        lax.all_gather(lower(feedforward_in), "shard", axis=1, tiled=True),
        lax.all_gather(lower(feedforward_out), "shard", axis=1, tiled=True),
    )
    forget_section = lax.dynamic_index_in_dim(forget_gate, section_id, 0, keepdims=False)
    gain_pair = lax.dynamic_slice_in_dim(norm_gains, 2 * section_id, 2, 0)
    weights = (
        gathered[0][0],
        gathered[1][0],
        gathered[2][0],
        gathered[3][0],
        lower(forget_section[:width]),
        forget_section[width],
        gain_pair[0],
        gain_pair[1],
    )
    owned_tok, column_tok = local_columns(tokens.reshape(-1), rows_each, shard_count, shard_id)
    embed_terms = jnp.where(owned_tok[:, None], table_low[column_tok], jnp.zeros((), jnp.bfloat16))
    embeds = (
        lax.psum_scatter(embed_terms, "shard", scatter_dimension=0, tiled=True)
        .astype(jnp.float32)
        .reshape(micro, tree_len, width)
    )
    own_parents = lax.dynamic_slice_in_dim(parents, own_start, micro, 0)
    masks = jax.vmap(partial(path_mask, tree_len=tree_len))(own_parents)
    received = jnp.zeros((tree_len, width), jnp.bfloat16)
    kept = []
    outputs = []
    for tick_index in range(micro + 1):
        early = min(tick_index, micro - 1)
        late = max(tick_index - 1, 0)
        layer_in = jnp.where(first_section, embeds[early], received.astype(jnp.float32))
        allowed = jnp.where(first_section, masks[early], masks[late])
        output, saved = layer_forward(layer_in, allowed, weights)
        kept.append((allowed, saved))
        outputs.append(output)
        if tick_index < micro:
            received = passed_along(lower(output), "section", 1)
    finals = jnp.stack(outputs[1:])
    own_positions = lax.dynamic_slice_in_dim(loss_positions, own_start, micro, 0)
    picked = jnp.take_along_axis(finals, own_positions[:, :, None], axis=1).reshape(
        micro * pos_count, width
    )
    final_gain = norm_gains[4]
    head_out, head_normed, head_inverse = rms_forward(picked, final_gain)
    head_rows = lax.all_gather(lower(head_out), "shard", axis=0, tiled=True)
    logits = product_right(head_rows, table_low)
    row_count = head_rows.shape[0]
    teacher_flat = teacher_index.reshape(row_count, -1)
    prob_flat = teacher_probability.reshape(row_count, -1)
    owned_target, column_target = local_columns(
        targets.reshape(-1), rows_each, shard_count, shard_id
    )
    owned_teacher, column_teacher = local_columns(teacher_flat, rows_each, shard_count, shard_id)
    target_pick = jnp.where(
        owned_target, jnp.take_along_axis(logits, column_target[:, None], axis=1)[:, 0], 0.0
    )
    teacher_pick = jnp.where(
        owned_teacher, jnp.take_along_axis(logits, column_teacher, axis=1), 0.0
    )
    local_peak = jnp.max(logits, axis=1)
    local_total = jnp.sum(jnp.exp(logits - local_peak[:, None]), axis=1)
    row_peak, row_total = combined_all((local_peak, local_total), "shard", combine_stats)
    log_norm = row_peak + jnp.log(row_total)
    prob_sum = jnp.sum(prob_flat, axis=1)
    row_part = log_norm * (1.0 + prob_sum) + jnp.sum(prob_flat * jnp.log(prob_flat), axis=1)
    own_part = lax.dynamic_slice_in_dim(
        row_part, shard_id * micro * pos_count, micro * pos_count, 0
    )
    linear_part = jnp.sum(target_pick) + jnp.sum(prob_flat * teacher_pick)
    loss_part = jnp.where(last_section, (jnp.sum(own_part) - linear_part) / pos_all, 0.0)
    grad_logits = (1.0 + prob_sum)[:, None] * jnp.exp(logits - log_norm[:, None])
    row_ids = jnp.arange(row_count, dtype=jnp.int32)
    grad_logits = grad_logits.at[row_ids, column_target].add(jnp.where(owned_target, -1.0, 0.0))
    grad_logits = grad_logits.at[row_ids[:, None], column_teacher].add(
        jnp.where(owned_teacher, -prob_flat, 0.0)
    )
    grad_logits = lower(grad_logits / pos_all)
    head_table = product_left(grad_logits, head_rows)
    grad_heads = lax.psum_scatter(
        product(grad_logits, table_low), "shard", scatter_dimension=0, tiled=True
    )
    grad_picked, grad_final = rms_backward(grad_heads, head_normed, head_inverse, final_gain)
    grad_finals = jax.vmap(partial(place_rows, tree_len=tree_len))(
        grad_picked.reshape(micro, pos_count, width), own_positions
    )
    grad_received = jnp.zeros((tree_len, width), jnp.bfloat16)
    embed_grads = [None] * micro
    weight_grads = tuple((jnp.zeros(piece.shape[1:], jnp.float32) for piece in gathered))
    forget_grad = jnp.zeros(forget_section.shape, jnp.float32)
    gain_grad = jnp.zeros((2, width), jnp.float32)
    for back_index in range(micro + 1):
        fwd_index = micro - back_index
        if back_index < micro:
            late_grad = grad_finals[micro - 1 - back_index]
        else:
            late_grad = jnp.zeros((tree_len, width), jnp.float32)
        grad_top = jnp.where(first_section, grad_received.astype(jnp.float32), late_grad)
        allowed, saved = kept[fwd_index]
        grad_in, tick_grads, tick_forget, tick_gains = layer_backward(
            grad_top, allowed, saved, weights
        )
        if back_index < micro:
            grad_received = passed_along(lower(grad_in), "section", -1)
        if back_index >= 1:
            embed_grads[micro - back_index] = grad_in
        weight_grads = tuple((total + term for total, term in zip(weight_grads, tick_grads)))
        forget_grad = forget_grad + tick_forget
        gain_grad = gain_grad + tick_gains
    shard_grads = reduce_shards(weight_grads)
    embed_low = lower(jnp.concatenate(embed_grads, axis=0))
    embed_all = lax.all_gather(embed_low, "shard", axis=0, tiled=True)
    slot_index = jnp.where(owned_tok, column_tok, replica_count * rows_each)
    embed_table_grad = jax.ops.segment_sum(
        embed_all.astype(jnp.float32), slot_index, num_segments=replica_count * rows_each + 1
    )[:-1]
    table_term = jnp.where(first_section, embed_table_grad, head_table)
    table_grad = lax.psum_scatter(
        jnp.concatenate([table_term] * section_count, axis=0).astype(jnp.bfloat16),
        ("section", "replica"),
        scatter_dimension=0,
        tiled=True,
    ).astype(jnp.float32)
    layer_grads = (
        lax.psum(shard_grads[0].astype(jnp.bfloat16), "replica").astype(jnp.float32),
        lax.psum(shard_grads[1].astype(jnp.bfloat16), "replica").astype(jnp.float32),
        lax.psum(shard_grads[2].astype(jnp.bfloat16), "replica").astype(jnp.float32),
        lax.psum(shard_grads[3].astype(jnp.bfloat16), "replica").astype(jnp.float32),
    )
    section_slot = jnp.arange(section_count, dtype=jnp.int32) == section_id
    forget_full = jnp.where(section_slot[:, None, None], forget_grad[None], 0.0)
    gain_rows = jnp.arange(norm_gains.shape[0], dtype=jnp.int32)
    gains_full = (
        jnp.where((gain_rows == 2 * section_id)[:, None], gain_grad[0][None], 0.0)
        + jnp.where((gain_rows == 2 * section_id + 1)[:, None], gain_grad[1][None], 0.0)
        + jnp.where(((gain_rows == 4) & last_section)[:, None], grad_final[None], 0.0)
    )
    table_square = jnp.where(first_section, jnp.sum(table_grad * table_grad), 0.0)
    layer_square = jnp.where(
        replica_id == 0, sum((jnp.sum(piece * piece) for piece in layer_grads)), 0.0
    )
    totals = lax.psum(
        (table_square + layer_square, forget_full, gains_full, loss_part),
        ("section", "replica", "shard"),
    )
    forget_total = totals[1]
    gains_total = totals[2]
    loss_total = totals[3]
    grad_norm = jnp.sqrt(
        totals[0] + jnp.sum(forget_total * forget_total) + jnp.sum(gains_total * gains_total)
    )
    clip_scale = jnp.minimum(1.0, clip_factor / jnp.sqrt(jnp.float32(pos_all)) / grad_norm)
    count_float = step_count.astype(jnp.float32)
    correct_first = 1.0 - jnp.power(beta_first, count_float)
    correct_second = 1.0 - jnp.power(beta_second, count_float)
    adam = partial(
        adam_step, clip_scale=clip_scale, correct_first=correct_first, correct_second=correct_second
    )
    table_first_new, table_second_new, table_direction = adam(
        embed_table, table_grad, table_first, table_second
    )
    layer_weights = (attention_in, attention_out, feedforward_in, feedforward_out)
    layer_firsts = (
        attention_in_first,
        attention_out_first,
        feedforward_in_first,
        feedforward_out_first,
    )
    layer_seconds = (
        attention_in_second,
        attention_out_second,
        feedforward_in_second,
        feedforward_out_second,
    )
    layer_steps = [
        adam(weight, grad, first, second)
        for weight, grad, first, second in zip(
            layer_weights, layer_grads, layer_firsts, layer_seconds
        )
    ]
    table_parts = jnp.where(
        first_section,
        jnp.stack([jnp.sum(embed_table * embed_table), jnp.sum(table_direction * table_direction)]),
        0.0,
    )
    layer_parts = jnp.stack(
        [
            jnp.stack([jnp.sum(weight * weight), jnp.sum(stepped[2] * stepped[2])])
            for weight, stepped in zip(layer_weights, layer_steps)
        ]
    )
    layer_parts = jnp.where(replica_id == 0, layer_parts, 0.0)
    layer_spread = layer_parts[:, None, :] * section_slot.astype(jnp.float32)[None, :, None]
    trust = lax.psum((table_parts, layer_spread), ("section", "replica", "shard"))
    table_norms = jnp.sqrt(trust[0])
    layer_norms = jnp.sqrt(trust[1])
    new_table = embed_table - learn_rate * (table_norms[0] / table_norms[1]) * table_direction
    mine = jnp.sum(layer_norms * section_slot.astype(jnp.float32)[None, :, None], axis=1)
    new_layers = []
    for mat_index in range(4):
        ratio = mine[mat_index, 0] / mine[mat_index, 1]
        stepped = layer_steps[mat_index]
        new_layers.append(
            (layer_weights[mat_index] - learn_rate * ratio * stepped[2], stepped[0], stepped[1])
        )
    forget_first_new, forget_second_new, forget_direction = adam(
        forget_gate, forget_total, forget_first, forget_second
    )
    forget_weight_norm = jnp.sqrt(jnp.sum(forget_gate * forget_gate, axis=(1, 2)))
    forget_update_norm = jnp.sqrt(jnp.sum(forget_direction * forget_direction, axis=(1, 2)))
    new_forget = (
        forget_gate
        - learn_rate * (forget_weight_norm / forget_update_norm)[:, None, None] * forget_direction
    )
    gains_first_new, gains_second_new, gains_direction = adam(
        norm_gains, gains_total, gains_first, gains_second
    )
    gains_weight_norm = jnp.sqrt(jnp.sum(norm_gains * norm_gains, axis=1))
    gains_update_norm = jnp.sqrt(jnp.sum(gains_direction * gains_direction, axis=1))
    new_gains = (
        norm_gains - learn_rate * (gains_weight_norm / gains_update_norm)[:, None] * gains_direction
    )
    tensor_norms = jnp.concatenate(
        [
            table_norms[None],
            layer_norms.reshape(4 * section_count, 2),
            jnp.stack([forget_weight_norm, forget_update_norm], axis=1),
            jnp.stack([gains_weight_norm, gains_update_norm], axis=1),
        ],
        axis=0,
    )
    return (
        new_table,
        table_first_new,
        table_second_new,
        new_layers[0][0],
        new_layers[0][1],
        new_layers[0][2],
        new_layers[1][0],
        new_layers[1][1],
        new_layers[1][2],
        new_layers[2][0],
        new_layers[2][1],
        new_layers[2][2],
        new_layers[3][0],
        new_layers[3][1],
        new_layers[3][2],
        new_forget,
        forget_first_new,
        forget_second_new,
        new_gains,
        gains_first_new,
        gains_second_new,
        tensor_norms,
        grad_norm,
        loss_total,
    )


def solution(mesh):
    in_specs = (
        P("replica", None),
        P("replica", None),
        P("replica", None),
        P("replica", None),
        P("replica", None, None),
        P("replica", None, None),
        P(),
        P(("replica", "shard"), None),
        P(("replica", "shard"), None),
        P(("replica", "shard"), None),
        P("section", "shard", None),
        P("section", "shard", None),
        P("section", "shard", None),
        P("section", "shard", None),
        P("section", "shard", None),
        P("section", "shard", None),
        P("section", "shard", None),
        P("section", "shard", None),
        P("section", "shard", None),
        P("section", "shard", None),
        P("section", "shard", None),
        P("section", "shard", None),
        P(),
        P(),
        P(),
        P(),
        P(),
        P(),
    )
    out_specs = (
        P(("replica", "shard"), None),
        P(("replica", "shard"), None),
        P(("replica", "shard"), None),
        P("section", "shard", None),
        P("section", "shard", None),
        P("section", "shard", None),
        P("section", "shard", None),
        P("section", "shard", None),
        P("section", "shard", None),
        P("section", "shard", None),
        P("section", "shard", None),
        P("section", "shard", None),
        P("section", "shard", None),
        P("section", "shard", None),
        P("section", "shard", None),
        P(),
        P(),
        P(),
        P(),
        P(),
        P(),
        P(),
        P(),
        P(),
    )
    return jax.shard_map(local, mesh=mesh, in_specs=in_specs, out_specs=out_specs, check_vma=False)
```

profile of v0, /device:TPU:0, one launch (start us, length us, event | category | flops | bytes accessed | tf_op | source)
XLA Modules:
  0.0 2038.1 jit_solution(3988445715562712416)
XLA Ops:
  17.7 17.4 all-gather.11.cloned.1.call-done
  35.1 27.1 %gather_fusion = bf16[5120,768]{1,0:T(8,128)(2,1)} fusion(bf16[4000,768]{1,0:T(8,128)(2,1)} %all-gather.11.cloned.1.call-done, s32[5120]{0:T(1024)S(1)} %broadcast_clamp_fusion), kind=kCustom, calls=%fused_computation | custom fusion | bytes 15749120 | tf_op jit(solution)/shard_map/gather | solution.py:336
  90.5 121.0 %reduce-scatter.8.cloned.1.call-done = bf16[640,768]{1,0:T(8,128)(2,1)} async-done(((bf16[5120,768]{1,0:T(8,128)(2,1)}), bf16[640,768]{1,0:T(8,128)(2,1)}) %reduce-scatter.8.cloned.1.call-update) | async-done | bytes 983056 | tf_op jit(solution)/shard_map/reduce_scatter | solution.py:338
  213.3 64.7 %all-gather.13.cloned.1.call-done = bf16[1,768,2304]{2,1,0:T(8,128)(2,1)} async-done(((bf16[1,96,2304]{2,1,0:T(8,128)(2,1)}), bf16[1,768,2304]{2,1,0:T(8,128)(2,1)}) %all-gather.13.cloned.1.call-update) | async-done | bytes 3538960 | tf_op jit(solution)/shard_map/all_gather | solution.py:318
  295.8 24.7 %all-gather.15.cloned.1.call-done = bf16[1,768,768]{2,1,0:T(8,128)(2,1)} async-done(((bf16[1,96,768]{2,1,0:T(8,128)(2,1)}), bf16[1,768,768]{2,1,0:T(8,128)(2,1)}) %all-gather.15.cloned.1.call-update) | async-done | bytes 1179664 | tf_op jit(solution)/shard_map/all_gather | solution.py:319
  323.5 97.0 %all-gather.17.cloned.1.call-done = bf16[1,768,4096]{2,1,0:T(8,128)(2,1)} async-done(((bf16[1,96,4096]{2,1,0:T(8,128)(2,1)}), bf16[1,768,4096]{2,1,0:T(8,128)(2,1)}) %all-gather.17.cloned.1.call-update) | async-done | bytes 6291472 | tf_op jit(solution)/shard_map/all_gather | solution.py:320
  430.1 51.3 %all-gather.19.cloned.1.call-done = bf16[1,2048,768]{2,1,0:T(8,128)(2,1)} async-done(((bf16[1,256,768]{2,1,0:T(8,128)(2,1)}), bf16[1,2048,768]{2,1,0:T(8,128)(2,1)}) %all-gather.19.cloned.1.call-update) | async-done | bytes 3145744 | tf_op jit(solution)/shard_map/all_gather | solution.py:321
  562.0 33.4 %all_gather.38 = bf16[256,768]{1,0:T(8,128)(2,1)S(1)} all-gather(bf16[32,768]{1,0:T(8,128)(2,1)S(1)} %multiply_convert_fusion.19), channel_id=1, replica_groups=mesh['section'=2,'replica'=2,'shard'=8] {'shard'}, dimensions={0}, use_global_device_ids=true | all-gather | bytes 442368 | tf_op jit(solution)/shard_map/all_gather | solution.py:364
  602.7 19.5 all-gather.3
  622.2 16.3 all-gather.2
  638.5 200.2 %gather_fusion.3 = f32[16384]{0:T(1024)S(1)} fusion(f32[256,4000]{0,1:T(8,128)} %copy-done.2, s32[16384]{0:T(1024)S(1)} %reshape.1221), kind=kCustom, calls=%fused_computation.3 | custom fusion | bytes 262144 | tf_op jit(solution)/shard_map/jit(take_along_axis)/gather | solution.py:377
  845.8 31.5 %scatter_fusion = f32[256,4000]{0,1:T(8,128)} fusion(f32[256,4000]{0,1:T(8,128)} %exponential_multiply_fusion, s32[256]{0:T(256)S(1)} %bitcast.454, f32[256]{0:T(256)S(1)} %copy-done.169), kind=kCustom, calls=%fused_computation.4 | custom fusion | flops 256 | bytes 5120 | tf_op jit(solution)/shard_map/scatter-add | solution.py:392
  883.5 82.7 %scatter_fusion.2 = f32[1024000]{0:T(1024)} fusion(f32[1024000]{0:T(1024)} %bitcast.428, s32[16384]{0:T(1024)S(1)} %reshape.1247, f32[16384]{0:T(1024)S(1)} %reshape.1249), kind=kCustom, calls=%fused_computation.7 | custom fusion | flops 16384 | bytes 262144
  976.8 62.8 %reduce-scatter.10.cloned.1.call-done = f32[32,768]{1,0:T(8,128)} async-done(((f32[256,768]{1,0:T(8,128)}), f32[32,768]{1,0:T(8,128)}) %reduce-scatter.10.cloned.1.call-update) | async-done | bytes 98320 | tf_op jit(solution)/shard_map/reduce_scatter | solution.py:398
  1213.2 65.8 %reduce-scatter.20.cloned.1.call-done = bf16[1,256,768]{2,1,0:T(8,128)(2,1)} async-done(((bf16[1,2048,768]{2,1,0:T(8,128)(2,1)}), bf16[1,256,768]{2,1,0:T(8,128)(2,1)}) %reduce-scatter.20.cloned.1.call-update) | async-done | bytes 393232 | tf_op jit(solution)/shard_map/reduce_scatter | solution.py:255
  1279.1 82.6 %reduce-scatter.14.cloned.1.call-done = bf16[1,96,2304]{2,1,0:T(8,128)(2,1)} async-done(((bf16[1,768,2304]{2,1,0:T(8,128)(2,1)}), bf16[1,96,2304]{2,1,0:T(8,128)(2,1)}) %reduce-scatter.14.cloned.1.call-update) | async-done | bytes 442384 | tf_op jit(solution)/shard_map/reduce_scatter | solution.py:246
  1361.7 121.2 %reduce-scatter.18.cloned.1.call-done = bf16[1,96,4096]{2,1,0:T(8,128)(2,1)} async-done(((bf16[1,768,4096]{2,1,0:T(8,128)(2,1)}), bf16[1,96,4096]{2,1,0:T(8,128)(2,1)}) %reduce-scatter.18.cloned.1.call-update) | async-done | bytes 786448 | tf_op jit(solution)/shard_map/reduce_scatter | solution.py:252
  1483.0 119.8 %all-gather.21.cloned.1.call-done = bf16[5120,768]{1,0:T(8,128)(2,1)} async-done(((bf16[640,768]{1,0:T(8,128)(2,1)}), bf16[5120,768]{1,0:T(8,128)(2,1)}) %all-gather.21.cloned.1.call-update) | async-done | bytes 7864336 | tf_op jit(solution)/shard_map/all_gather | solution.py:430
  1602.8 40.3 %scatter_custom_fusion.1 = f32[4001,768]{1,0:T(8,128)} fusion(s32[5120]{0:T(1024)S(1)} %bitcast.498, bf16[5120,768]{1,0:T(8,128)(2,1)} %all-gather.21.cloned.1.call-done, f32[]{:T(128)} %constant.328.clone.1), kind=kCustom, calls=%fused_computation.22 | custom fusion | flops 7864320 | bytes 20155396 | tf_op jit(solution)/shard_map/scatter-add | solution.py:432
  1675.9 75.4 %reduce-scatter.12.cloned.1.call-done = bf16[2000,768]{1,0:T(8,128)(2,1)} async-done(((bf16[8000,768]{1,0:T(8,128)(2,1)}), bf16[2000,768]{1,0:T(8,128)(2,1)}) %reduce-scatter.12.cloned.1.call-update) | async-done | bytes 3072016 | tf_op jit(solution)/shard_map/reduce_scatter | solution.py:436
  1756.0 122.9 %all-reduce.6.cloned.1.call-done = f32[2,769,12]{1,0,2:T(2,128)} async-done(((f32[2,769,12]{1,0,2:T(2,128)}), f32[2,769,12]{1,0,2:T(2,128)}) %all-reduce.6.cloned.1.call-update) | async-done | bytes 73840 | tf_op jit(solution)/shard_map/psum | solution.py:460
  1880.5 42.8 %all-reduce.1 = (f32[]{:T(128)}, f32[5,768]{1,0:T(8,128)S(1)}) all-reduce(f32[]{:T(128)S(6)} %add.1022, f32[5,768]{1,0:T(8,128)S(1)} %select_add_fusion), channel_id=1, replica_groups=mesh['section'=2,'replica'=2,'shard'=8] {'section','replica','shard'}, use_global_device_ids=true, to_apply=%region_57.58 | all-reduce | flops 3841 | bytes 30728 | tf_op jit(solution)/shard_map/psum | solution.py:460
  1943.8 15.6 multiply_reduce_fusion
  1960.8 39.7 %all-reduce = (f32[2]{0:T(128)}, f32[4,2,2]{1,0,2:T(4,128)S(1)}, f32[]{:T(128)}) all-reduce(f32[2]{0:T(128)S(1)} %broadcast_select_fusion.3, f32[4,2,2]{1,0,2:T(4,128)S(1)} %broadcast_multiply_fusion, f32[]{:T(128)S(6)} %select_n.629), channel_id=1, replica_groups=mesh['section'=2,'replica'=2,'shard'=8] {'section','replica','shard'}, use_global_device_ids=true, to_apply=%region_73.74 | all-reduce | flops 19 | bytes 152 | tf_op jit(solution)/shard_map/psum | solution.py:512
  (796 shorter events, 431.9 us)
Async XLA Ops:
  7.2 27.9 %all-gather.11.cloned.1.call-start = ((), (), s32[]{:S(2)}) async-start(), calls=%async_computation.7 | async-start | bytes 9216000 | tf_op jit(solution)/shard_map/all_gather | solution.py:316
  15.6 195.9 %reduce-scatter.8.cloned.1.call-start = ((), (), s32[]{:S(2)}) async-start(), calls=%async_computation.8 | async-start | bytes 8847360 | tf_op jit(solution)/shard_map/reduce_scatter | solution.py:338
  70.0 208.0 %all-gather.13.cloned.1.call-start = ((), (), s32[]{:S(2)}) async-start(), calls=%async_computation.9 | async-start | bytes 3981312 | tf_op jit(solution)/shard_map/all_gather | solution.py:318
  72.7 247.8 %all-gather.15.cloned.1.call-start = ((), (), s32[]{:S(2)}) async-start(), calls=%async_computation.10 | async-start | bytes 1327104 | tf_op jit(solution)/shard_map/all_gather | solution.py:319
  74.1 346.4 %all-gather.17.cloned.1.call-start = ((), (), s32[]{:S(2)}) async-start(), calls=%async_computation.11 | async-start | bytes 7077888 | tf_op jit(solution)/shard_map/all_gather | solution.py:320
  76.0 405.3 %all-gather.19.cloned.1.call-start = ((), (), s32[]{:S(2)}) async-start(), calls=%async_computation.12 | async-start | bytes 3538944 | tf_op jit(solution)/shard_map/all_gather | solution.py:321
  77.7 962.0 %reduce-scatter.10.cloned.1.call-start = ((), (), s32[]{:S(2)}) async-start(), calls=%async_computation.13 | async-start | bytes 884736 | tf_op jit(solution)/shard_map/reduce_scatter | solution.py:398
  78.9 459.8 %copy-start.109 = (bf16[1,768,12]{1,0,2:T(2,128)(2,1)}, bf16[1,768,12]{1,0,2:T(2,128)(2,1)S(1)}, u32[]{:S(2)}) copy-start(bf16[1,768,12]{1,0,2:T(2,128)(2,1)S(1)} %constant_dynamic-slice_fusion.2) | copy-start | bytes 55300
  83.6 417.5 %copy-start.25 = (f32[2,320,320]{2,1,0:T(8,128)}, f32[2,320,320]{2,1,0:T(8,128)S(1)}, u32[]{:S(2)}) copy-start(f32[2,320,320]{2,1,0:T(8,128)S(1)} %fusion.98) | copy-start | bytes 2457604
  87.0 450.6 %copy-start.119 = (f32[768]{0:T(1024)}, f32[768]{0:T(1024)S(1)}, u32[]{:S(2)}) copy-start(f32[768]{0:T(1024)S(1)} %get-tuple-element.219) | copy-start | bytes 9220
  212.9 323.4 %copy-start.6 = (f32[640,768]{1,0:T(8,128)}, f32[640,768]{1,0:T(8,128)S(1)}, u32[]{:S(2)}) copy-start(f32[640,768]{1,0:T(8,128)S(1)} %convert_element_type.357) | copy-start | bytes 5898244
  485.8 12.7 collective-permute-start
  523.6 12.7 collective-permute-start.1
  976.5 236.7 %reduce-scatter.16.cloned.1.call-start = ((), (), s32[]{:S(2)}) async-start(), calls=%async_computation.17 | async-start | bytes 1327104 | tf_op jit(solution)/shard_map/reduce_scatter | solution.py:249
  1077.1 13.1 collective-permute-start.2
  1117.7 12.4 collective-permute-start.3
  1138.3 140.8 %reduce-scatter.20.cloned.1.call-start = ((), (), s32[]{:S(2)}) async-start(), calls=%async_computation.19 | async-start | bytes 3538944 | tf_op jit(solution)/shard_map/reduce_scatter | solution.py:255
  1147.3 214.4 %reduce-scatter.14.cloned.1.call-start = ((), (), s32[]{:S(2)}) async-start(), calls=%async_computation.16 | async-start | bytes 3981312 | tf_op jit(solution)/shard_map/reduce_scatter | solution.py:246
  1175.2 307.8 %reduce-scatter.18.cloned.1.call-start = ((), (), s32[]{:S(2)}) async-start(), calls=%async_computation.18 | async-start | bytes 7077888 | tf_op jit(solution)/shard_map/reduce_scatter | solution.py:252
  1205.0 397.9 %all-gather.21.cloned.1.call-start = ((), (), s32[]{:S(2)}) async-start(), calls=%async_computation.14 | async-start | bytes 8847360 | tf_op jit(solution)/shard_map/all_gather | solution.py:430
  1213.1 452.3 %all-reduce.8.cloned.1.call-start = ((), (), s32[]{:S(2)}) async-start(), calls=%async_computation.21 | async-start | bytes 3538944 | tf_op jit(solution)/shard_map/psum | solution.py:443
  1483.0 268.4 %reduce-scatter.12.cloned.1.call-start = ((), (), s32[]{:S(2)}) async-start(), calls=%async_computation.15 | async-start | bytes 15360000 | tf_op jit(solution)/shard_map/reduce_scatter | solution.py:436
  1654.8 224.1 %all-reduce.6.cloned.1.call-start = ((), (), s32[]{:S(2)}) async-start(), calls=%async_computation.20 | async-start | bytes 172032 | tf_op jit(solution)/shard_map/psum | solution.py:460
  1664.2 261.7 %copy-start.78 = (f32[1,96,768]{2,1,0:T(8,128)S(1)}, f32[1,96,768]{2,1,0:T(8,128)}, u32[]{:S(2)}) copy-start(f32[1,96,768]{2,1,0:T(8,128)} %param.45) | copy-start | bytes 884740
  (210 other events, 4372.9 us)
Sparse Core Ops, SparseCore 0:
  15.7 19.2 all-gather.10
  70.1 141.3 reduce-scatter.7
  214.3 63.6 all-gather.12
  280.6 39.8 all-gather.14
  323.1 97.3 all-gather.16
  423.1 58.1 all-gather.18
  976.6 62.9 reduce-scatter.9
  1138.4 63.1 reduce-scatter.15
  1205.7 73.2 reduce-scatter.19
  1283.1 78.5 reduce-scatter.13
  1365.3 117.6 reduce-scatter.17
  1485.6 117.1 all-gather.20
  1605.4 19.0 all-reduce.7
  1654.9 96.3 reduce-scatter.11
  1757.3 121.5 all-reduce.5
where the time goes:
time: 2050 us; the launch traced here: 2040 us
  waiting for transfers between devices  1060 us (52%)
  other arithmetic  303 us (15%)
  local copies, waits for them, and re-layouts  295 us (14%)
  matrix products  185 us (9%)
  blocking collectives  152 us (7%)
  between operations  32.8 us (2%)
    gather x2, local copies, waits for them, and re-layouts, local(): jnp.take_along_axis(logits, column_teacher, axis=1)  200 us
    psum x1, waiting for transfers between devices, local(): lax.psum((table_square + layer_square, forget_full, gains_full, loss_part...  123 us
    reduce_scatter x1, waiting for transfers between devices, reduce_shards(): lax.psum_scatter(grads[2][None].astype(jnp.bfloat16), 'shard', scatter_di...  121 us
    reduce_scatter x1, waiting for transfers between devices, local(): lax.psum_scatter(embed_terms, 'shard', scatter_dimension=0, tiled=True)  121 us
    all_gather x1, waiting for transfers between devices, local(): embed_all = lax.all_gather(embed_low, 'shard', axis=0, tiled=True)  120 us
    all_gather x1, waiting for transfers between devices, local(): lax.all_gather(lower(feedforward_in), 'shard', axis=1, tiled=True)  97 us
    unnamed x16, other arithmetic  83.6 us
    reduce_scatter x1, waiting for transfers between devices, reduce_shards(): lax.psum_scatter(grads[0][None].astype(jnp.bfloat16), 'shard', scatter_di...  82.6 us
  transfers between devices with their start and end apart: 19, of which 17 were waited for; matrix products, arithmetic and copies ran while one was open for 10% of the time, Pallas kernels for 0%

commit v1 on v0

v1 whole, which is shorter than its diff:
```python
from functools import partial

import jax
import jax.numpy as jnp
from jax import lax
from jax.experimental import pallas as pl
from jax.experimental.pallas import tpu as pltpu
from jax.sharding import PartitionSpec as P

MESH = pl.DeviceIdType.MESH
VMEM = pl.BlockSpec(memory_space=pltpu.VMEM)
ANY = pl.BlockSpec(memory_space=pl.ANY)
DMA = pltpu.SemaphoreType.DMA
eps_norm = 1e-06
beta_first = 0.9
beta_second = 0.999
adam_eps = 1e-10
decay_rate = 0.01
learn_rate = 0.2
clip_factor = 8.0
highest = lax.Precision.HIGHEST
masked_score = -1e30
batch_rows = 40
every_axis = ("section", "replica", "shard")


class Place:
    def __init__(self):
        self.sections = lax.axis_size("section")
        self.replicas = lax.axis_size("replica")
        self.shards = lax.axis_size("shard")
        self.nz = min(4, self.shards)
        self.ny = self.shards // self.nz
        self.x = lax.axis_index("section")
        self.rep = lax.axis_index("replica")
        self.shard = lax.axis_index("shard")
        self.core = lax.rem(self.rep, 2)
        self.z = self.shard // self.ny
        self.y = lax.rem(self.shard, self.ny)

    def at(self, section=None, rep=None, z=None, y=None, shard=None):
        if shard is None:
            shard = (self.z if z is None else z) * self.ny + (self.y if y is None else y)
        return {
            "section": self.x if section is None else section,
            "replica": self.rep if rep is None else rep,
            "shard": shard,
        }

    def peer_x(self, i):
        return self.at(section=lax.rem(self.x + i, self.sections))

    def peer_y(self, j):
        return self.at(y=lax.rem(self.y + j, self.ny))

    def line(self, step):
        return self.at(z=self.z + step)

    def partner(self):
        return self.at(rep=self.rep + 1 - 2 * self.core)

    def group(self, p):
        count = self.replicas * self.shards
        place = lax.rem(self.rep * self.shards + self.shard + p, count)
        return place, self.at(rep=place // self.shards, shard=lax.rem(place, self.shards))

    def inside(self, k):
        if k == 0:
            return None
        return self.z + k < self.nz if k > 0 else self.z + k >= 0

    def greet(self, use_x=True):
        barrier = pltpu.get_barrier_semaphore()

        def signal(device):
            pl.semaphore_signal(barrier, inc=1, device_id=device, device_id_type=MESH)

        count = 1
        if use_x:
            for i in range(1, self.sections):
                signal(self.peer_x(i))
                count += 1
        for j in range(1, self.ny):
            signal(self.peer_y(j))
            count += 1
        signal(self.partner())
        up, down = self.inside(1), self.inside(-1)
        pl.when(up)(lambda: signal(self.line(1)))
        pl.when(down)(lambda: signal(self.line(-1)))
        ends = jnp.minimum(self.z, 1) + jnp.minimum(self.nz - 1 - self.z, 1)
        pl.semaphore_wait(barrier, count + ends)


def when(cond, fn):
    if cond is None:
        fn()
    else:
        pl.when(cond)(fn)


def both(a, b):
    if a is None:
        return b
    if b is None:
        return a
    return jnp.logical_and(a, b)


def remote(src, dst, send, recv, device):
    return pltpu.make_async_remote_copy(
        src_ref=src, dst_ref=dst, send_sem=send, recv_sem=recv, device_id=device, device_id_type=MESH
    )


def gather_kernel(count, pairs, split, orders, *refs):
    ins, refs = refs[:count], refs[count:]
    pair_ins, refs = refs[:pairs], refs[pairs:]
    outs, refs = refs[:count], refs[count:]
    pair_outs, refs = refs[:pairs], refs[pairs:]
    send_sem, recv_sem, cross_sem, pair_sem, local_sem = refs
    me = Place()
    nz, ny, nx = me.nz, me.ny, me.sections
    if "x" not in orders[0]:
        nx = 1
    me.greet(use_x=nx > 1)

    def slot(ref, k, j, i, half):
        section = lax.rem(me.x + i, nx) if nx > 1 else 0
        return ref.at[section, (me.z + k) * ny + lax.rem(me.y + j, ny), half]

    locals_ = []
    for a in range(count):
        if split:
            dst = outs[a].at[me.x if nx > 1 else 0, me.shard]
        else:
            dst = outs[a].at[me.x if nx > 1 else 0, me.shard, me.core]
        locals_.append(pltpu.make_async_copy(ins[a], dst, local_sem.at[a]))
    for p in range(pairs):
        locals_.append(
            pltpu.make_async_copy(pair_ins[p], pair_outs[p].at[me.core], local_sem.at[count + p])
        )
    for copy in locals_:
        copy.start()
    pair_copies = [
        remote(pair_ins[p], pair_outs[p].at[me.core], pair_sem.at[0, p], pair_sem.at[1, p], me.partner())
        for p in range(pairs)
    ]

    def run(core, order):
        sends = []

        def push(cond, src, dst, device, sem):
            copy = remote(src, dst, send_sem.at[len(sends)], sem, device)
            when(cond, copy.start)
            sends.append((cond, copy))

        def sem_of(a, k, j, i):
            return recv_sem.at[a, k + nz - 1, j, i]

        def spread(k, j, i, via):
            cond = me.inside(k)
            own = via is None
            later = order if own else order[order.index(via) + 1 :]
            for a in range(count):
                dst = slot(outs[a], k, j, i, core)
                src = dst
                if own:
                    src = ins[a].at[core] if split else ins[a]
                else:
                    arrival = remote(dst, dst, send_sem.at[0], sem_of(a, k, j, i), me.partner())
                    when(cond, arrival.wait_recv)
                steps = []
                if via == "z":
                    steps = [-1 if k > 0 else 1]
                elif "z" in later:
                    steps = [1, -1]
                for step in steps:
                    push(both(cond, me.inside(step)), src, dst, me.line(step), sem_of(a, k - step, j, i))
                if "y" in later:
                    for p in range(1, ny):
                        push(cond, src, dst, me.peer_y(p), sem_of(a, k, (j - p) % ny, i))
                if "x" in later:
                    for p in range(1, nx):
                        push(cond, src, dst, me.peer_x(p), sem_of(a, k, j, (i - p) % nx))
                if not (own and split):
                    push(cond, src, dst, me.partner(), cross_sem.at[a, k + nz - 1, j, i])

        events = []
        for k in range(1 - nz, nz):
            for j in range(ny):
                for i in range(nx):
                    via = [d for d in order if {"z": k, "y": j, "x": i}[d] != 0]
                    hops = abs(k) + (j != 0) + (i != 0)
                    stage = order.index(via[-1]) if via else -1
                    events.append((hops, stage, k, j, i, via[-1] if via else None))
        events.sort(key=lambda e: e[:5])
        for hops, stage, k, j, i, via in events:
            spread(k, j, i, via)
            if via is None:
                for copy in pair_copies:
                    copy.start()
        for hops, stage, k, j, i, via in events:
            if via is None and split:
                continue
            for a in range(count):
                dst = slot(outs[a], k, j, i, 1 - core)
                arrival = remote(dst, dst, send_sem.at[0], cross_sem.at[a, k + nz - 1, j, i], me.partner())
                when(me.inside(k), arrival.wait_recv)
        for cond, copy in sends:
            when(cond, copy.wait_send)

    for core, order in enumerate(orders):
        pl.when(me.core == core)(partial(run, core, order))
    for p in range(pairs):
        pair_copies[p].wait_send()
        remote(
            pair_ins[p], pair_outs[p].at[1 - me.core], pair_sem.at[0, p], pair_sem.at[1, p], me.partner()
        ).wait_recv()
    for copy in locals_:
        copy.wait()


def gather(parts, ident, pair_parts=(), split=False, orders=(("z", "y", "x"), ("x", "z", "y")), space=ANY):
    count, pairs = len(parts), len(pair_parts)
    shards = lax.axis_size("shard")
    nx = lax.axis_size("section") if "x" in orders[0] else 1
    nz = min(4, shards)
    ny = shards // nz
    lead = (nx, shards) if split else (nx, shards, 2)
    blocks = (2 * nz - 1) * ny * nx
    outs = pl.pallas_call(
        partial(gather_kernel, count, pairs, split, orders),
        out_shape=[jax.ShapeDtypeStruct(lead + p.shape, p.dtype) for p in parts]
        + [jax.ShapeDtypeStruct((2,) + p.shape, p.dtype) for p in pair_parts],
        in_specs=[VMEM] * (count + pairs),
        out_specs=[space] * (count + pairs),
        scratch_shapes=[
            DMA((blocks * count * 4,)),
            DMA((count, 2 * nz - 1, ny, nx)),
            DMA((count, 2 * nz - 1, ny, nx)),
            DMA((2, max(pairs, 1))),
            DMA((count + pairs,)),
        ],
        compiler_params=pltpu.CompilerParams(collective_id=ident, has_side_effects=True),
        name=f"gather_{ident}",
    )(*parts, *pair_parts)
    return outs[:count], outs[count:]


def exchange_kernel(relay, src_ref, out_ref, send_sem, recv_sem, relay_send, relay_recv, local_sem):
    me = Place()
    peers = me.replicas * me.shards
    barrier = pltpu.get_barrier_semaphore()
    for p in range(1, peers):
        pl.semaphore_signal(barrier, inc=1, device_id=me.group(p)[1], device_id_type=MESH)
    if relay:
        for i in range(1, me.sections):
            pl.semaphore_signal(barrier, inc=1, device_id=me.peer_x(i), device_id_type=MESH)
    pl.semaphore_wait(barrier, peers - 1 + (me.sections - 1 if relay else 0))
    mine = me.rep * me.shards + me.shard
    section = me.x if relay else 0
    own = pltpu.make_async_copy(src_ref.at[mine], out_ref.at[section, mine], local_sem.at[0])
    own.start()
    sends = []
    for p in range(1, peers):
        place, device = me.group(p)
        copy = remote(
            src_ref.at[place], out_ref.at[section, mine], send_sem.at[p], recv_sem.at[p], device
        )
        copy.start()
        sends.append(copy)
    relays = []

    def forward(p, src, dst):
        for i in range(1, me.sections):
            copy = remote(src, dst, relay_send.at[p, i], relay_recv.at[p, i], me.peer_x(i))
            copy.start()
            relays.append(copy)

    if relay:
        forward(0, src_ref.at[mine], out_ref.at[me.x, mine])
    for p in range(1, peers):
        source, device = me.group(peers - p)
        dst = out_ref.at[section, source]
        remote(dst, dst, send_sem.at[p], recv_sem.at[p], device).wait_recv()
        if relay:
            forward(p, dst, dst)
    if relay:
        for p in range(peers):
            source, _ = me.group(peers - p)
            for i in range(1, me.sections):
                dst = out_ref.at[lax.rem(me.x + me.sections - i, me.sections), source]
                remote(dst, dst, relay_send.at[p, i], relay_recv.at[p, i], me.peer_x(i)).wait_recv()
    for copy in sends + relays:
        copy.wait_send()
    own.wait()


def exchange(blocks, ident, relay=False):
    peers = blocks.shape[0]
    nx = lax.axis_size("section")
    return pl.pallas_call(
        partial(exchange_kernel, relay),
        out_shape=jax.ShapeDtypeStruct((nx if relay else 1,) + blocks.shape, blocks.dtype),
        in_specs=[VMEM],
        out_specs=VMEM,
        scratch_shapes=[DMA((peers,)), DMA((peers,)), DMA((peers, nx)), DMA((peers, nx)), DMA((1,))],
        compiler_params=pltpu.CompilerParams(collective_id=ident, has_side_effects=True),
        name=f"exchange_{ident}",
    )(blocks)


def total_kernel(value_ref, out_ref, held, send_sem, recv_sem):
    me = Place()
    steps = []
    for axis, size in (("replica", me.replicas), ("section", me.sections), ("shard", me.shards)):
        bit = 1
        while bit < size:
            steps.append((axis, bit))
            bit *= 2
    position = {"section": me.x, "replica": me.rep, "shard": me.shard}

    def other(axis, bit):
        index = position[axis]
        set_ = lax.rem(index // bit, 2)
        return {**position, axis: index + bit - 2 * bit * set_}

    barrier = pltpu.get_barrier_semaphore()
    for axis, bit in steps:
        pl.semaphore_signal(barrier, inc=1, device_id=other(axis, bit), device_id_type=MESH)
    pl.semaphore_wait(barrier, len(steps))
    held[0] = value_ref[...]
    copies = []
    for n, (axis, bit) in enumerate(steps):
        copy = remote(held.at[2 * n], held.at[2 * n + 1], send_sem.at[n], recv_sem.at[n], other(axis, bit))
        copy.start()
        copies.append(copy)
        copy.wait_recv()
        summed = held[2 * n] + held[2 * n + 1]
        if n + 1 < len(steps):
            held[2 * n + 2] = summed
        else:
            out_ref[...] = summed
    for copy in copies:
        copy.wait_send()


def total(value, ident):
    steps = sum((lax.axis_size(axis) - 1).bit_length() for axis in every_axis)
    return pl.pallas_call(
        total_kernel,
        out_shape=jax.ShapeDtypeStruct(value.shape, value.dtype),
        in_specs=[VMEM],
        out_specs=VMEM,
        scratch_shapes=[pltpu.VMEM((2 * steps,) + value.shape, value.dtype), DMA((steps,)), DMA((steps,))],
        compiler_params=pltpu.CompilerParams(collective_id=ident, has_side_effects=True),
        name=f"total_{ident}",
    )(value)


def add_rows(dst, src):
    rows = dst.shape[0]
    if rows % 16 != 0:
        dst[...] = (dst[...].astype(jnp.float32) + src[...].astype(jnp.float32)).astype(dst.dtype)
        return
    step = 16

    def body(n, carry):
        at = pl.ds(pl.multiple_of(n * step, step), step)
        dst[at, :] = (dst[at, :].astype(jnp.float32) + src[at, :].astype(jnp.float32)).astype(dst.dtype)
        return carry

    lax.fori_loop(0, rows // step, body, 0)


def reduce_kernel(count, *refs):
    ins, refs = refs[:count], refs[count:]
    outs, refs = refs[:count], refs[count:]
    acc, refs = refs[:count], refs[count:]
    from_core, refs = refs[:count], refs[count:]
    from_x, refs = refs[:count], refs[count:]
    from_y, refs = refs[:count], refs[count:]
    from_z, refs = refs[:count], refs[count:]
    load_sem, core_send, core_recv, send_sem, x_recv, y_recv, z_recv, last_sem = refs
    me = Place()
    nz, ny, nx = me.nz, me.ny, me.sections
    me.greet()
    far = sorted((k for k in range(1 - nz, nz)), key=lambda k: -abs(k))

    def block(k, j, i):
        return lax.rem(me.x + i, nx), (me.z + k) * ny + lax.rem(me.y + j, ny)

    def order_of(core):
        if core == 0:
            return [(k, j, i) for i in range(nx - 1, -1, -1) for j in range(ny - 1, -1, -1) for k in far]
        return [(k, j, i) for j in range(ny - 1, -1, -1) for k in far for i in range(nx - 1, -1, -1)]

    def run(core):
        other = 1 - core
        sends = []

        def start_core(k, j, i):
            x, s = block(k, j, i)

            def go():
                for a in range(count):
                    remote(
                        ins[a].at[x, s, other], from_core[a].at[x, s], core_send.at[a, x, s],
                        core_recv.at[a, x, s], me.partner(),
                    ).start()

            when(me.inside(k), go)

        def start_load(k, j, i):
            x, s = block(k, j, i)

            def go():
                for a in range(count):
                    pltpu.make_async_copy(ins[a].at[x, s, core], acc[a].at[x, s], load_sem.at[a, x, s]).start()

            when(me.inside(k), go)

        for b in order_of(other):
            start_core(*b)
        for b in order_of(core):
            start_load(*b)

        def push(cond, src, dst, sem, device):
            copy = remote(src, dst, send_sem.at[len(sends)], sem, device)
            when(cond, copy.start)
            sends.append((cond, copy))

        def take(cond, dst, src, sem):
            def go():
                remote(src, src, core_send.at[0, 0, 0], sem, me.partner()).wait_recv()
                add_rows(dst, src)

            when(cond, go)

        def join_core(a, k, j, i):
            x, s = block(k, j, i)

            def go():
                pltpu.make_async_copy(ins[a].at[x, s, core], acc[a].at[x, s], load_sem.at[a, x, s]).wait()

            when(me.inside(k), go)
            take(me.inside(k), acc[a].at[x, s], from_core[a].at[x, s], core_recv.at[a, x, s])

        def join_x(a, k, j):
            x, s = block(k, j, 0)
            for p in range(1, nx):
                take(me.inside(k), acc[a].at[x, s], from_x[a].at[p - 1, s], x_recv.at[a, p - 1, s])

        def join_y(a, k, i):
            x, s = block(k, 0, i)
            for p in range(1, ny):
                take(me.inside(k), acc[a].at[x, s], from_y[a].at[p - 1, x, me.z + k], y_recv.at[a, p - 1, x, me.z + k])

        def join_z(a, k, i):
            x, s = block(k, 0, i)
            if k >= 0:
                take(both(me.inside(k), me.inside(-1)), acc[a].at[x, s], from_z[a].at[x, me.z + k], z_recv.at[a, x, me.z + k])
            if k <= 0:
                place = nz if k == 0 else me.z + k
                take(both(me.inside(k), me.inside(1)), acc[a].at[x, s], from_z[a].at[x, place], z_recv.at[a, x, place])

        def send_x(a, k, j, i):
            x, s = block(k, j, i)
            push(me.inside(k), acc[a].at[x, s], from_x[a].at[i - 1, s], x_recv.at[a, i - 1, s], me.peer_x(i))

        def send_y(a, k, j, i):
            x, s = block(k, j, i)
            push(
                me.inside(k), acc[a].at[x, s], from_y[a].at[j - 1, x, me.z + k],
                y_recv.at[a, j - 1, x, me.z + k], me.peer_y(j),
            )

        def send_z(a, k, i):
            x, s = block(k, 0, i)
            place = nz if k == -1 else me.z + k
            push(
                me.inside(k), acc[a].at[x, s], from_z[a].at[x, place], z_recv.at[a, x, place],
                me.line(1 if k > 0 else -1),
            )

        each = range(count)
        if core == 0:
            for i in range(nx - 1, 0, -1):
                for j in range(ny - 1, -1, -1):
                    for k in far:
                        for a in each:
                            join_core(a, k, j, i)
                            send_x(a, k, j, i)
            for j in range(ny - 1, -1, -1):
                for k in far:
                    for a in each:
                        join_core(a, k, j, 0)
            for j in range(ny - 1, 0, -1):
                for k in far:
                    for a in each:
                        join_x(a, k, j)
                        send_y(a, k, j, 0)
            for k in far:
                for a in each:
                    join_x(a, k, 0)
                    join_y(a, k, 0)
                    join_z(a, k, 0)
                    if k != 0:
                        send_z(a, k, 0)
        else:
            for j in range(ny - 1, 0, -1):
                for k in far:
                    for i in range(nx - 1, -1, -1):
                        for a in each:
                            join_core(a, k, j, i)
                            send_y(a, k, j, i)
            for k in far:
                for i in range(nx - 1, -1, -1):
                    for a in each:
                        join_core(a, k, 0, i)
            for k in far:
                for i in range(nx - 1, -1, -1):
                    for a in each:
                        join_y(a, k, i)
                        join_z(a, k, i)
                        if k != 0:
                            send_z(a, k, i)
                        elif i != 0:
                            send_x(a, 0, 0, i)
                        else:
                            join_x(a, 0, 0)
        finals = []
        for a in each:
            copy = remote(
                acc[a].at[me.x, me.shard], outs[a].at[core], last_sem.at[0, a], last_sem.at[1, a], me.partner()
            )
            copy.start()
            finals.append(copy)
            outs[a][core] = acc[a][me.x, me.shard]
        for a in each:
            remote(outs[a].at[other], outs[a].at[other], last_sem.at[0, a], last_sem.at[1, a], me.partner()).wait_recv()
        for cond, copy in sends:
            when(cond, copy.wait_send)
        for copy in finals:
            copy.wait_send()
        for k, j, i in order_of(other):
            x, s = block(k, j, i)

            def finish():
                for a in each:
                    remote(
                        ins[a].at[x, s, other], from_core[a].at[x, s], core_send.at[a, x, s],
                        core_recv.at[a, x, s], me.partner(),
                    ).wait_send()

            when(me.inside(k), finish)

    pl.when(me.core == 0)(lambda: run(0))
    pl.when(me.core == 1)(lambda: run(1))


def reduce_shards(grads, ident):
    count = len(grads)
    nx, shards = lax.axis_size("section"), lax.axis_size("shard")
    nz = min(4, shards)
    ny = shards // nz
    blocks = (2 * nz - 1) * ny * nx

    def scratch(lead):
        return [pltpu.VMEM(lead + g.shape[3:], g.dtype) for g in grads]

    return pl.pallas_call(
        partial(reduce_kernel, count),
        out_shape=[jax.ShapeDtypeStruct(g.shape[2:], g.dtype) for g in grads],
        in_specs=[ANY] * count,
        out_specs=[VMEM] * count,
        scratch_shapes=scratch((nx, shards))
        + scratch((nx, shards))
        + scratch((max(nx - 1, 1), shards))
        + scratch((max(ny - 1, 1), nx, nz))
        + scratch((nx, nz + 1))
        + [
            DMA((count, nx, shards)),
            DMA((count, nx, shards)),
            DMA((count, nx, shards)),
            DMA((blocks * count * 2,)),
            DMA((count, max(nx - 1, 1), shards)),
            DMA((count, max(ny - 1, 1), nx, nz)),
            DMA((count, nx, nz + 1)),
            DMA((2, count)),
        ],
        compiler_params=pltpu.CompilerParams(
            collective_id=ident, has_side_effects=True, vmem_limit_bytes=67043328
        ),
        name=f"reduce_{ident}",
    )(*grads)


def reduce_parts(grads, ident):
    nx, shards = lax.axis_size("section"), lax.axis_size("shard")
    ny = shards // min(4, shards)
    slots = 2 * nx * shards + (nx - 1) * shards + (ny - 1) * nx * 4 + nx * 5 + 4
    groups, used = [[]], 0
    for n, grad in enumerate(grads):
        rows, columns = grad.shape[3:]
        size = slots * (-(-rows // 16) * 16) * columns * 2
        if used + size > 58 * 2**20 and groups[-1]:
            groups.append([])
            used = 0
        groups[-1].append(n)
        used += size
    out = [None] * len(grads)
    for g, group in enumerate(groups):
        for n, value in zip(group, reduce_shards([grads[n] for n in group], ident + g)):
            out[n] = value
    return out


def spread_kernel(columns_ref, weight_ref, out_ref):
    groups, entries = columns_ref.shape[0], columns_ref.shape[2]
    high = out_ref.shape[1] // 128
    each = entries // 8

    def body(g, carry):
        column = columns_ref[g]
        value = weight_ref[g]
        row = lax.broadcasted_iota(jnp.int32, (1, entries), 1) // each
        key = jnp.where(column >= 0, (column // 128) * 8 + row, -1)
        low_part = jnp.where(column >= 0, lax.rem(column, 128), -1)
        left = jnp.where(
            key == lax.broadcasted_iota(jnp.int32, (high * 8, entries), 0), value, 0.0
        )
        right = jnp.where(
            low_part == lax.broadcasted_iota(jnp.int32, (128, entries), 0), 1.0, 0.0
        ).astype(jnp.bfloat16)
        first = left.astype(jnp.bfloat16)
        second = (left - first.astype(jnp.float32)).astype(jnp.bfloat16)
        dims = (((1,), (1,)), ((), ()))
        placed = lax.dot_general(first, right, dims, preferred_element_type=jnp.float32)
        placed = placed + lax.dot_general(second, right, dims, preferred_element_type=jnp.float32)
        at = pl.ds(pl.multiple_of(g * 8, 8), 8)
        for h in range(high):
            out_ref[at, h * 128 : (h + 1) * 128] = placed[h * 8 : (h + 1) * 8]
        return carry

    lax.fori_loop(0, groups, body, 0)


def spread_entries(columns, values, width):
    rows, each = columns.shape
    return pl.pallas_call(
        spread_kernel,
        out_shape=jax.ShapeDtypeStruct((rows, width), jnp.float32),
        in_specs=[VMEM] * 2,
        out_specs=VMEM,
        name="spread_entries",
    )(columns.reshape(rows // 8, 1, 8 * each), values.reshape(rows // 8, 1, 8 * each))


def lower(values):
    return values.astype(jnp.bfloat16)


def product(left, right):
    return jnp.dot(left, right, preferred_element_type=jnp.float32)


def product_left(left, right):
    return lax.dot_general(left, right, (((0,), (0,)), ((), ())), preferred_element_type=jnp.float32)


def product_right(left, right):
    return lax.dot_general(left, right, (((1,), (1,)), ((), ())), preferred_element_type=jnp.float32)


def rms_forward(values, gain):
    inverse = lax.rsqrt(jnp.mean(values * values, axis=-1, keepdims=True) + eps_norm)
    normed = values * inverse
    return (normed * gain, normed, inverse)


def rms_backward(grad_out, normed, inverse, gain):
    grad_normed = grad_out * gain
    grad_in = inverse * (
        grad_normed - normed * jnp.mean(grad_normed * normed, axis=-1, keepdims=True)
    )
    return (grad_in, jnp.sum(grad_out * normed, axis=0))


def path_mask(parent_row, tree_len):
    seg_count = parent_row.shape[0]
    seglen = tree_len // seg_count
    seg_order = jnp.arange(seg_count, dtype=jnp.int32)
    parent_hot = ((parent_row[:, None] == seg_order[None, :]) & (seg_order[:, None] >= 1)).astype(
        jnp.float32
    )
    identity = jnp.eye(seg_count, dtype=jnp.float32)
    power, steps = parent_hot, 1
    reached = identity + parent_hot
    while steps < seg_count:
        reached = jnp.minimum(1.0, jnp.dot(reached, reached))
        steps *= 2
    strict = reached - identity
    seg_of = jnp.arange(tree_len, dtype=jnp.int32) // seglen
    seg_hot = (seg_of[:, None] == seg_order[None, :]).astype(jnp.float32)
    ancestor = jnp.dot(jnp.dot(seg_hot, strict), seg_hot.T)
    places = jnp.arange(tree_len, dtype=jnp.int32)
    inside = (seg_of[:, None] == seg_of[None, :]) & (places[None, :] <= places[:, None])
    return ancestor + inside.astype(jnp.float32)


def attention_scores(queries, keys_all, cumul):
    scale = queries.shape[-1] ** (-0.5)
    scores = (
        jnp.einsum("ihd,jhd->hij", queries, keys_all, preferred_element_type=jnp.float32) * scale
    )
    cumul_heads = cumul.T
    return scores + cumul_heads[:, :, None] - cumul_heads[:, None, :]


def layer_forward(values, allowed, weights):
    (
        weight_in,
        weight_out,
        weight_up,
        weight_down,
        forget_proj,
        forget_bias,
        gain_attention,
        gain_feedforward,
    ) = weights
    tree_len, width = values.shape
    head_count = forget_proj.shape[1]
    normed_out_a, normed_a, inverse_a = rms_forward(values, gain_attention)
    act_a = lower(normed_out_a)
    mixed = lower(product(act_a, weight_in))
    forget_logit = product(act_a, forget_proj) + forget_bias
    cumul = jnp.dot(allowed, jax.nn.log_sigmoid(forget_logit), precision=highest)
    parts = mixed.reshape(tree_len, 3, head_count, width // head_count)
    scores = attention_scores(parts[:, 0], parts[:, 1], cumul)
    scores = jnp.where(allowed[None] > 0, scores, masked_score)
    score_max = jnp.max(scores, axis=-1, keepdims=True)
    exp_scores = jnp.exp(scores - score_max)
    score_sum = jnp.sum(exp_scores, axis=-1, keepdims=True)
    probs = lower(exp_scores / score_sum)
    log_total = score_max + jnp.log(score_sum)
    attended = jnp.einsum("hij,jhd->ihd", probs, parts[:, 2], preferred_element_type=jnp.float32)
    attended = lower(attended.reshape(tree_len, width))
    middle = values + product(attended, weight_out)
    normed_out_b, normed_b, inverse_b = rms_forward(middle, gain_feedforward)
    act_b = lower(normed_out_b)
    gate_up = product(act_b, weight_up)
    half_width = gate_up.shape[1] // 2
    hidden = lower(jax.nn.silu(gate_up[:, :half_width]) * gate_up[:, half_width:])
    output = middle + product(hidden, weight_down)
    return (output, (values, mixed, forget_logit, log_total, attended, middle, gate_up))


def layer_backward(grad_out, allowed, saved, weights):
    (
        weight_in,
        weight_out,
        weight_up,
        weight_down,
        forget_proj,
        forget_bias,
        gain_attention,
        gain_feedforward,
    ) = weights
    values, mixed, forget_logit, log_total, attended, middle, gate_up = saved
    tree_len, width = values.shape
    head_count = forget_proj.shape[1]
    head_width = width // head_count
    half_width = gate_up.shape[1] // 2
    gate = gate_up[:, :half_width]
    upper = gate_up[:, half_width:]
    sigma = jax.nn.sigmoid(gate)
    silu_gate = gate * sigma
    hidden = lower(silu_gate * upper)
    normed_out_b, normed_b, inverse_b = rms_forward(middle, gain_feedforward)
    act_b = lower(normed_out_b)
    grad_branch = lower(grad_out)
    grad_down = lower(product_left(hidden, grad_branch))
    grad_hidden = product_right(grad_branch, weight_down)
    grad_gate = grad_hidden * upper * sigma * (1.0 + gate * (1.0 - sigma))
    grad_upper = grad_hidden * silu_gate
    grad_gate_up = lower(jnp.concatenate([grad_gate, grad_upper], axis=1))
    grad_up = lower(product_left(act_b, grad_gate_up))
    grad_norm_b, grad_gain_b = rms_backward(
        product_right(grad_gate_up, weight_up), normed_b, inverse_b, gain_feedforward
    )
    grad_middle = grad_out + grad_norm_b
    grad_attn_branch = lower(grad_middle)
    grad_out_weight = lower(product_left(attended, grad_attn_branch))
    grad_attended = lower(product_right(grad_attn_branch, weight_out)).reshape(
        tree_len, head_count, head_width
    )
    normed_out_a, normed_a, inverse_a = rms_forward(values, gain_attention)
    act_a = lower(normed_out_a)
    cumul = jnp.dot(allowed, jax.nn.log_sigmoid(forget_logit), precision=highest)
    parts = mixed.reshape(tree_len, 3, head_count, head_width)
    scale = head_width ** (-0.5)
    scores = attention_scores(parts[:, 0], parts[:, 1], cumul)
    scores = jnp.where(allowed[None] > 0, scores, masked_score)
    probs = jnp.exp(scores - log_total)
    grad_probs = jnp.einsum(
        "ihd,jhd->hij", grad_attended, parts[:, 2], preferred_element_type=jnp.float32
    )
    grad_values = jnp.einsum(
        "hij,ihd->jhd", lower(probs), grad_attended, preferred_element_type=jnp.float32
    )
    grad_scores = lower(probs * (grad_probs - jnp.sum(probs * grad_probs, axis=-1, keepdims=True)))
    grad_queries = (
        jnp.einsum("hij,jhd->ihd", grad_scores, parts[:, 1], preferred_element_type=jnp.float32)
        * scale
    )
    grad_keys = (
        jnp.einsum("hij,ihd->jhd", grad_scores, parts[:, 0], preferred_element_type=jnp.float32)
        * scale
    )
    grad_cumul = (
        jnp.sum(grad_scores, axis=2, dtype=jnp.float32)
        - jnp.sum(grad_scores, axis=1, dtype=jnp.float32)
    ).T
    grad_logit = lower(
        jnp.dot(allowed.T, grad_cumul, precision=highest) * jax.nn.sigmoid(-forget_logit)
    )
    grad_mixed = lower(
        jnp.stack([grad_queries, grad_keys, grad_values], axis=1).reshape(tree_len, 3 * width)
    )
    grad_in_weight = lower(product_left(act_a, grad_mixed))
    grad_forget = jnp.concatenate(
        [product_left(act_a, grad_logit), jnp.sum(grad_logit, axis=0, dtype=jnp.float32)[None]],
        axis=0,
    )
    grad_act_a = product_right(grad_mixed, weight_in) + product_right(grad_logit, forget_proj)
    grad_norm_a, grad_gain_a = rms_backward(grad_act_a, normed_a, inverse_a, gain_attention)
    grad_in = grad_middle + grad_norm_a
    return (
        grad_in,
        (grad_in_weight, grad_out_weight, grad_up, grad_down),
        grad_forget,
        jnp.stack([grad_gain_a, grad_gain_b]),
    )


def adam_step(weight, grad, first, second, clip_scale, correct_first, correct_second):
    scaled = clip_scale * grad
    first_new = beta_first * first + (1.0 - beta_first) * scaled
    second_new = beta_second * second + (1.0 - beta_second) * scaled * scaled
    direction = (
        first_new / correct_first / (jnp.sqrt(second_new / correct_second) + adam_eps)
        + decay_rate * weight
    )
    return (first_new, second_new, direction)


def square_sum(values):
    return jnp.sum(values * values)


def packed(parts):
    flat = jnp.concatenate([p.reshape(-1) for p in parts])
    rows = -(-flat.shape[0] // 1024) * 8
    return jnp.pad(flat, (0, rows * 128 - flat.shape[0])).reshape(rows, 128)


def unpacked(flat, like):
    flat, out, at = flat.reshape(-1), [], 0
    for p in like:
        out.append(flat[at : at + p.size].reshape(p.shape))
        at += p.size
    return out


def local(
    tokens,
    parents,
    loss_positions,
    targets,
    teacher_index,
    teacher_probability,
    step_count,
    embed_table,
    table_first,
    table_second,
    attention_in,
    attention_in_first,
    attention_in_second,
    attention_out,
    attention_out_first,
    attention_out_second,
    feedforward_in,
    feedforward_in_first,
    feedforward_in_second,
    feedforward_out,
    feedforward_out_first,
    feedforward_out_second,
    forget_gate,
    forget_first,
    forget_second,
    norm_gains,
    gains_first,
    gains_second,
):
    section_id = lax.axis_index("section")
    replica_id = lax.axis_index("replica")
    shard_id = lax.axis_index("shard")
    sections = lax.axis_size("section")
    replicas = lax.axis_size("replica")
    shards = lax.axis_size("shard")
    group_trees, tree_len = tokens.shape
    rows_each, width = embed_table.shape
    pos_count = loss_positions.shape[1]
    pos_all = group_trees * replicas * pos_count
    owners = replicas * shards
    owner_id = replica_id * shards + shard_id
    own_tree = section_id * shards + shard_id
    table_low = lower(embed_table)

    def own_row(values):
        return lax.dynamic_index_in_dim(values, own_tree, 0, keepdims=False)

    tree_tokens = own_row(tokens)
    token_owner = tree_tokens // rows_each
    token_row = tree_tokens % rows_each
    spots = jnp.arange(tree_len, dtype=jnp.int32)
    earlier = spots[None, :] < spots[:, None]
    same = tree_tokens[:, None] == tree_tokens[None, :]
    is_first = jnp.logical_not(jnp.any(same & earlier, axis=1))
    counted = earlier & (token_owner[:, None] == token_owner[None, :]) & is_first[None, :]
    number_first = jnp.sum(counted.astype(jnp.int32), axis=1)
    number = jnp.sum(jnp.where(same & is_first[None, :], number_first[None, :], 0), axis=1)
    most = jnp.max(number) + 1

    def asked(batch):
        slot = number - batch * batch_rows
        inside = (slot >= 0) & (slot < batch_rows)
        place = jnp.where(inside, token_owner * batch_rows + slot, -1)
        spot_of = jnp.arange(owners * batch_rows, dtype=jnp.int32)
        hot = place[None, :] == spot_of[:, None]
        rows = jnp.max(jnp.where(hot & is_first[None, :], token_row[None, :] + 1, 0), axis=1)
        return rows.reshape(owners, batch_rows), lower(hot)

    def all_devices(part, ident):
        if replicas != 2:
            out = part
            for axis in ("shard", "replica", "section"):
                out = lax.all_gather(out, axis)
            return out
        return jnp.swapaxes(gather([part], ident, space=VMEM)[0][0], 1, 2)

    def wanted(batch, ident):
        rows, hot = asked(batch)
        note = jnp.zeros((1, 128), jnp.int32) + most
        part = jnp.concatenate([jnp.pad(rows, ((0, 0), (0, 128 - batch_rows))), note], axis=0)
        part = jnp.pad(part, ((0, -part.shape[0] % 8), (0, 0)))
        every = all_devices(part, ident)
        mine = lax.dynamic_index_in_dim(every, owner_id, 3, keepdims=False)[..., :batch_rows]
        wish = mine.reshape(sections * owners * batch_rows) - 1
        row_of = jnp.arange(rows_each, dtype=jnp.int32)
        pick = lower(wish[:, None] == row_of[None, :])
        return hot, pick, jnp.max(every[:, :, :, owners, 0])

    def fetch(hot, pick, ident):
        own_pick = lax.dynamic_index_in_dim(
            pick.reshape(sections, owners * batch_rows, rows_each), section_id, 0, keepdims=False
        )
        sent = lower(product(own_pick, table_low)).reshape(owners, batch_rows, width)
        got = exchange(sent, ident)[0].reshape(owners * batch_rows, width)
        return product_left(hot, got)

    hot, pick, most_all = wanted(0, 0)
    batches = (most_all + batch_rows - 1) // batch_rows
    embeds = fetch(hot, pick, 1)

    def more_rows(state):
        batch, total_rows = state
        hot_more, pick_more, _ = wanted(batch, 0)
        return (batch + 1, total_rows + fetch(hot_more, pick_more, 1))

    _, embeds = lax.while_loop(lambda s: s[0] < batches, more_rows, (jnp.int32(1), embeds))

    def halves(weight):
        return lower(weight).reshape(2, weight.shape[1] // 2, weight.shape[2])

    layer_weights = (attention_in, attention_out, feedforward_in, feedforward_out)
    group_data = [targets, teacher_index.reshape(group_trees, -1), teacher_probability.reshape(group_trees, -1)]
    pair_parts = group_data if replicas == 2 else []
    gathered, group_all = gather([halves(w) for w in layer_weights], 2, pair_parts, split=True)
    if replicas != 2:
        group_all = [lax.all_gather(part, "replica") for part in group_data]
    forget_low = lower(forget_gate[:, :width])

    def weights_of(layer):
        mats = [g[layer].reshape(-1, g.shape[-1]) for g in gathered]
        return (
            *mats,
            forget_low[layer],
            forget_gate[layer, width],
            norm_gains[2 * layer],
            norm_gains[2 * layer + 1],
        )

    allowed = path_mask(own_row(parents), tree_len)
    out_0, saved_0 = layer_forward(embeds, allowed, weights_of(0))
    out_1, saved_1 = layer_forward(lower(out_0).astype(jnp.float32), allowed, weights_of(1))

    positions = own_row(loss_positions)
    position_hot = (positions[:, None] == spots[None, :]).astype(jnp.float32)
    picked = jnp.take(out_1, positions, axis=0)
    final_gain = norm_gains[4]
    head_out, head_normed, head_inverse = rms_forward(picked, final_gain)
    head_rows = jnp.swapaxes(all_devices(lower(head_out), 3), 0, 1).reshape(pos_all, width)

    flat = [part.reshape((replicas * group_trees * pos_count,) + (-1,) * (n > 0)) for n, part in enumerate(group_all)]
    target_all, index_all, prob_all = flat

    def owned(ids):
        column = ids - owner_id * rows_each
        return jnp.where((column >= 0) & (column < rows_each), column, -1)

    width_all = -(-rows_each // 128) * 128
    marks = spread_entries(owned(index_all), prob_all, width_all)[:, :rows_each]
    columns = jnp.arange(rows_each, dtype=jnp.int32)
    marks = marks + (owned(target_all)[:, None] == columns[None, :]).astype(jnp.float32)
    logits = product_right(head_rows, table_low)
    linear_part = jnp.sum(logits * marks)
    local_peak = jnp.max(logits, axis=1)
    local_total = jnp.sum(jnp.exp(logits - local_peak[:, None]), axis=1)
    stats = jnp.stack([local_peak, local_total]).reshape(2, -1, 128)
    if replicas == 2:
        stats_all = gather([stats], 4, orders=(("z", "y"), ("z", "y")), space=VMEM)[0][0]
    else:
        stats_all = lax.all_gather(lax.all_gather(stats, "replica"), "shard")
    stats_all = stats_all.reshape(owners, 2, pos_all)
    row_peak = jnp.max(stats_all[:, 0], axis=0)
    row_total = jnp.sum(stats_all[:, 1] * jnp.exp(stats_all[:, 0] - row_peak[None]), axis=0)
    log_norm = row_peak + jnp.log(row_total)
    prob_sum = jnp.sum(prob_all, axis=1)
    row_part = jnp.sum(log_norm * (1.0 + prob_sum) + jnp.sum(prob_all * jnp.log(prob_all), axis=1))
    grad_logits = lower(
        ((1.0 + prob_sum)[:, None] * jnp.exp(logits - log_norm[:, None]) - marks) / pos_all
    )
    own_rows = lax.dynamic_index_in_dim(
        grad_logits.reshape(replicas, sections, shards * pos_count, rows_each), section_id, 1, keepdims=False
    )
    grad_heads = lower(product(own_rows.reshape(-1, rows_each), table_low))
    grad_heads = exchange(grad_heads.reshape(owners, pos_count, width), 5)[0]
    grad_heads = jnp.sum(grad_heads.astype(jnp.float32), axis=0)
    head_table = product_left(grad_logits, head_rows)
    grad_picked, grad_final = rms_backward(grad_heads, head_normed, head_inverse, final_gain)
    grad_top = lax.dot_general(
        position_hot, grad_picked, (((0,), (0,)), ((), ())), precision=highest
    )

    grad_mid, grads_1, forget_1, gains_1 = layer_backward(grad_top, allowed, saved_1, weights_of(1))
    grad_low, grads_0, forget_0, gains_0 = layer_backward(
        lower(grad_mid).astype(jnp.float32), allowed, saved_0, weights_of(0)
    )
    embed_low = lower(grad_low)

    def deliver(hot, pick, ident):
        sent = lower(product(hot, embed_low)).reshape(owners, batch_rows, width)
        got = exchange(sent, ident, relay=True).reshape(sections * owners * batch_rows, width)
        return product_left(pick, got)

    embed_grad = deliver(hot, pick, 6)

    def more_grads(state):
        batch, total_rows = state
        hot_more, pick_more, _ = wanted(batch, 0)
        return (batch + 1, total_rows + deliver(hot_more, pick_more, 6))

    _, embed_grad = lax.while_loop(lambda s: s[0] < batches, more_grads, (jnp.int32(1), embed_grad))
    table_grad = embed_grad + head_table

    stacked = [
        jnp.stack([a, b]).reshape(sections, shards, 2, -1, a.shape[-1]) for a, b in zip(grads_0, grads_1)
    ]
    layer_grads = reduce_parts(stacked, 8)
    if replicas != 2:
        layer_grads = [lax.psum(g * jnp.bfloat16(0.5), "replica") for g in layer_grads]
    layer_grads = [
        g.astype(jnp.float32).reshape(w.shape) for g, w in zip(layer_grads, layer_weights)
    ]

    small = [
        jnp.zeros((8,), jnp.float32),
        jnp.stack([forget_0, forget_1]),
        jnp.concatenate([gains_0, gains_1, grad_final[None]], axis=0),
    ]
    first_section = section_id == 0
    first_replica = replica_id == 0
    square = jnp.where(first_section, square_sum(table_grad), 0.0) + jnp.where(
        first_replica, sum(square_sum(g) for g in layer_grads), 0.0
    )
    linear_once = jnp.where(first_section, linear_part, 0.0)
    small[0] = jnp.stack([square, linear_once] + [jnp.float32(0)] * 6)
    scalars, forget_total, gains_total = unpacked(total(packed(small), 15), small)
    loss_total = (row_part - scalars[1]) / pos_all
    grad_norm = jnp.sqrt(scalars[0] + square_sum(forget_total) + square_sum(gains_total))
    clip_scale = jnp.minimum(1.0, clip_factor / jnp.sqrt(jnp.float32(pos_all)) / grad_norm)
    count_float = step_count.astype(jnp.float32)
    correct_first = 1.0 - jnp.power(beta_first, count_float)
    correct_second = 1.0 - jnp.power(beta_second, count_float)
    adam = partial(
        adam_step, clip_scale=clip_scale, correct_first=correct_first, correct_second=correct_second
    )
    table_first_new, table_second_new, table_direction = adam(
        embed_table, table_grad, table_first, table_second
    )
    layer_firsts = (
        attention_in_first,
        attention_out_first,
        feedforward_in_first,
        feedforward_out_first,
    )
    layer_seconds = (
        attention_in_second,
        attention_out_second,
        feedforward_in_second,
        feedforward_out_second,
    )
    layer_steps = [
        adam(weight, grad, first, second)
        for weight, grad, first, second in zip(
            layer_weights, layer_grads, layer_firsts, layer_seconds
        )
    ]
    section_slot = (jnp.arange(sections, dtype=jnp.int32) == section_id).astype(jnp.float32)
    table_parts = jnp.where(
        first_section, jnp.stack([square_sum(embed_table), square_sum(table_direction)]), 0.0
    )
    layer_parts = jnp.stack(
        [
            jnp.stack([square_sum(weight), square_sum(stepped[2])])
            for weight, stepped in zip(layer_weights, layer_steps)
        ]
    )
    layer_parts = jnp.where(first_replica, layer_parts, 0.0)
    layer_spread = layer_parts[:, None, :] * section_slot[None, :, None]
    norm_parts = [table_parts, layer_spread]
    norm_totals = unpacked(total(packed(norm_parts), 16), norm_parts)
    table_norms = jnp.sqrt(norm_totals[0])
    layer_norms = jnp.sqrt(norm_totals[1])
    new_table = embed_table - learn_rate * (table_norms[0] / table_norms[1]) * table_direction
    mine = jnp.sum(layer_norms * section_slot[None, :, None], axis=1)
    new_layers = []
    for mat_index in range(4):
        ratio = mine[mat_index, 0] / mine[mat_index, 1]
        stepped = layer_steps[mat_index]
        new_layers.append(
            (layer_weights[mat_index] - learn_rate * ratio * stepped[2], stepped[0], stepped[1])
        )
    forget_first_new, forget_second_new, forget_direction = adam(
        forget_gate, forget_total, forget_first, forget_second
    )
    forget_weight_norm = jnp.sqrt(jnp.sum(forget_gate * forget_gate, axis=(1, 2)))
    forget_update_norm = jnp.sqrt(jnp.sum(forget_direction * forget_direction, axis=(1, 2)))
    new_forget = (
        forget_gate
        - learn_rate * (forget_weight_norm / forget_update_norm)[:, None, None] * forget_direction
    )
    gains_first_new, gains_second_new, gains_direction = adam(
        norm_gains, gains_total, gains_first, gains_second
    )
    gains_weight_norm = jnp.sqrt(jnp.sum(norm_gains * norm_gains, axis=1))
    gains_update_norm = jnp.sqrt(jnp.sum(gains_direction * gains_direction, axis=1))
    new_gains = (
        norm_gains - learn_rate * (gains_weight_norm / gains_update_norm)[:, None] * gains_direction
    )
    tensor_norms = jnp.concatenate(
        [
            table_norms[None],
            layer_norms.reshape(4 * sections, 2),
            jnp.stack([forget_weight_norm, forget_update_norm], axis=1),
            jnp.stack([gains_weight_norm, gains_update_norm], axis=1),
        ],
        axis=0,
    )
    return (
        new_table,
        table_first_new,
        table_second_new,
        *new_layers[0],
        *new_layers[1],
        *new_layers[2],
        *new_layers[3],
        new_forget,
        forget_first_new,
        forget_second_new,
        new_gains,
        gains_first_new,
        gains_second_new,
        tensor_norms,
        grad_norm,
        loss_total,
    )


def solution(mesh):
    group = P("replica", None)
    table = P(("replica", "shard"), None)
    layer = P("section", "shard", None)
    in_specs = (
        (group,) * 4
        + (P("replica", None, None),) * 2
        + (P(),)
        + (table,) * 3
        + (layer,) * 12
        + (P(),) * 6
    )
    out_specs = (table,) * 3 + (layer,) * 12 + (P(),) * 9
    return jax.shard_map(local, mesh=mesh, in_specs=in_specs, out_specs=out_specs, check_vma=False)
```

time: 2050 us -> 838 us (0.41)
  waiting for transfers between devices: 1060 us -> 0 us
  Pallas kernels: 0 us -> 448 us
  local copies, waits for them, and re-layouts: 295 us -> 91 us
  other arithmetic: 303 us -> 142 us
  blocking collectives: 152 us -> 0 us
  matrix products: 185 us -> 121 us
    reduce_scatter x7 -> x0, waiting for transfers between devices: 529 us -> none  [the longest x1 121 us: reduce_shards(): lax.psum_scatter(grads[2][None].astype(jnp.bfloat16), 'shard', scatter_di...]
    pallas_call x0 -> x11, Pallas kernels: none -> 448 us  [the longest x4 184 us: gather(): pl.pallas_call(partial(gather_kernel, count, pairs, split, orders), out_s...]
    all_gather x6 -> x0, waiting for transfers between devices: 375 us -> none  [the longest x1 120 us: local(): embed_all = lax.all_gather(embed_low, 'shard', axis=0, tiled=True)]
    gather x6 -> x1, local copies, waits for them, and re-layouts: 232 us -> 1.92 us  [local(): picked = jnp.take(out_1, positions, axis=0)]
    psum x2 -> x0, waiting for transfers between devices: 123 us -> none  [the longest x1 123 us: local(): lax.psum((table_square + layer_square, forget_full, gains_full, loss_part...]
    unnamed x16 -> x8, other arithmetic: 83.6 us -> 0.01 us
    psum x2 -> x0, blocking collectives: 82.5 us -> none  [the longest x1 42.8 us: local(): lax.psum((table_square + layer_square, forget_full, gains_full, loss_part...]
    scatter-add x4 -> x0, other arithmetic: 77.9 us -> none  [the longest x1 40.3 us: local(): jax.ops.segment_sum(embed_all.astype(jnp.float32), slot_index, num_segmen...]
  transfers between devices with their start and end apart: 19 -> 0, of which waited for: 17 -> 0; matrix products, arithmetic and copies ran while one was open for 10% -> 0% of each run, Pallas kernels for 0% -> 0%
where the time goes in v1:
time: 838 us; the launch traced here: 829 us
  Pallas kernels  448 us (53%)
  other arithmetic  142 us (17%)
  matrix products  121 us (14%)
  local copies, waits for them, and re-layouts  91 us (11%)
  between operations  21.5 us (3%)
    pallas_call x4, Pallas kernels, gather(): pl.pallas_call(partial(gather_kernel, count, pairs, split, orders), out_s...  184 us
    pallas_call x1, Pallas kernels, reduce_shards(): pl.pallas_call(partial(reduce_kernel, count), out_shape=[jax.ShapeDtypeSt...  133 us
    pallas_call x3, Pallas kernels, exchange(): pl.pallas_call(partial(exchange_kernel, relay), out_shape=jax.ShapeDtypeS...  74 us
    reduce_sum x16, other arithmetic, square_sum(): return jnp.sum(values * values)  52 us
    dot_general x13, matrix products, product_left(): lax.dot_general(left, right, (((0,), (0,)), ((), ())), preferred_element_...  38.6 us
    pallas_call x2, Pallas kernels, total(): pl.pallas_call(total_kernel, out_shape=jax.ShapeDtypeStruct(value.shape,...  38 us
    dot_general x11, matrix products, product_right(): lax.dot_general(left, right, (((1,), (1,)), ((), ())), preferred_element_...  30.3 us
    unnamed x333, local copies, waits for them, and re-layouts  29.5 us

profile of v1, /device:TPU:0, one launch (start us, length us, event | category | flops | bytes accessed | tf_op | source)
XLA Modules:
  0.0 828.6 jit_solution(5685901549469334616)
XLA Ops:
  5.0 21.9 %gather_0.9 = s32[2,8,2,24,128]{4,3,2,1,0:T(8,128)} custom-call(s32[24,128]{1,0:T(8,128)} %pad.46.refs_0_), custom_call_target="tpu_custom_call" | custom-call | tf_op jit(solution)/shard_map/gather_0/pallas_call | solution.py:231
  28.1 6.7 multiply_reduce_fusion.2
  38.2 25.7 %exchange_1.5 = bf16[1,16,40,768]{3,2,1,0:T(8,128)(2,1)} custom-call(bf16[16,40,768]{2,1,0:T(8,128)(2,1)} %bitcast.414), custom_call_target="tpu_custom_call" | custom-call | tf_op jit(solution)/shard_map/exchange_1/pallas_call | solution.py:302
  77.5 128.4 %gather_2.1 = (bf16[2,8,2,48,2304]{4,3,2,1,0:T(8,128)(2,1)}, bf16[2,8,2,48,768]{4,3,2,1,0:T(8,128)(2,1)}, bf16[2,8,2,48,4096]{4,3,2,1,0:T(8,128)(2,1)}, bf16[2,8...) custom-call(bf16[2,48,2304]{2,1,0:T(8,128)(2,1)} %bitcast.408, ...), custom_call_target="tpu_custom_call" | custom-call | tf_op jit(solution)/shard_map/gather_2/pallas_call | solution.py:231
  205.9 5.3 fusion.197
  282.6 19.4 %gather_3.1 = bf16[2,8,2,16,768]{4,3,2,1,0:T(8,128)(2,1)} custom-call(bf16[16,768]{1,0:T(8,128)(2,1)} %multiply_convert_fusion.12.refs_0_), custom_call_target="tpu_custom_call" | custom-call | tf_op jit(solution)/shard_map/gather_3/pallas_call | solution.py:231
  310.5 14.3 %gather_4.1 = f32[1,8,2,2,4,128]{5,4,3,2,1,0:T(4,128)} custom-call(f32[2,4,128]{2,1,0:T(4,128)} %pad_maximum_fusion.11.refs_0_), custom_call_target="tpu_custom_call" | custom-call | tf_op jit(solution)/shard_map/gather_4/pallas_call | solution.py:231
  332.7 5.6 copy.207
  345.1 19.0 %spread_entries.1 = f32[512,2048]{1,0:T(8,128)} custom-call(s32[64,1,512]{2,1,0:T(1,128)} %and_select_fusion.columns_ref, f32[64,1,512]{2,1,0:T(1,128)} %reshape_reshape.3.weight_ref), custom_call_target="tpu_custom_call" | custom-call | tf_op jit(solution)/shard_map/spread_entries/pallas_call | solution.py:651
  367.5 5.7 multiply_reduce_fusion.5
  375.1 14.9 %exchange_5.1 = bf16[1,16,16,768]{3,2,1,0:T(8,128)(2,1)} custom-call(bf16[16,16,768]{2,1,0:T(8,128)(2,1)} %bitcast.425), custom_call_target="tpu_custom_call" | custom-call | tf_op jit(solution)/shard_map/exchange_5/pallas_call | solution.py:302
  393.7 5.6 multiply_convert_fusion.6
  399.3 6.7 multiply_reduce_fusion.8
  439.1 4.7 multiply_reduce_fusion.3
  481.6 5.4 pad_maximum_fusion.refs_2_
  499.1 132.7 %reduce_8.1 = (bf16[2,48,2304]{2,1,0:T(8,128)(2,1)}, bf16[2,48,768]{2,1,0:T(8,128)(2,1)}, bf16[2,48,4096]{2,1,0:T(8,128)(2,1)}, bf16[2,128,768]{2,1,0:T(8,128)(2,1)}) custom-call(bf16[2,8,2,48,2304]{4,3,2,1,0:T(8,128)(2,1)} %pad_maximum_fusion.1.refs_0_, bf16[2,8,2,48,768]{4,3,2,1,0:T(8,128)(2,1)} %pad_maximum_fusion.5.refs_1_, ...), custom_call_target="tpu_custom_call" | custom-call | tf_op jit(solution)/shard_map/reduce_8/pallas_call | solution.py:572
  646.3 33.5 %exchange_6.5 = bf16[2,16,40,768]{3,2,1,0:T(8,128)(2,1)} custom-call(bf16[16,40,768]{2,1,0:T(8,128)(2,1)} %bitcast.415), custom_call_target="tpu_custom_call" | custom-call | tf_op jit(solution)/shard_map/exchange_6/pallas_call | solution.py:302
  679.9 8.3 %fusion.14 = f32[2000,768]{1,0:T(8,128)} fusion(bf16[1280,768]{1,0:T(8,128)(2,1)} %bitcast.403, s32[1280]{0:T(1024)S(1)} %sub.257), kind=kOutput, calls=%fused_computation.35 | convolution fusion | flops 3934720000 | bytes 8115200 | tf_op jit(solution)/shard_map/dot_general | solution.py:669
  688.2 6.0 while.25
  694.3 7.9 multiply_reduce_fusion.1
  704.5 25.0 %total_15.1 = f32[176,128]{1,0:T(8,128)} custom-call(f32[176,128]{1,0:T(8,128)} %pad_bitcast_fusion.value_ref), custom_call_target="tpu_custom_call" | custom-call | tf_op jit(solution)/shard_map/total_15/pallas_call | solution.py:350
  761.6 17.4 %multiply_reduce_fusion = (f32[]{:T(128)}, f32[2000,768]{1,0:T(8,128)}, f32[2000,768]{1,0:T(8,128)}, f32[2000,768]{1,0:T(8,128)}) fusion(f32[2000,768]{1,0:T(8,128)} %param.39, f32[]{:T(128)S(6)} %sub.302, f32[]{:T(128)S(6)} %sub.301, f32[2000,768]{1,0:T(8,128)} %get-tuple-element.584, f32[]{:T(128)S(6)} %min.19, f32[2000,768]{1,0:T(8,128)} %param.41, ...), kind=kLoop, calls=%fused_computation.47 | loop fusion | flops 24576000 | bytes 43008016 | tf_op jit(solution)/shard_map/reduce_sum | solution.py:859
  781.0 13.1 %total_16.1 = f32[8,128]{1,0:T(8,128)} custom-call(f32[8,128]{1,0:T(8,128)} %fusion.148.value_ref), custom_call_target="tpu_custom_call" | custom-call | tf_op jit(solution)/shard_map/total_16/pallas_call | solution.py:350
  819.9 6.2 multiply_subtract_fusion
  (554 shorter events, 268.0 us)
Async XLA Ops:
  2.8 61.1 %copy-start.128 = (s32[320]{0:T(512)}, s32[320]{0:T(512)S(1)}, u32[]{:S(2)}) copy-start(s32[320]{0:T(512)S(1)} %fusion.161) | copy-start | bytes 3844
  68.1 386.0 %copy-start = (f32[320,768]{1,0:T(8,128)}, f32[320,768]{1,0:T(8,128)S(1)}, u32[]{:S(2)}) copy-start(f32[320,768]{1,0:T(8,128)S(1)} %get-tuple-element.315) | copy-start | bytes 2949124
  68.7 188.5 %copy-start.114 = (f32[768]{0:T(1024)}, f32[768]{0:T(1024)S(1)}, u32[]{:S(2)}) copy-start(f32[768]{0:T(1024)S(1)} %get-tuple-element.420) | copy-start | bytes 9220
  68.7 337.3 %copy-start.96 = (f32[768]{0:T(1024)}, f32[768]{0:T(1024)S(1)}, u32[]{:S(2)}) copy-start(f32[768]{0:T(1024)S(1)} %get-tuple-element.419) | copy-start | bytes 9220
  68.7 364.3 %copy-start.92 = (f32[768]{0:T(1024)}, f32[768]{0:T(1024)S(1)}, u32[]{:S(2)}) copy-start(f32[768]{0:T(1024)S(1)} %get-tuple-element.421) | copy-start | bytes 9220
  68.8 385.4 %copy-start.110 = (f32[768]{0:T(1024)}, f32[768]{0:T(1024)S(1)}, u32[]{:S(2)}) copy-start(f32[768]{0:T(1024)S(1)} %get-tuple-element.422) | copy-start | bytes 9220
  69.9 148.9 %copy-start.28 = (bf16[320,768]{1,0:T(8,128)(2,1)}, bf16[320,768]{1,0:T(8,128)(2,1)S(1)}, u32[]{:S(2)}) copy-start(bf16[320,768]{1,0:T(8,128)(2,1)S(1)} %multiply_convert_fusion.11) | copy-start | bytes 1474564
  218.6 38.7 %copy-start.82 = (bf16[2,769,12]{1,2,0:T(8,128)(2,1)}, bf16[2,769,12]{1,2,0:T(8,128)(2,1)S(1)}, u32[]{:S(2)}) copy-start(bf16[2,769,12]{1,2,0:T(8,128)(2,1)S(1)} %copy.248) | copy-start | bytes 110740
  232.0 197.9 %copy-start.14 = (f32[320,768]{1,0:T(8,128)}, f32[320,768]{1,0:T(8,128)S(1)}, u32[]{:S(2)}) copy-start(f32[320,768]{1,0:T(8,128)S(1)} %get-tuple-element.566) | copy-start | bytes 2949124
  268.0 131.3 %copy-start.30 = (f32[320,768]{1,0:T(8,128)}, f32[320,768]{1,0:T(8,128)S(1)}, u32[]{:S(2)}) copy-start(f32[320,768]{1,0:T(8,128)S(1)} %get-tuple-element.572) | copy-start | bytes 2949124
  434.7 52.3 %copy-start.9 = (f32[320,768]{1,0:T(8,128)}, f32[320,768]{1,0:T(8,128)S(1)}, u32[]{:S(2)}) copy-start(f32[320,768]{1,0:T(8,128)S(1)} %multiply_add_fusion.3) | copy-start | bytes 2949124
  631.7 12.8 %copy-start.129 = (s32[320]{0:T(512)S(1)}, s32[320]{0:T(512)}, u32[]{:S(2)}) copy-start(s32[320]{0:T(512)} %copy-done.128) | copy-start | bytes 3844
  644.5 35.3 %copy-start.95 = (s32[2,2,8,40]{3,2,1,0:T(8,128)S(1)}, s32[2,2,8,40]{3,2,1,0:T(8,128)}, u32[]{:S(2)}) copy-start(s32[2,2,8,40]{3,2,1,0:T(8,128)} %copy-done.94) | copy-start | bytes 15364
  694.3 44.4 %copy-start.91 = (f32[5,768]{1,0:T(8,128)S(1)}, f32[5,768]{1,0:T(8,128)}, u32[]{:S(2)}) copy-start(f32[5,768]{1,0:T(8,128)} %param.57) | copy-start | bytes 46084
  694.3 44.4 %copy-start.125 = (f32[5,768]{1,0:T(8,128)S(1)}, f32[5,768]{1,0:T(8,128)}, u32[]{:S(2)}) copy-start(f32[5,768]{1,0:T(8,128)} %param.59) | copy-start | bytes 46084
  694.3 44.4 %copy-start.126 = (f32[5,768]{1,0:T(8,128)S(1)}, f32[5,768]{1,0:T(8,128)}, u32[]{:S(2)}) copy-start(f32[5,768]{1,0:T(8,128)} %param.58) | copy-start | bytes 46084
  694.3 47.6 %copy-start.73 = (f32[2,769,12]{1,0,2:T(2,128)S(1)}, f32[2,769,12]{1,0,2:T(2,128)}, u32[]{:S(2)}) copy-start(f32[2,769,12]{1,0,2:T(2,128)} %param.54) | copy-start | bytes 221476
  694.3 47.6 %copy-start.108 = (f32[2,769,12]{1,0,2:T(2,128)S(1)}, f32[2,769,12]{1,0,2:T(2,128)}, u32[]{:S(2)}) copy-start(f32[2,769,12]{1,0,2:T(2,128)} %param.56) | copy-start | bytes 221476
  694.3 47.6 %copy-start.109 = (f32[2,769,12]{1,0,2:T(2,128)S(1)}, f32[2,769,12]{1,0,2:T(2,128)}, u32[]{:S(2)}) copy-start(f32[2,769,12]{1,0,2:T(2,128)} %param.55) | copy-start | bytes 221476
  702.2 41.4 %copy-start.63 = (bf16[2,48,2304]{2,1,0:T(8,128)(2,1)S(1)}, bf16[2,48,2304]{2,1,0:T(8,128)(2,1)}, u32[]{:S(2)}) copy-start(bf16[2,48,2304]{2,1,0:T(8,128)(2,1)} %get-tuple-element.324) | copy-start | bytes 1327108
  702.2 41.5 %copy-start.17 = (f32[1,96,2304]{2,1,0:T(8,128)S(1)}, f32[1,96,2304]{2,1,0:T(8,128)}, u32[]{:S(2)}) copy-start(f32[1,96,2304]{2,1,0:T(8,128)} %param.42) | copy-start | bytes 2654212
  702.2 41.5 %copy-start.71 = (f32[1,96,2304]{2,1,0:T(8,128)S(1)}, f32[1,96,2304]{2,1,0:T(8,128)}, u32[]{:S(2)}) copy-start(f32[1,96,2304]{2,1,0:T(8,128)} %param.44) | copy-start | bytes 2654212
  761.4 17.6 %copy-start.140 = (f32[2]{0:T(128)}, f32[2]{0:T(128)S(1)}, u32[]{:S(2)}) copy-start(f32[2]{0:T(128)S(1)} %compare_convert_fusion) | copy-start | bytes 28
  794.1 25.8 %slice-start.8 = ((s8[6144000]{0:T(1024)(128)(4,1)}), s8[1949696]{0:T(1024)(128)(4,1)S(1)}, s32[]{:S(2)}) async-start(s8[6144000]{0:T(1024)(128)(4,1)} %bitcast.348), calls=%async_computation.8 | async-start | bytes 3899392
  (142 other events, 586.4 us)

commit v2 on v1

v2 whole, which is shorter than its diff:
```python
from functools import partial

import jax
import jax.numpy as jnp
from jax import lax
from jax.experimental import pallas as pl
from jax.experimental.pallas import tpu as pltpu
from jax.sharding import PartitionSpec as P

MESH = pl.DeviceIdType.MESH
VMEM = pl.BlockSpec(memory_space=pltpu.VMEM)
ANY = pl.BlockSpec(memory_space=pl.ANY)
DMA = pltpu.SemaphoreType.DMA
eps_norm = 1e-06
beta_first = 0.9
beta_second = 0.999
adam_eps = 1e-10
decay_rate = 0.01
learn_rate = 0.2
clip_factor = 8.0
highest = lax.Precision.HIGHEST
masked_score = -1e30
batch_rows = 32
every_axis = ("section", "replica", "shard")


class Place:
    def __init__(self):
        self.sections = lax.axis_size("section")
        self.replicas = lax.axis_size("replica")
        self.shards = lax.axis_size("shard")
        self.nz = min(4, self.shards)
        self.ny = self.shards // self.nz
        self.x = lax.axis_index("section")
        self.rep = lax.axis_index("replica")
        self.shard = lax.axis_index("shard")
        self.core = lax.rem(self.rep, 2)
        self.z = self.shard // self.ny
        self.y = lax.rem(self.shard, self.ny)

    def at(self, section=None, rep=None, z=None, y=None, shard=None):
        if shard is None:
            shard = (self.z if z is None else z) * self.ny + (self.y if y is None else y)
        return {
            "section": self.x if section is None else section,
            "replica": self.rep if rep is None else rep,
            "shard": shard,
        }

    def peer_x(self, i):
        return self.at(section=lax.rem(self.x + i, self.sections))

    def peer_y(self, j):
        return self.at(y=lax.rem(self.y + j, self.ny))

    def line(self, step):
        return self.at(z=self.z + step)

    def partner(self):
        return self.at(rep=self.rep + 1 - 2 * self.core)

    def group(self, p):
        count = self.replicas * self.shards
        place = lax.rem(self.rep * self.shards + self.shard + p, count)
        return place, self.at(rep=place // self.shards, shard=lax.rem(place, self.shards))

    def device(self, i, p):
        place, _ = self.group(p)
        section = lax.rem(self.x + i, self.sections)
        return place, self.at(section=section, rep=place // self.shards, shard=lax.rem(place, self.shards))

    def greet_all(self):
        barrier = pltpu.get_barrier_semaphore()
        peers = self.replicas * self.shards
        for i in range(self.sections):
            for p in range(peers):
                if i or p:
                    pl.semaphore_signal(barrier, inc=1, device_id=self.device(i, p)[1], device_id_type=MESH)
        pl.semaphore_wait(barrier, self.sections * peers - 1)

    def greet_group(self):
        barrier = pltpu.get_barrier_semaphore()
        peers = self.replicas * self.shards
        for p in range(1, peers):
            pl.semaphore_signal(barrier, inc=1, device_id=self.group(p)[1], device_id_type=MESH)
        for i in range(1, self.sections):
            pl.semaphore_signal(barrier, inc=1, device_id=self.peer_x(i), device_id_type=MESH)
        pl.semaphore_wait(barrier, peers + self.sections - 2)

    def inside(self, k):
        if k == 0:
            return None
        return self.z + k < self.nz if k > 0 else self.z + k >= 0

    def greet(self, use_x=True):
        barrier = pltpu.get_barrier_semaphore()

        def signal(device):
            pl.semaphore_signal(barrier, inc=1, device_id=device, device_id_type=MESH)

        count = 1
        if use_x:
            for i in range(1, self.sections):
                signal(self.peer_x(i))
                count += 1
        for j in range(1, self.ny):
            signal(self.peer_y(j))
            count += 1
        signal(self.partner())
        up, down = self.inside(1), self.inside(-1)
        pl.when(up)(lambda: signal(self.line(1)))
        pl.when(down)(lambda: signal(self.line(-1)))
        ends = jnp.minimum(self.z, 1) + jnp.minimum(self.nz - 1 - self.z, 1)
        pl.semaphore_wait(barrier, count + ends)


def when(cond, fn):
    if cond is None:
        fn()
    else:
        pl.when(cond)(fn)


def both(a, b):
    if a is None:
        return b
    if b is None:
        return a
    return jnp.logical_and(a, b)


def remote(src, dst, send, recv, device):
    return pltpu.make_async_remote_copy(
        src_ref=src, dst_ref=dst, send_sem=send, recv_sem=recv, device_id=device, device_id_type=MESH
    )


def rows_errand(me, ask_ref, table_ref, asked_ref, got_ref, hot, found, ask_sem, row_sem, own_sem):
    peers = me.replicas * me.shards
    mine = me.rep * me.shards + me.shard
    width = table_ref.shape[1]
    asks = []
    for i in range(me.sections):
        for p in range(peers):
            place, device = me.device(i, p)
            if i or p:
                asks.append(remote(ask_ref.at[place], asked_ref.at[me.x, mine], ask_sem.at[0, i, p], ask_sem.at[1, i, p], device))
    for copy in asks:
        copy.start()
    own_ask = pltpu.make_async_copy(ask_ref.at[mine], asked_ref.at[me.x, mine], own_sem.at[0])
    own_ask.start()
    rows = [
        remote(found.at[me.group(p)[0]], got_ref.at[mine], row_sem.at[0, p], row_sem.at[1, p], me.group(p)[1])
        for p in range(1, peers)
    ]
    own_rows = pltpu.make_async_copy(found.at[mine], got_ref.at[mine], own_sem.at[1])

    def look_up():
        own_ask.wait()
        for i in range(me.sections):
            for p in range(peers):
                if i or p:
                    source = lax.rem(mine + peers - p, peers)
                    dst = asked_ref.at[lax.rem(me.x + me.sections - i, me.sections), source]
                    remote(dst, dst, ask_sem.at[0, i, p], ask_sem.at[1, i, p], me.partner()).wait_recv()
        wish = asked_ref[me.x].reshape(peers, 128).astype(jnp.float32).T
        column = lax.broadcasted_iota(jnp.int32, (batch_rows, table_ref.shape[0]), 1).astype(jnp.float32) + 1.0
        for s in range(peers):
            ours = wish[0:batch_rows, s : s + 1] == column
            hot[s * batch_rows : (s + 1) * batch_rows, :] = jnp.where(ours, 1.0, 0.0).astype(jnp.bfloat16)

        def take(n, carry):
            at = pl.ds(pl.multiple_of(n * 256, 256), 256)
            values = jnp.dot(hot[...], table_ref[:, at], preferred_element_type=jnp.float32)
            found[:, :, at] = values.reshape(peers, batch_rows, 256).astype(jnp.bfloat16)
            return carry

        lax.fori_loop(0, width // 256, take, 0)
        own_rows.start()
        for copy in rows:
            copy.start()

    def finish():
        for p in range(1, peers):
            source = lax.rem(mine + peers - p, peers)
            dst = got_ref.at[source]
            remote(dst, dst, row_sem.at[0, p], row_sem.at[1, p], me.partner()).wait_recv()
        own_rows.wait()
        for copy in asks + rows:
            copy.wait_send()

    return {1: look_up, "end": finish}


def gather_kernel(count, pairs, split, orders, errand, *refs):
    ins, refs = refs[:count], refs[count:]
    pair_ins, refs = refs[:pairs], refs[pairs:]
    errand_in, refs = refs[: 2 * errand], refs[2 * errand :]
    outs, refs = refs[:count], refs[count:]
    pair_outs, refs = refs[:pairs], refs[pairs:]
    errand_out, refs = refs[: 2 * errand], refs[2 * errand :]
    errand_refs = errand_in + errand_out
    send_sem, recv_sem, cross_sem, pair_sem, local_sem = refs[:5]
    me = Place()
    nz, ny, nx = me.nz, me.ny, me.sections
    if "x" not in orders[0][0][0]:
        nx = 1
    hooks = {}
    if errand:
        me.greet_all()
        hooks = rows_errand(me, *errand_refs, *refs[5:])
    else:
        me.greet(use_x=nx > 1)

    def slot(ref, k, j, i, half):
        section = lax.rem(me.x + i, nx) if nx > 1 else 0
        return ref.at[section, (me.z + k) * ny + lax.rem(me.y + j, ny), half]

    locals_ = []
    for a in range(count):
        if split:
            dst = outs[a].at[me.x if nx > 1 else 0, me.shard]
        else:
            dst = outs[a].at[me.x if nx > 1 else 0, me.shard, me.core]
        locals_.append(pltpu.make_async_copy(ins[a], dst, local_sem.at[a]))
    for p in range(pairs):
        locals_.append(
            pltpu.make_async_copy(pair_ins[p], pair_outs[p].at[me.core], local_sem.at[count + p])
        )
    for copy in locals_:
        copy.start()
    pair_copies = [
        remote(pair_ins[p], pair_outs[p].at[me.core], pair_sem.at[0, p], pair_sem.at[1, p], me.partner())
        for p in range(pairs)
    ]

    def run(core, plan):
        sends = []

        def push(cond, src, dst, device, sem):
            copy = remote(src, dst, send_sem.at[len(sends)], sem, device)
            when(cond, copy.start)
            sends.append((cond, copy))

        def sem_of(a, k, j, i):
            return recv_sem.at[a, k + nz - 1, j, i]

        def spread(order, arrays, k, j, i, via):
            cond = me.inside(k)
            own = via is None
            later = order if own else order[order.index(via) + 1 :]
            for a in arrays:
                dst = slot(outs[a], k, j, i, core)
                src = dst
                if own:
                    src = ins[a].at[core] if split else ins[a]
                else:
                    arrival = remote(dst, dst, send_sem.at[0], sem_of(a, k, j, i), me.partner())
                    when(cond, arrival.wait_recv)
                steps = []
                if via == "z":
                    steps = [-1 if k > 0 else 1]
                elif "z" in later:
                    steps = [1, -1]
                for step in steps:
                    push(both(cond, me.inside(step)), src, dst, me.line(step), sem_of(a, k - step, j, i))
                if "y" in later:
                    for p in range(1, ny):
                        push(cond, src, dst, me.peer_y(p), sem_of(a, k, (j - p) % ny, i))
                if "x" in later:
                    for p in range(1, nx):
                        push(cond, src, dst, me.peer_x(p), sem_of(a, k, j, (i - p) % nx))
                if not (own and split):
                    push(cond, src, dst, me.partner(), cross_sem.at[a, k + nz - 1, j, i])

        events = []
        for order, arrays in plan:
            for k in range(1 - nz, nz):
                for j in range(ny):
                    for i in range(nx):
                        via = [d for d in order if {"z": k, "y": j, "x": i}[d] != 0]
                        hops = abs(k) + (j != 0) + (i != 0)
                        stage = order.index(via[-1]) if via else -1
                        events.append((hops, stage, k, j, i, order, arrays, via[-1] if via else None))
        events.sort(key=lambda e: e[:5])
        for n, (hops, stage, k, j, i, order, arrays, via) in enumerate(events):
            spread(order, arrays, k, j, i, via)
            if n + 1 < len(events) and events[n + 1][0] == hops:
                continue
            if hops == 0:
                for copy in pair_copies:
                    copy.start()
            if hops in hooks:
                hooks[hops]()
        for hops, stage, k, j, i, order, arrays, via in events:
            if via is None and split:
                continue
            for a in arrays:
                dst = slot(outs[a], k, j, i, 1 - core)
                arrival = remote(dst, dst, send_sem.at[0], cross_sem.at[a, k + nz - 1, j, i], me.partner())
                when(me.inside(k), arrival.wait_recv)
        for cond, copy in sends:
            when(cond, copy.wait_send)

    for core, plan in enumerate(orders):
        pl.when(me.core == core)(partial(run, core, plan))
    if errand:
        hooks["end"]()
    for p in range(pairs):
        pair_copies[p].wait_send()
        remote(
            pair_ins[p], pair_outs[p].at[1 - me.core], pair_sem.at[0, p], pair_sem.at[1, p], me.partner()
        ).wait_recv()
    for copy in locals_:
        copy.wait()


def gather(parts, ident, pair_parts=(), split=False, use_x=True, space=ANY, errand=()):
    count, pairs = len(parts), len(pair_parts)
    every = list(range(count))
    if not use_x:
        orders = [[(("z", "y"), every)]] * 2
    elif split:
        orders = [[(("z", "y", "x"), every)], [(("x", "z", "y"), every[:-1]), (("x", "y", "z"), every[-1:])]]
    else:
        orders = [[(("z", "y", "x"), every)], [(("x", "z", "y"), every)]]
    shards = lax.axis_size("shard")
    nx = lax.axis_size("section") if use_x else 1
    nz = min(4, shards)
    ny = shards // nz
    lead = (nx, shards) if split else (nx, shards, 2)
    blocks = (2 * nz - 1) * ny * nx
    errand_shapes, errand_scratch = [], []
    if errand:
        asks, table = errand
        peers, wide = asks.shape[0], table.shape[1]
        errand_shapes = [
            jax.ShapeDtypeStruct((nx, peers) + asks.shape[1:], asks.dtype),
            jax.ShapeDtypeStruct((peers, batch_rows, wide), table.dtype),
        ]
        errand_scratch = [
            pltpu.VMEM((peers * batch_rows, table.shape[0]), table.dtype),
            pltpu.VMEM((peers, batch_rows, wide), table.dtype),
            DMA((2, nx, peers)),
            DMA((2, peers)),
            DMA((2,)),
        ]
    outs = pl.pallas_call(
        partial(gather_kernel, count, pairs, split, orders, bool(errand)),
        out_shape=[jax.ShapeDtypeStruct(lead + p.shape, p.dtype) for p in parts]
        + [jax.ShapeDtypeStruct((2,) + p.shape, p.dtype) for p in pair_parts]
        + errand_shapes,
        in_specs=[VMEM] * (count + pairs + len(errand)),
        out_specs=[space] * (count + pairs) + [VMEM] * len(errand_shapes),
        scratch_shapes=[
            DMA((blocks * count * 4,)),
            DMA((count, 2 * nz - 1, ny, nx)),
            DMA((count, 2 * nz - 1, ny, nx)),
            DMA((2, max(pairs, 1))),
            DMA((count + pairs,)),
        ]
        + errand_scratch,
        compiler_params=pltpu.CompilerParams(collective_id=ident, has_side_effects=True),
        name=f"gather_{ident}",
    )(*parts, *pair_parts, *errand)
    return outs[:count], outs[count : count + pairs], outs[count + pairs :]


def exchange_kernel(relay, src_ref, out_ref, send_sem, recv_sem, relay_send, relay_recv, local_sem):
    me = Place()
    peers = me.replicas * me.shards
    barrier = pltpu.get_barrier_semaphore()
    for p in range(1, peers):
        pl.semaphore_signal(barrier, inc=1, device_id=me.group(p)[1], device_id_type=MESH)
    if relay:
        for i in range(1, me.sections):
            pl.semaphore_signal(barrier, inc=1, device_id=me.peer_x(i), device_id_type=MESH)
    pl.semaphore_wait(barrier, peers - 1 + (me.sections - 1 if relay else 0))
    mine = me.rep * me.shards + me.shard
    section = me.x if relay else 0
    own = pltpu.make_async_copy(
        src_ref.at[mine if src_ref.shape[0] > 1 else 0], out_ref.at[section, mine], local_sem.at[0]
    )
    own.start()
    sends = []
    for p in range(1, peers):
        place, device = me.group(p)
        copy = remote(
            src_ref.at[place if src_ref.shape[0] > 1 else 0], out_ref.at[section, mine], send_sem.at[p], recv_sem.at[p], device
        )
        copy.start()
        sends.append(copy)
    relays = []

    def forward(p, src, dst):
        for i in range(1, me.sections):
            copy = remote(src, dst, relay_send.at[p, i], relay_recv.at[p, i], me.peer_x(i))
            copy.start()
            relays.append(copy)

    if relay:
        forward(0, src_ref.at[mine], out_ref.at[me.x, mine])
    for p in range(1, peers):
        source, device = me.group(peers - p)
        dst = out_ref.at[section, source]
        remote(dst, dst, send_sem.at[p], recv_sem.at[p], device).wait_recv()
        if relay:
            forward(p, dst, dst)
    if relay:
        for p in range(peers):
            source, _ = me.group(peers - p)
            for i in range(1, me.sections):
                dst = out_ref.at[lax.rem(me.x + me.sections - i, me.sections), source]
                remote(dst, dst, relay_send.at[p, i], relay_recv.at[p, i], me.peer_x(i)).wait_recv()
    for copy in sends + relays:
        copy.wait_send()
    own.wait()


def exchange(blocks, ident, relay=False):
    peers = lax.axis_size("replica") * lax.axis_size("shard")
    nx = lax.axis_size("section")
    return pl.pallas_call(
        partial(exchange_kernel, relay),
        out_shape=jax.ShapeDtypeStruct((nx if relay else 1, peers) + blocks.shape[1:], blocks.dtype),
        in_specs=[VMEM],
        out_specs=VMEM,
        scratch_shapes=[DMA((peers,)), DMA((peers,)), DMA((peers, nx)), DMA((peers, nx)), DMA((1,))],
        compiler_params=pltpu.CompilerParams(collective_id=ident, has_side_effects=True),
        name=f"exchange_{ident}",
    )(blocks)


def total_steps(me):
    steps = []
    for axis, size in (("replica", me.replicas), ("section", me.sections), ("shard", me.shards)):
        bit = 1
        while bit < size:
            steps.append((axis, bit))
            bit *= 2
    return steps


def total_kernel(count, *refs):
    ins, refs = refs[:count], refs[count:]
    outs, refs = refs[:count], refs[count:]
    held, refs = refs[:count], refs[count:]
    send_sem, recv_sem = refs
    me = Place()
    steps = total_steps(me)
    position = {"section": me.x, "replica": me.rep, "shard": me.shard}

    def other(axis, bit):
        index = position[axis]
        return {**position, axis: index + bit - 2 * bit * lax.rem(index // bit, 2)}

    barrier = pltpu.get_barrier_semaphore()
    for axis, bit in steps:
        pl.semaphore_signal(barrier, inc=1, device_id=other(axis, bit), device_id_type=MESH)
    pl.semaphore_wait(barrier, len(steps))
    for a in range(count):
        held[a][0] = ins[a][...]
    copies = []
    for n, (axis, bit) in enumerate(steps):
        step_copies = [
            remote(held[a].at[2 * n], held[a].at[2 * n + 1], send_sem.at[n, a], recv_sem.at[n, a], other(axis, bit))
            for a in range(count)
        ]
        for copy in step_copies:
            copy.start()
        copies += step_copies
        for a in range(count):
            step_copies[a].wait_recv()
            summed = held[a][2 * n] + held[a][2 * n + 1]
            if n + 1 < len(steps):
                held[a][2 * n + 2] = summed
            else:
                outs[a][...] = summed
    for copy in copies:
        copy.wait_send()


def total(values, ident):
    count = len(values)
    steps = sum((lax.axis_size(axis) - 1).bit_length() for axis in every_axis)
    return pl.pallas_call(
        partial(total_kernel, count),
        out_shape=[jax.ShapeDtypeStruct(v.shape, v.dtype) for v in values],
        in_specs=[VMEM] * count,
        out_specs=[VMEM] * count,
        scratch_shapes=[pltpu.VMEM((2 * steps,) + v.shape, v.dtype) for v in values]
        + [DMA((steps, count)), DMA((steps, count))],
        compiler_params=pltpu.CompilerParams(collective_id=ident, has_side_effects=True),
        name=f"total_{ident}",
    )(*values)


def add_rows(dst, src):
    rows = dst.shape[0]
    if rows % 16 != 0:
        dst[...] = (dst[...].astype(jnp.float32) + src[...].astype(jnp.float32)).astype(dst.dtype)
        return
    step = 16

    def body(n, carry):
        at = pl.ds(pl.multiple_of(n * step, step), step)
        dst[at, :] = (dst[at, :].astype(jnp.float32) + src[at, :].astype(jnp.float32)).astype(dst.dtype)
        return carry

    lax.fori_loop(0, rows // step, body, 0)


def grads_errand(me, sent, got, sum_in, sum_out, *refs):
    n_sums = len(sum_in)
    held, refs = refs[:n_sums], refs[n_sums:]
    row_sem, relay_sem, own_sem, sum_sem = refs
    peers = me.replicas * me.shards
    mine = me.rep * me.shards + me.shard
    direct = [
        remote(sent.at[me.group(p)[0]], got.at[me.x, mine], row_sem.at[0, p], row_sem.at[1, p], me.group(p)[1])
        for p in range(1, peers)
    ]
    own = pltpu.make_async_copy(sent.at[mine], got.at[me.x, mine], own_sem.at[0])
    relays = []

    def source(p):
        return lax.rem(mine + peers - p, peers)

    def begin():
        own.start()
        for copy in direct:
            copy.start()
        for i in range(1, me.sections):
            copy = remote(sent.at[mine], got.at[me.x, mine], relay_sem.at[0, 0, i], relay_sem.at[1, 0, i], me.peer_x(i))
            copy.start()
            relays.append(copy)

    steps = total_steps(me)
    position = {"section": me.x, "replica": me.rep, "shard": me.shard}

    def other(axis, bit):
        index = position[axis]
        return {**position, axis: index + bit - 2 * bit * lax.rem(index // bit, 2)}

    def sum_copies(n):
        axis, bit = steps[n]
        return [
            remote(held[a].at[2 * n], held[a].at[2 * n + 1], sum_sem.at[0, n, a], sum_sem.at[1, n, a], other(axis, bit))
            for a in range(n_sums)
        ]

    def sum_step(n):
        if n == 0:
            for a in range(n_sums):
                held[a][0] = sum_in[a][...]
        else:
            for a, copy in enumerate(sum_copies(n - 1)):
                copy.wait_recv()
                summed = held[a][2 * n - 2] + held[a][2 * n - 1]
                if n < len(steps):
                    held[a][2 * n] = summed
                else:
                    sum_out[a][...] = summed
        if n < len(steps):
            for copy in sum_copies(n):
                copy.start()

    def relay(first, last):
        for p in range(first, last):
            dst = got.at[me.x, source(p)]
            remote(dst, dst, row_sem.at[0, p], row_sem.at[1, p], me.partner()).wait_recv()
            for i in range(1, me.sections):
                copy = remote(dst, dst, relay_sem.at[0, p, i], relay_sem.at[1, p, i], me.peer_x(i))
                copy.start()
                relays.append(copy)

    def finish():
        for p in range(peers):
            for i in range(1, me.sections):
                dst = got.at[lax.rem(me.x + me.sections - i, me.sections), source(p)]
                remote(dst, dst, relay_sem.at[0, p, i], relay_sem.at[1, p, i], me.partner()).wait_recv()
        for p in range(peers):
            for i in range(1, me.sections):
                dst = got.at[me.x, source(p)]
                remote(dst, dst, relay_sem.at[0, p, i], relay_sem.at[1, p, i], me.peer_x(i)).wait_send()
        for copy in direct:
            copy.wait_send()
        for n in range(len(steps)):
            for copy in sum_copies(n):
                copy.wait_send()
        own.wait()

    hooks = [begin, partial(sum_step, 0)]
    middle = (peers + 1) // 2
    pieces = [partial(relay, 1, middle), partial(relay, middle, peers)]
    sums = [partial(sum_step, n) for n in range(1, len(steps) + 1)]
    hooks += [sums[0], pieces[0], sums[1], pieces[1]] + sums[2:] + [finish]
    return hooks


def reduce_kernel(count, sections, sums, *refs):
    ins, refs = [refs[a * sections : (a + 1) * sections] for a in range(count)], refs[count * sections :]
    sum_in, refs = refs[:sums], refs[sums:]
    sent = None
    if sums:
        sent, refs = refs[0], refs[1:]
    outs, refs = refs[:count], refs[count:]
    sum_out, refs = refs[:sums], refs[sums:]
    if sums:
        got, refs = refs[0], refs[1:]
    acc, refs = refs[:count], refs[count:]
    from_core, refs = refs[:count], refs[count:]
    from_x, refs = refs[:count], refs[count:]
    from_y, refs = refs[:count], refs[count:]
    from_z, refs = refs[:count], refs[count:]
    load_sem, core_send, core_recv, send_sem, x_recv, y_recv, z_recv, last_sem = refs[:8]
    me = Place()
    nz, ny, nx = me.nz, me.ny, me.sections
    hooks = []
    if sums:
        me.greet_group()
        hooks = grads_errand(me, sent, got, sum_in, sum_out, *refs[8 : 8 + sums], *refs[8 + sums :])
    else:
        me.greet()

    far = sorted((k for k in range(1 - nz, nz)), key=lambda k: -abs(k))

    def block(k, j, i):
        return lax.rem(me.x + i, nx), (me.z + k) * ny + lax.rem(me.y + j, ny)

    def order_of(core):
        if core == 0:
            return [(k, j, i) for i in range(nx - 1, -1, -1) for j in range(ny - 1, -1, -1) for k in far]
        return [(k, j, i) for j in range(ny - 1, -1, -1) for k in far for i in range(nx - 1, -1, -1)]

    def run(core):
        other = 1 - core
        sends = []

        def start_core(k, j, i):
            x, s = block(k, j, i)

            def go(layer):
                for a in range(count):
                    remote(
                        ins[a][layer].at[s, other], from_core[a].at[x, s], core_send.at[a, x, s],
                        core_recv.at[a, x, s], me.partner(),
                    ).start()

            for layer in range(nx):
                when(both(me.inside(k), x == layer), partial(go, layer))

        def start_load(k, j, i):
            x, s = block(k, j, i)

            def go(layer):
                for a in range(count):
                    pltpu.make_async_copy(ins[a][layer].at[s, core], acc[a].at[x, s], load_sem.at[a, x, s]).start()

            for layer in range(nx):
                when(both(me.inside(k), x == layer), partial(go, layer))

        for b in order_of(other):
            start_core(*b)
        for b in order_of(core):
            start_load(*b)
        todo = list(hooks)

        def errand(last=False):
            while todo and (last or len(todo) > 1):
                todo.pop(0)()
                if not last:
                    break

        errand()

        def push(cond, src, dst, sem, device):
            copy = remote(src, dst, send_sem.at[len(sends)], sem, device)
            when(cond, copy.start)
            sends.append((cond, copy))

        def take(cond, dst, src, sem):
            def go():
                remote(src, src, core_send.at[0, 0, 0], sem, me.partner()).wait_recv()
                add_rows(dst, src)

            when(cond, go)

        def join_core(a, k, j, i):
            x, s = block(k, j, i)

            def go():
                pltpu.make_async_copy(ins[a][0].at[s, core], acc[a].at[x, s], load_sem.at[a, x, s]).wait()

            when(me.inside(k), go)
            take(me.inside(k), acc[a].at[x, s], from_core[a].at[x, s], core_recv.at[a, x, s])

        def join_x(a, k, j):
            x, s = block(k, j, 0)
            for p in range(1, nx):
                take(me.inside(k), acc[a].at[x, s], from_x[a].at[p - 1, s], x_recv.at[a, p - 1, s])

        def join_y(a, k, i):
            x, s = block(k, 0, i)
            for p in range(1, ny):
                take(me.inside(k), acc[a].at[x, s], from_y[a].at[p - 1, x, me.z + k], y_recv.at[a, p - 1, x, me.z + k])

        def join_z(a, k, i):
            x, s = block(k, 0, i)
            if k >= 0:
                take(both(me.inside(k), me.inside(-1)), acc[a].at[x, s], from_z[a].at[x, me.z + k], z_recv.at[a, x, me.z + k])
            if k <= 0:
                place = nz if k == 0 else me.z + k
                take(both(me.inside(k), me.inside(1)), acc[a].at[x, s], from_z[a].at[x, place], z_recv.at[a, x, place])

        def send_x(a, k, j, i):
            x, s = block(k, j, i)
            push(me.inside(k), acc[a].at[x, s], from_x[a].at[i - 1, s], x_recv.at[a, i - 1, s], me.peer_x(i))

        def send_y(a, k, j, i):
            x, s = block(k, j, i)
            push(
                me.inside(k), acc[a].at[x, s], from_y[a].at[j - 1, x, me.z + k],
                y_recv.at[a, j - 1, x, me.z + k], me.peer_y(j),
            )

        def send_z(a, k, i):
            x, s = block(k, 0, i)
            place = nz if k == -1 else me.z + k
            push(
                me.inside(k), acc[a].at[x, s], from_z[a].at[x, place], z_recv.at[a, x, place],
                me.line(1 if k > 0 else -1),
            )

        each = range(count)
        if core == 0:
            for i in range(nx - 1, 0, -1):
                for j in range(ny - 1, -1, -1):
                    for k in far:
                        for a in each:
                            join_core(a, k, j, i)
                            send_x(a, k, j, i)
                        errand()
            for j in range(ny - 1, -1, -1):
                for k in far:
                    for a in each:
                        join_core(a, k, j, 0)
            for j in range(ny - 1, 0, -1):
                for k in far:
                    for a in each:
                        join_x(a, k, j)
                        send_y(a, k, j, 0)
            for k in far:
                for a in each:
                    join_x(a, k, 0)
                    join_y(a, k, 0)
                    join_z(a, k, 0)
                    if k != 0:
                        send_z(a, k, 0)
        else:
            for j in range(ny - 1, 0, -1):
                for k in far:
                    for i in range(nx - 1, -1, -1):
                        for a in each:
                            join_core(a, k, j, i)
                            send_y(a, k, j, i)
                        errand()
            for k in far:
                for i in range(nx - 1, -1, -1):
                    for a in each:
                        join_core(a, k, 0, i)
            for k in far:
                for i in range(nx - 1, -1, -1):
                    for a in each:
                        join_y(a, k, i)
                        join_z(a, k, i)
                        if k != 0:
                            send_z(a, k, i)
                        elif i != 0:
                            send_x(a, 0, 0, i)
                        else:
                            join_x(a, 0, 0)
        errand(last=True)
        finals = []
        for a in each:
            copy = remote(
                acc[a].at[me.x, me.shard], outs[a].at[core], last_sem.at[0, a], last_sem.at[1, a], me.partner()
            )
            copy.start()
            finals.append(copy)
            outs[a][core] = acc[a][me.x, me.shard]
        for a in each:
            remote(outs[a].at[other], outs[a].at[other], last_sem.at[0, a], last_sem.at[1, a], me.partner()).wait_recv()
        for cond, copy in sends:
            when(cond, copy.wait_send)
        for copy in finals:
            copy.wait_send()
        for k, j, i in order_of(other):
            x, s = block(k, j, i)

            def finish():
                for a in each:
                    remote(
                        ins[a][0].at[s, other], from_core[a].at[x, s], core_send.at[a, x, s],
                        core_recv.at[a, x, s], me.partner(),
                    ).wait_send()

            when(me.inside(k), finish)

    pl.when(me.core == 0)(lambda: run(0))
    pl.when(me.core == 1)(lambda: run(1))


def reduce_shards(grads, ident, errand=None):
    count = len(grads)
    nx, shards = lax.axis_size("section"), lax.axis_size("shard")
    nz = min(4, shards)
    ny = shards // nz
    blocks = (2 * nz - 1) * ny * nx

    def scratch(lead):
        return [pltpu.VMEM(lead + g[0].shape[2:], g[0].dtype) for g in grads]

    extra_in, extra_shapes, extra_scratch, sums = [], [], [], 0
    if errand:
        values, sent = errand
        sums, peers = len(values), sent.shape[0]
        steps = sum((lax.axis_size(axis) - 1).bit_length() for axis in every_axis)
        extra_in = [*values, sent]
        extra_shapes = [jax.ShapeDtypeStruct(v.shape, v.dtype) for v in values] + [
            jax.ShapeDtypeStruct((nx,) + sent.shape, sent.dtype)
        ]
        extra_scratch = [pltpu.VMEM((2 * steps,) + v.shape, v.dtype) for v in values] + [
            DMA((2, peers)),
            DMA((2, peers, nx)),
            DMA((1,)),
            DMA((2, steps, sums)),
        ]
    return pl.pallas_call(
        partial(reduce_kernel, count, nx, sums),
        out_shape=[jax.ShapeDtypeStruct(g[0].shape[1:], g[0].dtype) for g in grads] + extra_shapes,
        in_specs=[ANY] * (count * nx) + [VMEM] * sums + [ANY] * bool(sums),
        out_specs=[VMEM] * (count + sums) + [ANY] * bool(sums),
        scratch_shapes=scratch((nx, shards))
        + scratch((nx, shards))
        + scratch((max(nx - 1, 1), shards))
        + scratch((max(ny - 1, 1), nx, nz))
        + scratch((nx, nz + 1))
        + [
            DMA((count, nx, shards)),
            DMA((count, nx, shards)),
            DMA((count, nx, shards)),
            DMA((blocks * count * 2,)),
            DMA((count, max(nx - 1, 1), shards)),
            DMA((count, max(ny - 1, 1), nx, nz)),
            DMA((count, nx, nz + 1)),
            DMA((2, count)),
        ]
        + extra_scratch,
        compiler_params=pltpu.CompilerParams(
            collective_id=ident, has_side_effects=True, vmem_limit_bytes=67043328
        ),
        name=f"reduce_{ident}",
    )(*[layer for g in grads for layer in g], *extra_in)


def reduce_parts(grads, ident, errand):
    nx, shards = lax.axis_size("section"), lax.axis_size("shard")
    ny = shards // min(4, shards)
    slots = 2 * nx * shards + (nx - 1) * shards + (ny - 1) * nx * 4 + nx * 5 + 4
    groups, used = [[]], 0
    for n, grad in enumerate(grads):
        rows, columns = grad[0].shape[2:]
        size = slots * (-(-rows // 16) * 16) * columns * 2
        if used + size > 58 * 2**20 and groups[-1]:
            groups.append([])
            used = 0
        groups[-1].append(n)
        used += size
    out = [None] * len(grads)
    for g, group in enumerate(groups):
        done = reduce_shards([grads[n] for n in group], ident + g, errand if g == 0 else None)
        for n, value in zip(group, done):
            out[n] = value
        if g == 0:
            extra = done[len(group) :]
    return out, extra


def spread_kernel(columns_ref, weight_ref, target_ref, out_ref):
    groups, entries = columns_ref.shape[0], columns_ref.shape[2]
    high = out_ref.shape[1] // 128
    each = entries // 8

    def body(g, carry):
        column = columns_ref[g]
        value = weight_ref[g]
        row = lax.broadcasted_iota(jnp.int32, (1, entries), 1) // each
        key = jnp.where(column >= 0, (column // 128) * 8 + row, -1)
        low_part = jnp.where(column >= 0, lax.rem(column, 128), -1)
        left = jnp.where(
            key == lax.broadcasted_iota(jnp.int32, (high * 8, entries), 0), value, 0.0
        ).astype(jnp.bfloat16)
        right = jnp.where(
            low_part == lax.broadcasted_iota(jnp.int32, (128, entries), 0), 1.0, 0.0
        ).astype(jnp.bfloat16)
        dims = (((1,), (1,)), ((), ()))
        placed = lax.dot_general(left, right, dims, preferred_element_type=jnp.float32)
        at = pl.ds(pl.multiple_of(g * 8, 8), 8)
        target = target_ref[at, :]
        for h in range(high):
            one = jnp.where(lax.broadcasted_iota(jnp.int32, (8, 128), 1) + 128 * h == target, 1.0, 0.0)
            out_ref[at, h * 128 : (h + 1) * 128] = placed[h * 8 : (h + 1) * 8] + one
        return carry

    lax.fori_loop(0, groups, body, 0)


def spread_entries(columns, values, targets, width):
    rows, each = columns.shape
    return pl.pallas_call(
        spread_kernel,
        out_shape=jax.ShapeDtypeStruct((rows, width), jnp.float32),
        in_specs=[VMEM] * 3,
        out_specs=VMEM,
        name="spread_entries",
    )(columns.reshape(rows // 8, 1, 8 * each), values.reshape(rows // 8, 1, 8 * each), targets[:, None])


def ask_kernel(owners, token_row, token_col, owner_row, owner_col, row_col, hot_ref, ask_ref):
    count = token_row.shape[1]
    i = lax.broadcasted_iota(jnp.int32, (count, count), 0)
    j = lax.broadcasted_iota(jnp.int32, (count, count), 1)
    same = token_col[...] == token_row[...]
    kin = owner_col[...] == owner_row[...]
    first_col = 1.0 - jnp.max(jnp.where(same & (j < i), 1.0, 0.0), axis=1, keepdims=True)
    first_row = 1.0 - jnp.max(jnp.where(same & (i < j), 1.0, 0.0), axis=0, keepdims=True)
    place_col = jnp.sum(jnp.where(kin & (j < i), first_row, 0.0), axis=1, keepdims=True)
    place_row = jnp.sum(jnp.where(kin & (i < j), first_col, 0.0), axis=0, keepdims=True)
    number_col = jnp.sum(jnp.where(same, first_row * place_row, 0.0), axis=1, keepdims=True)
    number_row = jnp.sum(jnp.where(same, first_col * place_col, 0.0), axis=0, keepdims=True)
    size = float(batch_rows)
    slot_row = jnp.where(number_row < size, owner_row[...].astype(jnp.float32) * size + number_row, -1.0)
    slot_col = jnp.where(number_col < size, owner_col[...].astype(jnp.float32) * size + number_col, -1.0)
    spots = owners * batch_rows
    part = 512 if spots % 512 == 0 else spots
    for at in range(0, spots, part):
        line = lax.broadcasted_iota(jnp.int32, (part, count), 0).astype(jnp.float32) + float(at)
        hot_ref[at : at + part, :] = jnp.where(slot_row == line, 1.0, 0.0).astype(jnp.bfloat16)
    most = jnp.max(number_col) + 1.0
    wanted = first_col * (row_col[...].astype(jnp.float32) + 1.0)
    lane = lax.broadcasted_iota(jnp.int32, (1, 128), 1)
    for at in range(0, spots, 128):
        line = lax.broadcasted_iota(jnp.int32, (count, 128), 1).astype(jnp.float32) + float(at)
        rows = jnp.max(jnp.where(slot_col == line, wanted, 0.0), axis=0, keepdims=True)
        for n in range(128 // batch_rows):
            shifted = pltpu.roll(rows, (128 - n * batch_rows) % 128, 1) if n else rows
            values = jnp.where(lane < batch_rows, shifted, jnp.where(lane == 127, most, 0.0))
            ask_ref[at // batch_rows + n] = values.astype(jnp.int32)


def ask_rows(tokens, owner, row, owners):
    count = tokens.shape[0]
    return pl.pallas_call(
        partial(ask_kernel, owners),
        out_shape=[
            jax.ShapeDtypeStruct((owners * batch_rows, count), jnp.bfloat16),
            jax.ShapeDtypeStruct((owners, 1, 128), jnp.int32),
        ],
        in_specs=[VMEM] * 5,
        out_specs=[VMEM] * 2,
        name="ask_rows",
    )(tokens[None], tokens[:, None], owner[None], owner[:, None], row[:, None])


def table_kernel(asked_ref, got_ref, head_ref, *refs):
    layers, table_ref, square_ref = refs[:-2], refs[-2], refs[-1]
    sections, peers = asked_ref.shape[:2]
    each = 128 // batch_rows
    lane = lax.broadcasted_iota(jnp.int32, (1, 128), 1)
    lists = []
    for at in range(0, sections * peers, each):
        wish = jnp.zeros((1, 128), jnp.int32)
        for n in range(each):
            part = asked_ref[(at + n) // peers, (at + n) % peers]
            part = pltpu.roll(part, n * batch_rows, 1) if n else part
            wish = jnp.where((lane >= n * batch_rows) & (lane < (n + 1) * batch_rows), part, wish)
        lists.append(wish)
    wish = jnp.concatenate(lists, axis=1)
    rows = table_ref.shape[0]
    step = 400 if rows % 400 == 0 else rows

    def body(n, square):
        at = pl.ds(pl.multiple_of(n * step, 8), step) if step != rows else slice(0, rows)
        row = lax.broadcasted_iota(jnp.int32, (step, wish.shape[1]), 0) + 1 + n * step
        hot = jnp.where(row == wish, 1.0, 0.0).astype(jnp.bfloat16)
        values = head_ref[at, :] + jnp.dot(hot, got_ref[...], preferred_element_type=jnp.float32)
        table_ref[at, :] = values
        return square + jnp.sum(values * values, axis=0, keepdims=True)

    zero = jnp.zeros((1, table_ref.shape[1]), jnp.float32)
    square = jnp.sum(lax.fori_loop(0, rows // step, body, zero)) if step != rows else jnp.sum(body(0, zero))
    square = jnp.where(lax.axis_index("section") == 0, square, 0.0)
    others = jnp.float32(0)
    for layer in layers:
        for half in range(2):
            values = layer[half].astype(jnp.float32)
            others = others + jnp.sum(values * values)
    square = square + jnp.where(lax.axis_index("replica") == 0, others, 0.0)
    corner = lax.broadcasted_iota(jnp.int32, (8, 128), 0) + lax.broadcasted_iota(jnp.int32, (8, 128), 1)
    square_ref[...] = jnp.where(corner == 0, square, 0.0)


def table_gradient(rows_each, asked, got, head_table, layer_grads):
    width = head_table.shape[1]
    return pl.pallas_call(
        table_kernel,
        out_shape=[
            jax.ShapeDtypeStruct((rows_each, width), jnp.float32),
            jax.ShapeDtypeStruct((8, 128), jnp.float32),
        ],
        in_specs=[VMEM] * (3 + len(layer_grads)),
        out_specs=[VMEM] * 2,
        compiler_params=pltpu.CompilerParams(vmem_limit_bytes=56 * 2**20),
        name="table_gradient",
    )(asked, got, head_table, *layer_grads)
def dims_nt(left, right):
    return lax.dot_general(left, right, (((1,), (1,)), ((), ())), preferred_element_type=jnp.float32)


def dims_tn(left, right):
    return lax.dot_general(left, right, (((0,), (0,)), ((), ())), preferred_element_type=jnp.float32)


def three_parts(values):
    first = lower(values)
    rest = values - first.astype(jnp.float32)
    second = lower(rest)
    return first, second, lower(rest - second.astype(jnp.float32))


def log_sigmoid(values):
    return jnp.minimum(values, 0.0) - jnp.log1p(jnp.exp(-jnp.abs(values)))


def norm_parts(values, gain):
    inverse = lax.rsqrt(jnp.mean(values * values, axis=-1, keepdims=True) + eps_norm)
    normed = values * inverse
    return normed, inverse, lower(normed * gain)


class HeadPair:
    def __init__(self, tree_len, cumul):
        self.lane = lax.broadcasted_iota(jnp.int32, (tree_len, 128), 1)
        self.parts = jnp.concatenate(three_parts(cumul), axis=1)
        self.row = lax.broadcasted_iota(jnp.int32, (384, 128), 0)
        self.column = lax.broadcasted_iota(jnp.int32, (384, 128), 1)

    def augmented(self, head, side, query, key):
        start = 64 - 64 * side
        mine = (self.lane >= 64 * side) & (self.lane < 64 * side + 64)
        wanted = (self.row - 128 * (self.row // 128) == head) & (self.column == self.row // 128 + start)
        placed = product(self.parts, lower(jnp.where(wanted, 1.0, 0.0)))
        wanted = (self.row - 128 * (self.row // 128) == head) & (self.column == self.row // 128 + start + 3)
        negative = product(self.parts, lower(jnp.where(wanted, -1.0, 0.0)))
        ones_q = jnp.where((self.lane >= start + 3) & (self.lane < start + 6), 1.0, 0.0)
        ones_k = jnp.where((self.lane >= start) & (self.lane < start + 3), 1.0, 0.0)
        query = lower(jnp.where(mine, query.astype(jnp.float32) * 0.125, placed + ones_q))
        key = lower(jnp.where(mine, key.astype(jnp.float32), negative + ones_k))
        return query, key, mine


def forward_kernel(layer, round_input, x_ref, allowed_ref, w_in, w_out, w_up, w_down, forget_ref, bias_ref, gain_ref,
                   y_ref, qkv_ref, logit_ref, lse_ref, att_ref, mid_ref, gu_ref,
                   b_in, b_out, b_up, b_down, gu_buf, hidden, mask, sem, gu_sem):
    tree_len, width = x_ref.shape
    heads = width // 64
    half = hidden.shape[1]
    loads = [
        pltpu.make_async_copy(src.at[layer], dst, sem.at[n])
        for n, (src, dst) in enumerate(((w_in, b_in), (w_out, b_out), (w_up, b_up), (w_down, b_down)))
    ]
    for copy in loads:
        copy.start()
    x = x_ref[...]
    if round_input:
        x = lower(x).astype(jnp.float32)
    _, _, act = norm_parts(x, gain_ref[0:1, :])
    allowed = allowed_ref[...]
    mask[...] = jnp.where(allowed > 0, 0.0, masked_score)
    logit = product(act, forget_ref[...]) + bias_ref[...]
    logit_ref[...] = logit
    cumul = sum(product(allowed, part) for part in three_parts(log_sigmoid(logit)))
    loads[0].wait()

    def project(n, carry):
        at = pl.ds(pl.multiple_of(n * 256, 256), 256)
        qkv_ref[:, at] = lower(product(act, b_in[:, at]))
        return carry

    lax.fori_loop(0, 3 * width // 256, project, 0)
    pair = HeadPair(tree_len, cumul)
    lse_ref[...] = jnp.zeros_like(lse_ref)

    def attend(p, carry):
        base = pl.multiple_of(p * 128, 128)
        query = qkv_ref[:, pl.ds(base, 128)]
        key = qkv_ref[:, pl.ds(base + width, 128)]
        value = qkv_ref[:, pl.ds(base + 2 * width, 128)]
        outs = []
        for side in range(2):
            q_side, k_side, mine = pair.augmented(2 * p + side, side, query, key)
            scores = dims_nt(q_side, k_side) + mask[...]
            peak = jnp.max(scores, axis=1, keepdims=True)
            probs = jnp.exp(scores - peak)
            count = jnp.sum(probs, axis=1, keepdims=True)
            outs.append(product(lower(probs * (1.0 / count)), value))
            lse_ref[...] = jnp.where(pair.lane == 2 * p + side, peak + jnp.log(count), lse_ref[...])
        att_ref[:, pl.ds(base, 128)] = lower(jnp.where(pair.lane < 64, outs[0], outs[1]))
        return carry

    lax.fori_loop(0, heads // 2, attend, 0)
    loads[1].wait()
    middle = x + product(att_ref[...], b_out[...])
    mid_ref[...] = middle
    _, _, act_b = norm_parts(middle, gain_ref[1:2, :])
    loads[2].wait()

    def stores(n):
        return [
            pltpu.make_async_copy(
                gu_buf.at[:, pl.ds(n * 512 + s * half, 512)], gu_ref.at[:, pl.ds(n * 512 + s * half, 512)], gu_sem.at[n, s]
            )
            for s in range(2)
        ]

    for n in range(half // 512):
        def expand(h, carry):
            at = pl.ds(pl.multiple_of(n * 512 + h * 256, 256), 256)
            at_up = pl.ds(pl.multiple_of(half + n * 512 + h * 256, 256), 256)
            gate = product(act_b, b_up[:, at])
            upper = product(act_b, b_up[:, at_up])
            gu_buf[:, at] = gate
            gu_buf[:, at_up] = upper
            hidden[:, at] = lower(gate / (1.0 + jnp.exp(-gate)) * upper)
            return carry

        lax.fori_loop(0, 2, expand, 0)
        for copy in stores(n):
            copy.start()
    loads[3].wait()

    def contract(n, carry):
        at = pl.ds(pl.multiple_of(n * 256, 256), 256)
        y_ref[:, at] = mid_ref[:, at] + product(hidden[...], b_down[:, at])
        return carry

    lax.fori_loop(0, width // 256, contract, 0)
    for n in range(half // 512):
        for copy in stores(n):
            copy.wait()


def layer_forward(layer, round_input, values, allowed, mats, forget_w, forget_b, gains):
    tree_len, width = values.shape
    w_in, w_out, w_up, w_down = mats
    half = w_down.shape[1]
    f32, b16 = jnp.float32, jnp.bfloat16
    shape = jax.ShapeDtypeStruct
    return pl.pallas_call(
        partial(forward_kernel, layer, round_input),
        out_shape=[
            shape((tree_len, width), f32),
            shape((tree_len, 3 * width), b16),
            shape((tree_len, 128), f32),
            shape((tree_len, 128), f32),
            shape((tree_len, width), b16),
            shape((tree_len, width), f32),
            shape((tree_len, 2 * half), f32),
        ],
        in_specs=[VMEM] * 2 + [ANY] * 4 + [VMEM] * 3,
        out_specs=[VMEM] * 6 + [ANY],
        scratch_shapes=[pltpu.VMEM(w.shape[1:], b16) for w in mats]
        + [
            pltpu.VMEM((tree_len, 2 * half), f32),
            pltpu.VMEM((tree_len, half), b16),
            pltpu.VMEM((tree_len, tree_len), f32),
            DMA((4,)),
            DMA((half // 512, 2)),
        ],
        compiler_params=pltpu.CompilerParams(vmem_limit_bytes=56 * 2**20),
        name=f"forward_{layer}",
    )(values, allowed, *mats, forget_w, forget_b, gains)


def backward_kernel(layer, round_input, round_grad, dy_ref, x_ref, allowed_ref, qkv_ref, logit_ref, lse_ref, att_ref,
                    mid_ref, forget_ref, gain_ref, gu_hbm, w_in, w_out, w_up, w_down,
                    dx_ref, dforget_ref, dgain_ref, dw_in, dw_out, dw_up, dw_down,
                    b_in, b_out, b_up, b_down, gu, dqkv, act_t, grad_b, mask, dcum,
                    g_in, g_out, g_up, g_down, sem, gu_sem, store_sem):
    tree_len, width = x_ref.shape
    heads = width // 64
    half = b_down.shape[0]
    chunk = 256
    gu_loads = [
        [
            pltpu.make_async_copy(
                gu_hbm.at[:, pl.ds(n * chunk + s * half, chunk)], gu.at[:, pl.ds(n * chunk + s * half, chunk)], gu_sem.at[n, s]
            )
            for s in range(2)
        ]
        for n in range(half // chunk)
    ]
    loads = [
        pltpu.make_async_copy(src.at[layer], dst, sem.at[n])
        for n, (src, dst) in enumerate(((w_in, b_in), (w_out, b_out), (w_up, b_up), (w_down, b_down)))
    ]
    loads[3].start()
    for pair_copies in gu_loads:
        for copy in pair_copies:
            copy.start()
    for n in (2, 1, 0):
        loads[n].start()
    dy = dy_ref[...]
    if round_grad:
        dy = lower(dy).astype(jnp.float32)
    branch = lower(dy)
    normed_b, inverse_b, act_b = norm_parts(mid_ref[...], gain_ref[1:2, :])
    act_t[...] = lower((normed_b * gain_ref[1:2, :]).T)
    grad_b[...] = jnp.zeros_like(grad_b)
    loads[3].wait()
    for copies in gu_loads:
        for copy in copies:
            copy.wait()
    loads[2].wait()

    def feed(n, carry):
        at = pl.ds(pl.multiple_of(n * chunk, chunk), chunk)
        at_up = pl.ds(pl.multiple_of(half + n * chunk, chunk), chunk)
        gate, upper = gu[:, at], gu[:, at_up]
        sigma = 1.0 / (1.0 + jnp.exp(-gate))
        silu = gate * sigma
        hidden = lower(silu * upper)
        grad_hidden = dims_nt(branch, b_down[at, :])
        g_down[at, :] = lower(dims_tn(hidden, branch))
        grad_gate = lower(grad_hidden * upper * sigma * (1.0 + gate * (1.0 - sigma)))
        grad_upper = lower(grad_hidden * silu)
        g_up[:, at] = lower(product(act_t[...], grad_gate))
        g_up[:, at_up] = lower(product(act_t[...], grad_upper))
        grad_b[...] += dims_nt(grad_gate, b_up[:, at]) + dims_nt(grad_upper, b_up[:, at_up])
        return carry

    lax.fori_loop(0, half // chunk, feed, 0)
    stores = [
        pltpu.make_async_copy(src, dst, store_sem.at[n])
        for n, (src, dst) in enumerate(((g_down, dw_down), (g_up, dw_up), (g_out, dw_out), (g_in, dw_in)))
    ]
    stores[0].start()
    stores[1].start()

    def norm_backward(grad, normed, inverse, gain):
        grad_normed = grad * gain
        back = inverse * (grad_normed - normed * jnp.mean(grad_normed * normed, axis=-1, keepdims=True))
        return back, jnp.sum(grad * normed, axis=0, keepdims=True)

    back_b, dgain_b = norm_backward(grad_b[...], normed_b, inverse_b, gain_ref[1:2, :])
    grad_mid = dy + back_b
    branch_a = lower(grad_mid)
    g_out[...] = lower(dims_tn(att_ref[...], branch_a))
    stores[2].start()
    loads[1].wait()
    att_ref_grad = lower(dims_nt(branch_a, b_out[...]))
    x = x_ref[...]
    if round_input:
        x = lower(x).astype(jnp.float32)
    normed_a, inverse_a, act_a = norm_parts(x, gain_ref[0:1, :])
    act_t[...] = lower((normed_a * gain_ref[0:1, :]).T)
    allowed = allowed_ref[...]
    mask[...] = jnp.where(allowed > 0, 0.0, masked_score)
    logit = logit_ref[...]
    cumul = sum(product(allowed, part) for part in three_parts(log_sigmoid(logit)))
    pair = HeadPair(tree_len, cumul)
    dcum[...] = jnp.zeros_like(dcum)
    grad_att = grad_b
    grad_att[...] = att_ref_grad.astype(jnp.float32)

    def attend(p, carry):
        base = pl.multiple_of(p * 128, 128)
        query = qkv_ref[:, pl.ds(base, 128)]
        key = qkv_ref[:, pl.ds(base + width, 128)]
        value = qkv_ref[:, pl.ds(base + 2 * width, 128)]
        grad_out = grad_att[:, pl.ds(base, 128)]
        grad_low = lower(grad_out)
        results = []
        for side in range(2):
            head = 2 * p + side
            start = 64 - 64 * side
            q_side, k_side, mine = pair.augmented(head, side, query, key)
            lse = jnp.sum(jnp.where(pair.lane == head, lse_ref[...], 0.0), axis=1, keepdims=True)
            probs = jnp.exp(dims_nt(q_side, k_side) + (mask[...] - lse))
            grad_probs = dims_nt(lower(jnp.where(mine, grad_out, 0.0)), value)
            weighted = probs * grad_probs
            row = jnp.sum(weighted, axis=1, keepdims=True)
            grad_scores = lower(weighted - probs * row)
            grad_value = dims_tn(lower(probs), grad_low)
            grad_query = product(grad_scores, k_side)
            grad_key = dims_tn(grad_scores, q_side)
            taken = jnp.sum(
                jnp.where(pair.lane == start, grad_query, 0.0) - jnp.where(pair.lane == start + 3, grad_key, 0.0),
                axis=1, keepdims=True,
            )
            dcum[...] = jnp.where(pair.lane == head, taken, dcum[...])
            results.append((grad_query * 0.125, grad_key, grad_value))
        for part in range(3):
            merged = jnp.where(pair.lane < 64, results[0][part], results[1][part])
            dqkv[:, pl.ds(base + part * width, 128)] = lower(merged)
        return carry

    lax.fori_loop(0, heads // 2, attend, 0)
    rising = sum(dims_tn(allowed, part) for part in three_parts(dcum[...]))
    grad_logit = rising / (1.0 + jnp.exp(logit))
    lane = lax.broadcasted_iota(jnp.int32, grad_logit.shape, 1)
    grad_logit = lower(jnp.where(lane < heads, grad_logit, 0.0))
    dforget_ref[0:128, :] = dims_tn(grad_logit, act_a)
    bias = jnp.sum(grad_logit.astype(jnp.float32), axis=0, keepdims=True)
    dforget_ref[128:136, :] = jnp.concatenate(
        [jnp.broadcast_to(bias, (8, 128)), jnp.zeros((8, width - 128), jnp.float32)], axis=1
    )

    def weigh(n, carry):
        at = pl.ds(pl.multiple_of(n * 256, 256), 256)
        g_in[:, at] = lower(product(act_t[...], dqkv[:, at]))
        return carry

    lax.fori_loop(0, 3 * width // 256, weigh, 0)
    stores[3].start()
    loads[0].wait()
    grad_b[...] = dims_nt(grad_logit, forget_ref[...])

    def gather_back(n, carry):
        at = pl.ds(pl.multiple_of(n * 256, 256), 256)
        grad_b[...] += dims_nt(dqkv[:, at], b_in[:, at])
        return carry

    lax.fori_loop(0, 3 * width // 256, gather_back, 0)
    back_a, dgain_a = norm_backward(grad_b[...], normed_a, inverse_a, gain_ref[0:1, :])
    dx_ref[...] = grad_mid + back_a
    dgain_ref[...] = jnp.concatenate([dgain_a, dgain_b, jnp.zeros((6, width), jnp.float32)], axis=0)
    for copy in stores:
        copy.wait()


def layer_backward(layer, round_input, round_grad, grad, values, allowed, saved, mats, forget_w, gains):
    tree_len, width = values.shape
    qkv, logit, lse, att, middle, gate_up = saved
    w_in, w_out, w_up, w_down = mats
    half = w_down.shape[1]
    f32, b16 = jnp.float32, jnp.bfloat16
    shape = jax.ShapeDtypeStruct
    return pl.pallas_call(
        partial(backward_kernel, layer, round_input, round_grad),
        out_shape=[
            shape((tree_len, width), f32),
            shape((136, width), f32),
            shape((8, width), f32),
        ]
        + [shape(w.shape[1:], b16) for w in mats],
        in_specs=[VMEM] * 10 + [ANY] * 5,
        out_specs=[VMEM] * 3 + [ANY] * 4,
        scratch_shapes=[pltpu.VMEM(w.shape[1:], b16) for w in mats]
        + [
            pltpu.VMEM((tree_len, 2 * half), f32),
            pltpu.VMEM((tree_len, 3 * width), b16),
            pltpu.VMEM((width, tree_len), b16),
            pltpu.VMEM((tree_len, width), f32),
            pltpu.VMEM((tree_len, tree_len), f32),
            pltpu.VMEM((tree_len, 128), f32),
        ]
        + [pltpu.VMEM(w.shape[1:], b16) for w in mats]
        + [DMA((4,)), DMA((half // 256, 2)), DMA((4,))],
        compiler_params=pltpu.CompilerParams(vmem_limit_bytes=60 * 2**20),
        name=f"backward_{layer}",
    )(grad, values, allowed, qkv, logit, lse, att, middle, forget_w, gains, gate_up, *mats)
def head_forward_kernel(rows_each, z_ref, table_ref, marks_ref, logits_ref, stats_ref):
    rows = z_ref.shape[0]
    chunk = 256 if table_ref.shape[0] % 256 == 0 else 128
    z = z_ref[...]

    def body(n, carry):
        peak, count, linear = carry
        at = pl.ds(pl.multiple_of(n * chunk, chunk), chunk)
        logits = dims_nt(z, table_ref[at, :])
        column = lax.broadcasted_iota(jnp.int32, (rows, chunk), 1) + n * chunk
        linear = linear + jnp.sum(logits * marks_ref[:, at], axis=1, keepdims=True)
        logits = jnp.where(column < rows_each, logits, masked_score)
        logits_ref[:, at] = logits
        new_peak = jnp.maximum(peak, jnp.max(logits, axis=1, keepdims=True))
        count = count * jnp.exp(peak - new_peak) + jnp.sum(jnp.exp(logits - new_peak), axis=1, keepdims=True)
        return new_peak, count, linear

    start = jnp.full((rows, 1), masked_score, jnp.float32)
    zero = jnp.zeros((rows, 1), jnp.float32)
    peak, count, linear = lax.fori_loop(0, table_ref.shape[0] // chunk, body, (start, zero, zero))
    lane = lax.broadcasted_iota(jnp.int32, (rows, 128), 1)
    stats = jnp.where(lane == 0, peak, jnp.where(lane == 1, count, jnp.where(lane == 2, linear, 0.0)))
    stats_ref[...] = stats.T[0:4, :]


def head_forward(rows_each, z, table, marks):
    rows, width = z.shape[0], table.shape[0]
    return pl.pallas_call(
        partial(head_forward_kernel, rows_each),
        out_shape=[jax.ShapeDtypeStruct((rows, width), jnp.float32), jax.ShapeDtypeStruct((4, rows), jnp.float32)],
        in_specs=[VMEM] * 3,
        out_specs=[VMEM] * 2,
        name="head_forward",
    )(z, table, marks)


def head_backward_kernel(sections, span, pos_all, z_ref, table_ref, marks_ref, logits_ref, stats_ref,
                         prob_ref, dz_ref, dtable_ref, row_ref, grads):
    rows, width = logits_ref.shape
    peak = jnp.max(stats_ref[:, 0, :], axis=0, keepdims=True)
    count = jnp.sum(stats_ref[:, 1, :] * jnp.exp(stats_ref[:, 0, :] - peak), axis=0, keepdims=True)
    log_norm = peak + jnp.log(count)
    prob = prob_ref[...]
    prob_sum = jnp.sum(prob, axis=1, keepdims=True)
    entropy = jnp.sum(prob * jnp.log(prob), axis=1, keepdims=True)
    log_norm = jnp.broadcast_to(log_norm, (128, rows)).T[:, 0:1]
    whole = jnp.sum(log_norm * (1.0 + prob_sum) + entropy) - jnp.sum(stats_ref[:, 2, :])
    row_ref[...] = jnp.full((8, 128), whole)
    chunk = 256 if width % 256 == 0 else 128
    weight = 1.0 + prob_sum

    def body(n, carry):
        at = pl.ds(pl.multiple_of(n * chunk, chunk), chunk)
        grad = (weight * jnp.exp(logits_ref[:, at] - log_norm) - marks_ref[:, at]) * (1.0 / pos_all)
        grads[:, at] = lower(grad)
        dtable_ref[at, :] = dims_tn(lower(grad), z_ref[...])
        return carry

    lax.fori_loop(0, width // chunk, body, 0)
    section = lax.axis_index("section")
    for r in range(rows // (sections * span)):
        at = pl.ds(pl.multiple_of((r * sections + section) * span, span), span)
        dz_ref[r * span : (r + 1) * span, :] = lower(product(grads[at, :], table_ref[...]))


def head_backward(z, table, marks, logits, stats_all, prob, span, pos_all):
    rows, width = logits.shape
    sections = lax.axis_size("section")
    return pl.pallas_call(
        partial(head_backward_kernel, sections, span, pos_all),
        out_shape=[
            jax.ShapeDtypeStruct((rows // sections, z.shape[1]), jnp.bfloat16),
            jax.ShapeDtypeStruct((width, z.shape[1]), jnp.float32),
            jax.ShapeDtypeStruct((8, 128), jnp.float32),
        ],
        in_specs=[VMEM] * 6,
        out_specs=[VMEM] * 3,
        scratch_shapes=[pltpu.VMEM((rows, width), jnp.bfloat16)],
        name="head_backward",
    )(z, table, marks, logits, stats_all, prob)
def pieces_of(rows):
    part = 400 if rows % 400 == 0 else rows
    return [(at, part) for at in range(0, rows, part)]


def each_tile(rows, columns, fn, carry):
    step = 16
    wide = 256 if columns % 256 == 0 else columns

    def body(n, carry):
        at = pl.ds(pl.multiple_of(n * step, step), step)
        for c in range(0, columns, wide):
            carry = fn(at, slice(c, c + wide), carry)
        return carry

    carry = lax.fori_loop(0, rows // step, body, carry)
    if rows % step:
        at = slice(rows // step * step, rows)
        tail = [jnp.zeros((rows % step, wide), jnp.float32)] * 2
        for c in range(0, columns, wide):
            tail = fn(at, slice(c, c + wide), tail)
        carry = [carry[0], carry[1]] + [jnp.sum(t) for t in tail]
    return carry


def step_kernel(shapes, scalar_ref, sums_ref, forget_sum_ref, gains_sum_ref, *refs):
    n = len(shapes)
    small_in, refs = refs[:6], refs[6:]
    grads, refs = refs[:n], refs[n:]
    weights, refs = refs[:n], refs[n:]
    firsts, refs = refs[:n], refs[n:]
    seconds, refs = refs[:n], refs[n:]
    out_first, refs = refs[:n], refs[n:]
    out_second, refs = refs[:n], refs[n:]
    out_dir, refs = refs[:n], refs[n:]
    small_out, refs = refs[:6], refs[6:]
    norm_ref, small_norm_ref, refs = refs[0], refs[1], refs[2:]
    g_buf, refs = refs[:n], refs[n:]
    w_buf, refs = refs[:n], refs[n:]
    m_buf, refs = refs[:n], refs[n:]
    v_buf, refs = refs[:n], refs[n:]
    d_buf, refs = refs[:n], refs[n:]
    load_sem, store_sem = refs
    work = []
    for a in range(n):
        for at, part in pieces_of(shapes[a][0]):
            rows = pl.ds(at, part)
            p = len(work)
            loads = [
                pltpu.make_async_copy(src.at[rows], dst.at[rows], load_sem.at[p, q])
                for q, (src, dst) in enumerate(
                    ((grads[a], g_buf[a]), (weights[a], w_buf[a]), (firsts[a], m_buf[a]), (seconds[a], v_buf[a]))
                )
            ]
            stores = [
                pltpu.make_async_copy(src.at[rows], dst.at[rows], store_sem.at[p, q])
                for q, (src, dst) in enumerate(
                    ((m_buf[a], out_first[a]), (v_buf[a], out_second[a]), (d_buf[a], out_dir[a]))
                )
            ]
            work.append((a, at, part, loads, stores))
    for _, _, _, loads, _ in work:
        for copy in loads:
            copy.start()
    lane = lax.broadcasted_iota(jnp.int32, (8, 128), 1)
    row = lax.broadcasted_iota(jnp.int32, (8, 128), 0)

    def scalar_at(values, r, c):
        return jnp.sum(jnp.where((row == r) & (lane == c), values, 0.0))

    forget_sum, gains_sum = forget_sum_ref[...], gains_sum_ref[...]
    norm = jnp.sqrt(
        jnp.full((1, 1), scalar_at(sums_ref[...], 0, 0) + square_sum(forget_sum) + square_sum(gains_sum))
    )
    clip = jnp.minimum(1.0, scalar_ref[2] / norm)
    inverse_first = scalar_ref[0]
    inverse_second = scalar_ref[1]

    def adam(weight, grad, first, second):
        scaled = clip * grad
        first_new = beta_first * first + (1.0 - beta_first) * scaled
        second_new = beta_second * second + (1.0 - beta_second) * scaled * scaled
        direction = (first_new * inverse_first) / (
            jnp.sqrt(second_new * inverse_second) + adam_eps
        ) + decay_rate * weight
        return first_new, second_new, direction

    small_norms = []
    for s, (grad, group) in enumerate(((forget_sum, scalar_heads(forget_sum)), (gains_sum, 1))):
        w_ref, m_ref, v_ref = small_in[3 * s : 3 * s + 3]
        weight = w_ref[...]
        first_new, second_new, direction = adam(weight, grad, m_ref[...], v_ref[...])
        w_norm = jnp.sum(weight * weight, axis=1, keepdims=True)
        d_norm = jnp.sum(direction * direction, axis=1, keepdims=True)
        rows = weight.shape[0]
        owner = lax.broadcasted_iota(jnp.int32, (rows, 1), 0) // group
        ratio = jnp.zeros((rows, 1), jnp.float32)
        for t in range(-(-rows // group)):
            ours = owner == t
            w_total = jnp.sqrt(jnp.full((1, 1), jnp.sum(jnp.where(ours, w_norm, 0.0))))
            d_total = jnp.sqrt(jnp.full((1, 1), jnp.sum(jnp.where(ours, d_norm, 0.0))))
            ratio = jnp.where(ours, w_total / d_total, ratio)
            small_norms += [w_total, d_total]
        small_out[3 * s][...] = weight - learn_rate * ratio * direction
        small_out[3 * s + 1][...] = first_new
        small_out[3 * s + 2][...] = second_new
    table = jnp.where((row == 0) & (lane == 0), norm, 0.0)
    for t, value in enumerate(small_norms):
        table = jnp.where((row == 1) & (lane == t), value, table)
    small_norm_ref[...] = table

    sums = [[jnp.float32(0), jnp.float32(0)] for _ in range(n)]
    for a, at, part, loads, stores in work:
        for copy in loads:
            copy.wait()
        g, w, m, v, d = (buf[a].at[pl.ds(at, part)] for buf in (g_buf, w_buf, m_buf, v_buf, d_buf))
        columns = shapes[a][1]
        wide = 256 if columns % 256 == 0 else columns

        def tile(rows, cols, carry):
            weight = w[rows, cols]
            first_new, second_new, direction = adam(
                weight, g[rows, cols].astype(jnp.float32), m[rows, cols], v[rows, cols]
            )
            m[rows, cols] = first_new
            v[rows, cols] = second_new
            d[rows, cols] = direction
            return [carry[0] + weight * weight, carry[1] + direction * direction]

        zero = jnp.zeros((16, wide), jnp.float32)
        done = each_tile(part, columns, tile, [zero, zero])
        for copy in stores:
            copy.start()
        for q in range(2):
            sums[a][q] = sums[a][q] + jnp.sum(done[q])
            if len(done) > 2:
                sums[a][q] = sums[a][q] + done[2 + q]
    section = lax.axis_index("section")
    table = jnp.zeros((8, 128), jnp.float32)
    for a in range(n):
        here = (section if a == 0 else lax.axis_index("replica")) == 0
        place = 0 if a == 0 else 2 * section
        for q in range(2):
            value = jnp.where(here, sums[a][q], 0.0)
            table = jnp.where((row == a) & (lane == place + q), value, table)
    norm_ref[...] = table
    for _, _, _, _, stores in work:
        for copy in stores:
            copy.wait()


def scalar_heads(forget_sum):
    return forget_sum.shape[0] // 2


def optimizer_step(scalars, sums, forget_sum, gains_sum, small, grads, weights, firsts, seconds):
    n = len(grads)
    shapes = [w.shape for w in weights]
    flat = [jax.ShapeDtypeStruct(s, jnp.float32) for s in shapes]
    buffers = lambda kinds: [pltpu.VMEM(s, k) for s, k in zip(shapes, kinds)]
    parts = sum(len(pieces_of(s[0])) for s in shapes)
    out = pl.pallas_call(
        partial(step_kernel, shapes),
        out_shape=flat * 3
        + [jax.ShapeDtypeStruct(s.shape, jnp.float32) for s in small]
        + [jax.ShapeDtypeStruct((8, 128), jnp.float32)] * 2,
        in_specs=[pl.BlockSpec(memory_space=pltpu.SMEM)] + [VMEM] * 9 + [ANY] * (4 * n),
        out_specs=[ANY] * (3 * n) + [VMEM] * 8,
        scratch_shapes=buffers([g.dtype for g in grads])
        + buffers([jnp.float32] * n) * 4
        + [DMA((parts, 4)), DMA((parts, 3))],
        compiler_params=pltpu.CompilerParams(vmem_limit_bytes=60 * 2**20),
        name="optimizer_step",
    )(scalars, sums, forget_sum, gains_sum, *small, *grads, *weights, *firsts, *seconds)
    return out[:n], out[n : 2 * n], out[2 * n : 3 * n], out[3 * n : 3 * n + 6], out[-2], out[-1]


def apply_kernel(shapes, ratio_ref, *refs):
    n = len(shapes)
    weights, directions, outs = refs[:n], refs[n : 2 * n], refs[2 * n : 3 * n]
    w_buf, d_buf = refs[3 * n : 4 * n], refs[4 * n : 5 * n]
    load_sem, store_sem = refs[5 * n :]
    work = []
    for a in range(n):
        for at, part in pieces_of(shapes[a][0]):
            rows = pl.ds(at, part)
            p = len(work)
            loads = [
                pltpu.make_async_copy(weights[a].at[rows], w_buf[a].at[rows], load_sem.at[p, 0]),
                pltpu.make_async_copy(directions[a].at[rows], d_buf[a].at[rows], load_sem.at[p, 1]),
            ]
            store = pltpu.make_async_copy(w_buf[a].at[rows], outs[a].at[rows], store_sem.at[p])
            work.append((a, at, part, loads, store))
    for _, _, _, loads, _ in work:
        for copy in loads:
            copy.start()
    for a, at, part, loads, store in work:
        for copy in loads:
            copy.wait()
        w, d = w_buf[a].at[pl.ds(at, part)], d_buf[a].at[pl.ds(at, part)]
        rate = ratio_ref[a]

        def tile(rows, cols, carry):
            w[rows, cols] = w[rows, cols] - rate * d[rows, cols]
            return carry

        each_tile(part, shapes[a][1], tile, [jnp.float32(0), jnp.float32(0)])
        store.start()
    for _, _, _, _, store in work:
        store.wait()


def apply_step(rates, weights, directions):
    n = len(weights)
    shapes = [w.shape for w in weights]
    parts = sum(len(pieces_of(s[0])) for s in shapes)
    return pl.pallas_call(
        partial(apply_kernel, shapes),
        out_shape=[jax.ShapeDtypeStruct(s, jnp.float32) for s in shapes],
        in_specs=[pl.BlockSpec(memory_space=pltpu.SMEM)] + [ANY] * (2 * n),
        out_specs=[ANY] * n,
        scratch_shapes=[pltpu.VMEM(s, jnp.float32) for s in shapes] * 2 + [DMA((parts, 2)), DMA((parts,))],
        compiler_params=pltpu.CompilerParams(vmem_limit_bytes=40 * 2**20),
        name="apply_step",
    )(rates, *weights, *directions)


def lower(values):
    return values.astype(jnp.bfloat16)


def product(left, right):
    return jnp.dot(left, right, preferred_element_type=jnp.float32)


def product_left(left, right):
    return lax.dot_general(left, right, (((0,), (0,)), ((), ())), preferred_element_type=jnp.float32)


def product_right(left, right):
    return lax.dot_general(left, right, (((1,), (1,)), ((), ())), preferred_element_type=jnp.float32)


def rms_forward(values, gain):
    inverse = lax.rsqrt(jnp.mean(values * values, axis=-1, keepdims=True) + eps_norm)
    normed = values * inverse
    return (normed * gain, normed, inverse)


def rms_backward(grad_out, normed, inverse, gain):
    grad_normed = grad_out * gain
    grad_in = inverse * (
        grad_normed - normed * jnp.mean(grad_normed * normed, axis=-1, keepdims=True)
    )
    return (grad_in, jnp.sum(grad_out * normed, axis=0))


def path_mask(parent_row, tree_len):
    seg_count = parent_row.shape[0]
    seglen = tree_len // seg_count
    seg_order = jnp.arange(seg_count, dtype=jnp.int32)
    parent_hot = ((parent_row[:, None] == seg_order[None, :]) & (seg_order[:, None] >= 1)).astype(
        jnp.float32
    )
    identity = jnp.eye(seg_count, dtype=jnp.float32)
    power, steps = parent_hot, 1
    reached = identity + parent_hot
    while steps < seg_count:
        reached = jnp.minimum(1.0, jnp.dot(reached, reached))
        steps *= 2
    strict = reached - identity
    seg_of = jnp.arange(tree_len, dtype=jnp.int32) // seglen
    seg_hot = (seg_of[:, None] == seg_order[None, :]).astype(jnp.float32)
    ancestor = jnp.dot(jnp.dot(seg_hot, strict), seg_hot.T)
    places = jnp.arange(tree_len, dtype=jnp.int32)
    inside = (seg_of[:, None] == seg_of[None, :]) & (places[None, :] <= places[:, None])
    return ancestor + inside.astype(jnp.float32)


def square_sum(values):
    return jnp.sum(values * values)


def local(
    tokens,
    parents,
    loss_positions,
    targets,
    teacher_index,
    teacher_probability,
    step_count,
    embed_table,
    table_first,
    table_second,
    attention_in,
    attention_in_first,
    attention_in_second,
    attention_out,
    attention_out_first,
    attention_out_second,
    feedforward_in,
    feedforward_in_first,
    feedforward_in_second,
    feedforward_out,
    feedforward_out_first,
    feedforward_out_second,
    forget_gate,
    forget_first,
    forget_second,
    norm_gains,
    gains_first,
    gains_second,
):
    section_id = lax.axis_index("section")
    replica_id = lax.axis_index("replica")
    shard_id = lax.axis_index("shard")
    sections = lax.axis_size("section")
    replicas = lax.axis_size("replica")
    shards = lax.axis_size("shard")
    group_trees, tree_len = tokens.shape
    rows_each, width = embed_table.shape
    pos_count = loss_positions.shape[1]
    pos_all = group_trees * replicas * pos_count
    owners = replicas * shards
    owner_id = replica_id * shards + shard_id
    own_tree = section_id * shards + shard_id
    table_low = lower(embed_table)

    def own_row(values):
        return lax.dynamic_index_in_dim(values, own_tree, 0, keepdims=False)

    tree_tokens = own_row(tokens)
    token_owner = tree_tokens // rows_each
    token_row = tree_tokens % rows_each
    spots = jnp.arange(tree_len, dtype=jnp.int32)

    def asked(batch):
        earlier = spots[None, :] < spots[:, None]
        same = tree_tokens[:, None] == tree_tokens[None, :]
        is_first = jnp.logical_not(jnp.any(same & earlier, axis=1))
        counted = earlier & (token_owner[:, None] == token_owner[None, :]) & is_first[None, :]
        number_first = jnp.sum(counted.astype(jnp.int32), axis=1)
        number = jnp.sum(jnp.where(same & is_first[None, :], number_first[None, :], 0), axis=1)
        slot = number - batch * batch_rows
        inside = (slot >= 0) & (slot < batch_rows)
        place = jnp.where(inside, token_owner * batch_rows + slot, -1)
        spot_of = jnp.arange(owners * batch_rows, dtype=jnp.int32)
        hot = place[None, :] == spot_of[:, None]
        rows = jnp.max(jnp.where(hot & is_first[None, :], token_row[None, :] + 1, 0), axis=1)
        return rows.reshape(owners, batch_rows), lower(hot)

    def all_devices(part, ident):
        if replicas != 2:
            out = part
            for axis in ("shard", "replica", "section"):
                out = lax.all_gather(out, axis)
            return out
        return jnp.swapaxes(gather([part], ident, space=VMEM)[0][0], 1, 2)

    def wanted(batch):
        rows, hot = asked(batch)
        every = all_devices(jnp.pad(rows, ((0, 0), (0, 128 - batch_rows))), 0)
        mine = lax.dynamic_index_in_dim(every, owner_id, 3, keepdims=False)[..., :batch_rows]
        wish = mine.reshape(sections * owners * batch_rows) - 1
        row_of = jnp.arange(rows_each, dtype=jnp.int32)
        return hot, lower(wish[:, None] == row_of[None, :])

    def more_rows(state):
        batch, total_rows = state
        hot_more, pick = wanted(batch)
        own_pick = lax.dynamic_index_in_dim(
            pick.reshape(sections, owners * batch_rows, rows_each), section_id, 0, keepdims=False
        )
        sent = lower(product(own_pick, table_low)).reshape(owners, batch_rows, width)
        got_more = exchange(sent, 1)[0].reshape(owners * batch_rows, width)
        return (batch + 1, total_rows + product_left(hot_more, got_more))

    def more_grads(state):
        batch, total_rows = state
        hot_more, pick = wanted(batch)
        sent = lower(product(hot_more, embed_low)).reshape(owners, batch_rows, width)
        got_more = exchange(sent, 6, relay=True).reshape(sections * owners * batch_rows, width)
        return (batch + 1, total_rows + product_left(pick, got_more))

    def halves(weight):
        return lower(weight).reshape(2, weight.shape[1] // 2, weight.shape[2])

    width_all = -(-rows_each // 128) * 128
    table_wide = jnp.pad(table_low, ((0, width_all - rows_each), (0, 0)))
    layer_weights = (attention_in, attention_out, feedforward_in, feedforward_out)
    group_data = [targets, teacher_index.reshape(group_trees, -1), teacher_probability.reshape(group_trees, -1)]
    pair_parts = group_data if replicas == 2 else []
    hot, asks = ask_rows(tree_tokens, token_owner, token_row, owners)
    gathered, group_all, (asked_all, got) = gather(
        [halves(w) for w in layer_weights], 2, pair_parts, split=True, errand=(asks, table_wide)
    )
    if replicas != 2:
        group_all = [lax.all_gather(part, "replica") for part in group_data]
    batches = (jnp.max(asked_all[:, :, 0, 127]) + batch_rows - 1) // batch_rows
    embeds = product_left(hot, got.reshape(owners * batch_rows, width))
    _, embeds = lax.while_loop(lambda s: s[0] < batches, more_rows, (jnp.int32(1), embeds))
    mats = [g.reshape(sections, -1, g.shape[-1]) for g in gathered]
    heads = forget_gate.shape[2]
    forget_low = jnp.pad(lower(forget_gate[:, :width]), ((0, 0), (0, 0), (0, 128 - heads)))
    forget_bias = jnp.pad(forget_gate[:, width:], ((0, 0), (0, 0), (0, 128 - heads)))
    gains_of = [jnp.pad(norm_gains[2 * n : 2 * n + 2], ((0, 6), (0, 0))) for n in range(2)]

    allowed = lower(path_mask(own_row(parents), tree_len))
    out_0, *saved_0 = layer_forward(0, False, embeds, allowed, mats, forget_low[0], forget_bias[0], gains_of[0])
    out_1, *saved_1 = layer_forward(1, True, out_0, allowed, mats, forget_low[1], forget_bias[1], gains_of[1])

    positions = own_row(loss_positions)
    position_hot = (positions[:, None] == spots[None, :]).astype(jnp.float32)
    picked = jnp.take(out_1, positions, axis=0)
    final_gain = norm_gains[4]
    head_out, head_normed, head_inverse = rms_forward(picked, final_gain)
    head_rows = jnp.swapaxes(all_devices(lower(head_out), 3), 0, 1).reshape(pos_all, width)

    target_all, index_all, prob_all = [
        part.reshape((pos_all,) + (-1,) * (n > 0)) for n, part in enumerate(group_all)
    ]

    def owned(ids):
        column = ids - owner_id * rows_each
        return jnp.where((column >= 0) & (column < rows_each), column, -1)

    marks = spread_entries(owned(index_all), prob_all, owned(target_all), width_all)
    logits, stats = head_forward(rows_each, head_rows, table_wide, marks)
    if replicas == 2:
        stats_all = exchange(stats[None], 4)[0]
    else:
        stats_all = lax.all_gather(lax.all_gather(stats, "replica"), "shard")
    grad_heads, head_table, loss_sum = head_backward(
        head_rows, table_wide, marks, logits, stats_all.reshape(owners, 4, pos_all), prob_all, shards * pos_count, pos_all
    )
    grad_heads = exchange(grad_heads.reshape(owners, pos_count, width), 5)[0]
    grad_heads = jnp.sum(grad_heads.astype(jnp.float32), axis=0)
    grad_picked, grad_final = rms_backward(grad_heads, head_normed, head_inverse, final_gain)
    grad_top = lax.dot_general(
        position_hot, grad_picked, (((0,), (0,)), ((), ())), precision=highest
    )

    grad_mid, forget_1, gains_1, *grads_1 = layer_backward(
        1, True, False, grad_top, out_0, allowed, saved_1, mats, forget_low[1], gains_of[1]
    )
    grad_low, forget_0, gains_0, *grads_0 = layer_backward(
        0, False, True, grad_mid, embeds, allowed, saved_0, mats, forget_low[0], gains_of[0]
    )
    embed_low = lower(grad_low)

    stacked = [
        [g.reshape(shards, 2, -1, g.shape[-1]) for g in pair] for pair in zip(grads_0, grads_1)
    ]
    def forget_form(values):
        return jnp.pad(jnp.swapaxes(values, 1, 2).reshape(-1, values.shape[1]), ((0, 0), (0, -values.shape[1] % 128)))

    def forget_terms(values):
        bias = jnp.swapaxes(values[128:129, :heads], 0, 1)
        return jnp.concatenate([values[:heads], jnp.pad(bias, ((0, 0), (0, -(width + 1) % 128)))], axis=1)

    def forget_back(values):
        return jnp.swapaxes(values[:, : width + 1].reshape(forget_gate.shape[0], -1, width + 1), 1, 2)

    def gains_form(values):
        return jnp.pad(values, ((0, 8 - values.shape[0]), (0, 0)))

    sent = lower(product(hot, embed_low)).reshape(owners, batch_rows, width)
    small_sums = [
        jnp.concatenate([forget_terms(forget_0), forget_terms(forget_1)], axis=0),
        gains_form(jnp.concatenate([gains_0[:2], gains_1[:2], grad_final[None]], axis=0)),
    ]
    layer_grads, (forget_total, gains_total, got_grads) = reduce_parts(stacked, 8, (small_sums, sent))
    if replicas != 2:
        layer_grads = [lax.psum(g * jnp.bfloat16(0.5), "replica") for g in layer_grads]
    _, head_table = lax.while_loop(lambda s: s[0] < batches, more_grads, (jnp.int32(1), head_table[:rows_each]))
    table_grad, square = table_gradient(
        rows_each, asked_all, got_grads.reshape(-1, width), head_table, layer_grads
    )
    layer_grads = [g.reshape(w.shape[1:]) for g, w in zip(layer_grads, layer_weights)]
    (scalars,) = total([square], 15)
    loss_total = loss_sum[0, 0] / pos_all
    count_float = step_count.astype(jnp.float32)
    rates = jnp.stack(
        [
            1.0 / (1.0 - jnp.power(beta_first, count_float)),
            1.0 / (1.0 - jnp.power(beta_second, count_float)),
            clip_factor / jnp.sqrt(jnp.float32(pos_all)),
        ]
    )
    small = [forget_form(v) for v in (forget_gate, forget_first, forget_second)] + [
        gains_form(v) for v in (norm_gains, gains_first, gains_second)
    ]
    weights = [embed_table] + [w[0] for w in layer_weights]
    firsts = [table_first] + [
        m[0] for m in (attention_in_first, attention_out_first, feedforward_in_first, feedforward_out_first)
    ]
    seconds = [table_second] + [
        m[0] for m in (attention_in_second, attention_out_second, feedforward_in_second, feedforward_out_second)
    ]
    firsts_new, seconds_new, directions, small_new, norms, small_norms = optimizer_step(
        rates, scalars, forget_total, gains_total, small, [table_grad, *layer_grads], weights, firsts, seconds
    )
    norms = jnp.sqrt(total([norms], 16)[0])
    table_norms = norms[0, :2]
    layer_norms = norms[1:5, : 2 * sections].reshape(4, sections, 2)
    mine = lax.dynamic_index_in_dim(layer_norms, section_id, 1, keepdims=False)
    both_norms = jnp.concatenate([table_norms[None], mine], axis=0)
    weights_new = apply_step(learn_rate * both_norms[:, 0] / both_norms[:, 1], weights, directions)
    new_table, table_first_new, table_second_new = weights_new[0], firsts_new[0], seconds_new[0]
    new_layers = [(weights_new[n][None], firsts_new[n][None], seconds_new[n][None]) for n in range(1, 5)]
    new_forget, forget_first_new, forget_second_new = [forget_back(v) for v in small_new[:3]]
    gain_count = norm_gains.shape[0]
    new_gains, gains_first_new, gains_second_new = [v[:gain_count] for v in small_new[3:]]
    layer_count = forget_gate.shape[0]
    grad_norm = small_norms[0, 0]
    tensor_norms = jnp.concatenate(
        [
            table_norms[None],
            layer_norms.reshape(4 * sections, 2),
            small_norms[1, : 2 * (layer_count + gain_count)].reshape(-1, 2),
        ],
        axis=0,
    )
    return (
        new_table,
        table_first_new,
        table_second_new,
        *new_layers[0],
        *new_layers[1],
        *new_layers[2],
        *new_layers[3],
        new_forget,
        forget_first_new,
        forget_second_new,
        new_gains,
        gains_first_new,
        gains_second_new,
        tensor_norms,
        grad_norm,
        loss_total,
    )


def solution(mesh):
    group = P("replica", None)
    table = P(("replica", "shard"), None)
    layer = P("section", "shard", None)
    in_specs = (
        (group,) * 4
        + (P("replica", None, None),) * 2
        + (P(),)
        + (table,) * 3
        + (layer,) * 12
        + (P(),) * 6
    )
    out_specs = (table,) * 3 + (layer,) * 12 + (P(),) * 9
    return jax.shard_map(local, mesh=mesh, in_specs=in_specs, out_specs=out_specs, check_vma=False)
```

time: 838 us -> 677 us (0.81)
  Pallas kernels: 448 us -> 589 us
  other arithmetic: 142 us -> 20.1 us
  matrix products: 121 us -> 5.3 us
  local copies, waits for them, and re-layouts: 91 us -> 48.7 us
  between operations: 21.5 us -> 4.68 us
    pallas_call x7 -> x15, Pallas kernels: 355 us -> 548 us  [the longest x1 160 us: reduce_shards(): pl.pallas_call(partial(reduce_kernel, count, nx, sums), out_shape=[jax.Sh...]
    reduce_sum x30 -> x0, other arithmetic: 71.1 us -> none  [the longest x16 52 us: square_sum(): return jnp.sum(values * values)]
    dot_general x27 -> x0, matrix products: 57.3 us -> none  [the longest x11 30.3 us: product_right(): lax.dot_general(left, right, (((1,), (1,)), ((), ())), preferred_element_...]
    pallas_call x3 -> x2, Pallas kernels: 74 us -> 24.5 us  [exchange(): pl.pallas_call(partial(exchange_kernel, relay), out_shape=jax.ShapeDtypeS...]
    dot_general x13 -> x1, matrix products: 38.6 us -> 0.45 us  [product_left(): lax.dot_general(left, right, (((0,), (0,)), ((), ())), preferred_element_...]
    another operation x12 -> x1, other arithmetic: 21.5 us -> 0.59 us  [local(): jnp.stack([1.0 / (1.0 - jnp.power(beta_first, count_float)), 1.0 / (1.0 -...]
    dot_general x13 -> x1, matrix products: 21.7 us -> 1.45 us  [product(): return jnp.dot(left, right, preferred_element_type=jnp.float32)]
    unnamed x333 -> x64, local copies, waits for them, and re-layouts: 29.5 us -> 10.6 us
where the time goes in v2:
time: 677 us; the launch traced here: 669 us
  Pallas kernels  589 us (87%)
  local copies, waits for them, and re-layouts  48.7 us (7%)
  other arithmetic  20.1 us (3%)
    pallas_call x1, Pallas kernels, reduce_shards(): pl.pallas_call(partial(reduce_kernel, count, nx, sums), out_shape=[jax.Sh...  160 us
    pallas_call x2, Pallas kernels, gather(): pl.pallas_call(partial(gather_kernel, count, pairs, split, orders, bool(e...  154 us
    pallas_call x2, Pallas kernels, layer_backward(): pl.pallas_call(partial(backward_kernel, layer, round_input, round_grad),...  83.1 us
    pallas_call x2, Pallas kernels, layer_forward(): pl.pallas_call(partial(forward_kernel, layer, round_input), out_shape=[sh...  47.8 us
    pallas_call x2, Pallas kernels, total(): pl.pallas_call(partial(total_kernel, count), out_shape=[jax.ShapeDtypeStr...  35.2 us
    pallas_call x1, Pallas kernels, optimizer_step(): pl.pallas_call(partial(step_kernel, shapes), out_shape=flat * 3 + [jax.Sh...  25.3 us
    pallas_call x2, Pallas kernels, exchange(): pl.pallas_call(partial(exchange_kernel, relay), out_shape=jax.ShapeDtypeS...  24.5 us
    pallas_call x1, Pallas kernels, spread_entries(): pl.pallas_call(spread_kernel, out_shape=jax.ShapeDtypeStruct((rows, width...  16.6 us

profile of v2, /device:TPU:0, one launch (start us, length us, event | category | flops | bytes accessed | tf_op | source)
XLA Modules:
  0.0 668.8 jit_solution(15755953245328140467)
XLA Ops:
  3.0 2.5 ask_rows.1
  5.5 3.0 convert_element_type.114
  8.6 1.8 pad.56.refs_8_.table_ref
  15.8 134.3 %gather_2.1 = (bf16[2,8,2,48,2304]{4,3,2,1,0:T(8,128)(2,1)}, bf16[2,8,2,48,768]{4,3,2,1,0:T(8,128)(2,1)}, bf16[2,8,2,48,4096]{4,3,2,1,0:T(8,128)(2,1)}, bf16[2,8...) custom-call(bf16[2,48,2304]{2,1,0:T(8,128)(2,1)} %bitcast.186, ...), custom_call_target="tpu_custom_call" | custom-call | tf_op jit(solution)/shard_map/gather_2/pallas_call | solution.py:348
  155.5 16.6 %spread_entries.1.marks_ref = f32[512,2048]{1,0:T(8,128)} custom-call(s32[64,1,512]{2,1,0:T(1,128)} %and_select_fusion.columns_ref, f32[64,1,512]{2,1,0:T(1,128)} %reshape_reshape.6.weight_ref, s32[512,1]{1,0:T(8,128)} %and_select_fusion.1.target_ref), custom_call_target="tpu_custom_call" | custom-call | tf_op jit(solution)/shard_map/spread_entries/pallas_call | solution.py:921
  180.6 23.9 %forward_0.1 = (f32[320,768]{1,0:T(8,128)}, bf16[320,2304]{1,0:T(8,128)(2,1)}, f32[320,128]{1,0:T(8,128)}, f32[320,128]{1,0:T(8,128)}, bf16[320,768]{1,0:T(8,128...) custom-call(f32[320,768]{1,0:T(8,128)S(1)} %get-tuple-element.641.x_ref, bf16[320,320]{1,0:T(8,128)(2,1)} %fusion.22.allowed_ref, ...), custom_call_target="tpu_custom_call" | custom-call | tf_op jit(solution)/shard_map/forward_0/pallas_call | solution.py:1170
  205.1 23.9 %forward_1.1 = (f32[320,768]{1,0:T(8,128)}, bf16[320,2304]{1,0:T(8,128)(2,1)}, f32[320,128]{1,0:T(8,128)}, f32[320,128]{1,0:T(8,128)}, bf16[320,768]{1,0:T(8,128...) custom-call(f32[320,768]{1,0:T(8,128)} %get-tuple-element.646.x_ref, bf16[320,320]{1,0:T(8,128)(2,1)} %fusion.22.allowed_ref, ...), custom_call_target="tpu_custom_call" | custom-call | tf_op jit(solution)/shard_map/forward_1/pallas_call | solution.py:1170
  229.8 1.8 gather_fusion
  233.2 19.5 %gather_3.1 = bf16[2,8,2,16,768]{4,3,2,1,0:T(8,128)(2,1)} custom-call(bf16[16,768]{1,0:T(8,128)(2,1)} %multiply_convert_fusion.refs_0_), custom_call_target="tpu_custom_call" | custom-call | tf_op jit(solution)/shard_map/gather_3/pallas_call | solution.py:348
  252.7 2.1 copy.144
  254.7 10.7 %head_forward.1 = (f32[512,2048]{1,0:T(8,128)}, f32[4,512]{1,0:T(4,128)}) custom-call(bf16[512,768]{1,0:T(8,128)(2,1)} %bitcast.173, bf16[2048,768]{1,0:T(8,128)(2,1)} %pad.56.refs_8_.table_ref, f32[512,2048]{1,0:T(8,128)} %spread_entries.1.marks_ref), custom_call_target="tpu_custom_call" | custom-call | tf_op jit(solution)/shard_map/head_forward/pallas_call | solution.py:1411
  265.4 9.6 %exchange_4.1 = f32[1,16,4,512]{3,2,1,0:T(4,128)} custom-call(f32[1,4,512]{2,1,0:T(4,128)} %bitcast.217), custom_call_target="tpu_custom_call" | custom-call | tf_op jit(solution)/shard_map/exchange_4/pallas_call | solution.py:423
  275.9 12.7 %head_backward.1 = (bf16[256,768]{1,0:T(8,128)(2,1)}, f32[2048,768]{1,0:T(8,128)}, f32[8,128]{1,0:T(8,128)}) custom-call(bf16[512,768]{1,0:T(8,128)(2,1)} %bitcast.174, bf16[2048,768]{1,0:T(8,128)(2,1)} %pad.56.refs_8_.table_ref, f32[512,2048]{1,0:T(8,128)} %spread_entries.1.marks_ref, f32[512,2048]{1,0:T(8,128)} %get-tuple-element.651.logits_ref, ...), custom_call_target="tpu_custom_call" | custom-call | tf_op jit(solution)/shard_map/head_backward/pallas_call | solution.py:1452
  288.6 14.9 %exchange_5.1 = bf16[1,16,16,768]{3,2,1,0:T(8,128)(2,1)} custom-call(bf16[16,16,768]{2,1,0:T(8,128)(2,1)} %bitcast.207), custom_call_target="tpu_custom_call" | custom-call | tf_op jit(solution)/shard_map/exchange_5/pallas_call | solution.py:423
  306.3 41.4 %backward_1.1 = (f32[320,768]{1,0:T(8,128)}, f32[136,768]{1,0:T(8,128)}, f32[8,768]{1,0:T(8,128)}, bf16[768,2304]{1,0:T(8,128)(2,1)}, bf16[768,768]{1,0:T(8,128)...) custom-call(f32[320,768]{1,0:T(8,128)} %fusion.39.dy_ref, f32[320,768]{1,0:T(8,128)} %get-tuple-element.646.x_ref, ...), custom_call_target="tpu_custom_call" | custom-call | tf_op jit(solution)/shard_map/backward_1/pallas_call | solution.py:1360
  347.8 41.6 %backward_0.1 = (f32[320,768]{1,0:T(8,128)}, f32[136,768]{1,0:T(8,128)}, f32[8,768]{1,0:T(8,128)}, bf16[768,2304]{1,0:T(8,128)(2,1)}, bf16[768,768]{1,0:T(8,128)...) custom-call(f32[320,768]{1,0:T(8,128)} %get-tuple-element.660.dy_ref, ...), custom_call_target="tpu_custom_call" | custom-call | tf_op jit(solution)/shard_map/backward_0/pallas_call | solution.py:1360
  390.7 5.8 slice.127
  404.0 159.6 %reduce_8.1 = (bf16[2,48,2304]{2,1,0:T(8,128)(2,1)}, bf16[2,48,768]{2,1,0:T(8,128)(2,1)}, bf16[2,48,4096]{2,1,0:T(8,128)(2,1)}, bf16[2,128,768]{2,1,0:T(8,128)(2...) custom-call(bf16[8,2,48,2304]{3,2,1,0:T(8,128)(2,1)} %bitcast.178, ...), custom_call_target="tpu_custom_call" | custom-call | tf_op jit(solution)/shard_map/reduce_8/pallas_call | solution.py:839
  563.7 10.5 %table_gradient.1 = (f32[2000,768]{1,0:T(8,128)}, f32[8,128]{1,0:T(8,128)}) custom-call(s32[2,16,1,128]{3,2,1,0:T(1,128)} %get-tuple-element.638.asked_ref, bf16[1024,768]{1,0:T(8,128)(2,1)} %bitcast.192, f32[2000,768]{1,0:T(8,128)} %get-tuple-element.682.head_ref, bf16[2,48,2304]{2,1,0:T(8,128)(2,1)} %get-tuple-element.683.refs_0_, ...), custom_call_target="tpu_custom_call" | custom-call | tf_op jit(solution)/shard_map/table_gradient/pallas_call | solution.py:1016
  574.2 22.2 %total_15.1.sums_ref = f32[8,128]{1,0:T(8,128)} custom-call(f32[8,128]{1,0:T(8,128)} %get-tuple-element.687.refs_0_), custom_call_target="tpu_custom_call" | custom-call | tf_op jit(solution)/shard_map/total_15/pallas_call | solution.py:486
  601.6 25.3 %optimizer_step.1 = (f32[2000,768]{1,0:T(8,128)}, f32[96,2304]{1,0:T(8,128)}, f32[96,768]{1,0:T(8,128)}, f32[96,4096]{1,0:T(8,128)}, f32[256,768]{1,0:T(8,128)},...) custom-call(f32[3]{0:T(128)} %pad_maximum_fusion.2.scalar_ref, ...), custom_call_target="tpu_custom_call" | custom-call | tf_op jit(solution)/shard_map/optimizer_step/pallas_call | solution.py:1625
  626.9 13.1 %total_16.1 = f32[8,128]{1,0:T(8,128)} custom-call(f32[8,128]{1,0:T(8,128)} %get-tuple-element.691.refs_0_), custom_call_target="tpu_custom_call" | custom-call | tf_op jit(solution)/shard_map/total_16/pallas_call | solution.py:486
  645.1 2.7 copy-done
  652.5 7.1 %apply_step.1 = (f32[2000,768]{1,0:T(8,128)}, f32[96,2304]{1,0:T(8,128)}, f32[96,768]{1,0:T(8,128)}, f32[96,4096]{1,0:T(8,128)}, f32[256,768]{1,0:T(8,128)}) custom-call(f32[5]{0:T(128)S(1)} %fusion.67.ratio_ref, f32[2000,768]{1,0:T(8,128)S(1)} %copy-done, f32[96,2304]{1,0:T(8,128)S(1)} %bitcast.148, f32[96,768]{1,0:T(8,128)S(1)} %bitcast.152, ...), custom_call_target="tpu_custom_call" | custom-call | tf_op jit(solution)/shard_map/apply_step/pallas_call | solution.py:1680
  (158 shorter events, 57.6 us)
Async XLA Ops:
  8.5 3.6 copy-start.13
  8.6 3.5 copy-start.3
  8.6 4.3 copy-start.5
  11.1 2.6 copy-start.7
  11.1 3.3 copy-start.20
  11.1 4.0 copy-start.21
  150.2 22.0 %copy-start.24 = (s32[2,16,1,128]{3,2,1,0:T(1,128)S(1)}, s32[2,16,1,128]{3,2,1,0:T(1,128)}, u32[]{:S(2)}) copy-start(s32[2,16,1,128]{3,2,1,0:T(1,128)} %get-tuple-element.638.asked_ref) | copy-start | bytes 49156
  150.2 23.4 %copy-start.14 = (bf16[512,320]{1,0:T(8,128)(2,1)S(1)}, bf16[512,320]{1,0:T(8,128)(2,1)}, u32[]{:S(2)}) copy-start(bf16[512,320]{1,0:T(8,128)(2,1)} %get-tuple-element.639) | copy-start | bytes 983044
  150.2 23.4 %copy-start.16 = (bf16[16,32,768]{2,1,0:T(8,128)(2,1)S(1)}, bf16[16,32,768]{2,1,0:T(8,128)(2,1)}, u32[]{:S(2)}) copy-start(bf16[16,32,768]{2,1,0:T(8,128)(2,1)} %get-tuple-element.640) | copy-start | bytes 2359300
  174.2 3.1 copy-start.18
  174.3 4.2 copy-start.25
  174.3 4.8 slice-start
  254.7 20.3 %copy-start.17 = (f32[2,16,1024]{2,1,0:T(8,128)S(1)}, f32[2,16,1024]{2,1,0:T(8,128)}, u32[]{:S(2)}) copy-start(f32[2,16,1024]{2,1,0:T(8,128)} %get-tuple-element.649) | copy-start | bytes 393220
  563.6 34.1 %copy-start.19 = (f32[2,769,12]{1,0,2:T(2,128)S(1)}, f32[2,769,12]{1,0,2:T(2,128)}, u32[]{:S(2)}) copy-start(f32[2,769,12]{1,0,2:T(2,128)} %param.54) | copy-start | bytes 221476
  563.6 34.8 %copy-start.22 = (f32[2,769,12]{1,0,2:T(2,128)S(1)}, f32[2,769,12]{1,0,2:T(2,128)}, u32[]{:S(2)}) copy-start(f32[2,769,12]{1,0,2:T(2,128)} %param.55) | copy-start | bytes 221476
  563.6 35.5 %copy-start.23 = (f32[2,769,12]{1,0,2:T(2,128)S(1)}, f32[2,769,12]{1,0,2:T(2,128)}, u32[]{:S(2)}) copy-start(f32[2,769,12]{1,0,2:T(2,128)} %param.56) | copy-start | bytes 221476
  563.6 36.2 %copy-start.26 = (f32[5,768]{1,0:T(8,128)S(1)}, f32[5,768]{1,0:T(8,128)}, u32[]{:S(2)}) copy-start(f32[5,768]{1,0:T(8,128)} %param.57) | copy-start | bytes 46084
  563.6 36.8 %copy-start.27 = (f32[5,768]{1,0:T(8,128)S(1)}, f32[5,768]{1,0:T(8,128)}, u32[]{:S(2)}) copy-start(f32[5,768]{1,0:T(8,128)} %param.58) | copy-start | bytes 46084
  563.7 37.4 %copy-start.28 = (f32[5,768]{1,0:T(8,128)S(1)}, f32[5,768]{1,0:T(8,128)}, u32[]{:S(2)}) copy-start(f32[5,768]{1,0:T(8,128)} %param.59) | copy-start | bytes 46084
  601.6 43.5 %copy-start.2 = (f32[1,96,4096]{2,1,0:T(8,128)S(1)}, f32[1,96,4096]{2,1,0:T(8,128)}, u32[]{:S(2)}) copy-start(f32[1,96,4096]{2,1,0:T(8,128)} %param.48) | copy-start | bytes 4718596
  601.6 43.5 %copy-start.4 = (f32[1,96,2304]{2,1,0:T(8,128)S(1)}, f32[1,96,2304]{2,1,0:T(8,128)}, u32[]{:S(2)}) copy-start(f32[1,96,2304]{2,1,0:T(8,128)} %param.42) | copy-start | bytes 2654212
  601.6 43.5 %copy-start.6 = (f32[1,256,768]{2,1,0:T(8,128)S(1)}, f32[1,256,768]{2,1,0:T(8,128)}, u32[]{:S(2)}) copy-start(f32[1,256,768]{2,1,0:T(8,128)} %param.51) | copy-start | bytes 2359300
  601.6 43.5 %copy-start.8 = (f32[1,96,768]{2,1,0:T(8,128)S(1)}, f32[1,96,768]{2,1,0:T(8,128)}, u32[]{:S(2)}) copy-start(f32[1,96,768]{2,1,0:T(8,128)} %param.45) | copy-start | bytes 884740
  645.1 2.7 copy-start
  (7 other events, 10.4 us)

commit v3 on v2

--- a/solution.py
+++ b/solution.py
@@ -195,10 +195,13 @@
 def gather_kernel(count, pairs, split, orders, errand, *refs):
     ins, refs = refs[:count], refs[count:]
     pair_ins, refs = refs[:pairs], refs[pairs:]
-    errand_in, refs = refs[: 2 * errand], refs[2 * errand :]
+    asked = 2 if errand else 0
+    errand_in, refs = refs[:asked], refs[asked:]
     outs, refs = refs[:count], refs[count:]
     pair_outs, refs = refs[:pairs], refs[pairs:]
-    errand_out, refs = refs[: 2 * errand], refs[2 * errand :]
+    errand_out, refs = refs[:asked], refs[asked:]
+    if errand and pairs:
+        marks_ref, refs = refs[0], refs[1:]
     errand_refs = errand_in + errand_out
     send_sem, recv_sem, cross_sem, pair_sem, local_sem = refs[:5]
     me = Place()
@@ -302,20 +305,35 @@
         for cond, copy in sends:
             when(cond, copy.wait_send)
 
+    if errand and pairs:
+        groups = 2 * pair_ins[0].shape[0]
+        shift = (me.rep * me.shards + me.shard) * errand
+        far_hops = [hops for hops in range(2, nz + 2)]
+
+        def spread_some(n):
+            if n == 0:
+                for copy in locals_[count:]:
+                    copy.wait()
+                for p in range(pairs):
+                    pair_copies[p].wait_send()
+                    remote(
+                        pair_ins[p], pair_outs[p].at[1 - me.core], pair_sem.at[0, p], pair_sem.at[1, p], me.partner()
+                    ).wait_recv()
+            edges = [groups * t // len(far_hops) for t in range(len(far_hops) + 1)]
+            spread_range(edges[n], edges[n + 1], shift, errand, *pair_outs, marks_ref)
+
+        for n, hops in enumerate(far_hops):
+            hooks[hops] = partial(spread_some, n)
+
     for core, plan in enumerate(orders):
         pl.when(me.core == core)(partial(run, core, plan))
     if errand:
         hooks["end"]()
-    for p in range(pairs):
-        pair_copies[p].wait_send()
-        remote(
-            pair_ins[p], pair_outs[p].at[1 - me.core], pair_sem.at[0, p], pair_sem.at[1, p], me.partner()
-        ).wait_recv()
-    for copy in locals_:
+    for copy in locals_[:count]:
         copy.wait()
 
 
-def gather(parts, ident, pair_parts=(), split=False, use_x=True, space=ANY, errand=()):
+def gather(parts, ident, pair_parts=(), split=False, use_x=True, space=ANY, errand=(), rows_each=0):
     count, pairs = len(parts), len(pair_parts)
     every = list(range(count))
     if not use_x:
@@ -338,6 +356,9 @@
             jax.ShapeDtypeStruct((nx, peers) + asks.shape[1:], asks.dtype),
             jax.ShapeDtypeStruct((peers, batch_rows, wide), table.dtype),
         ]
+        if pairs:
+            rows = 2 * pair_parts[2].shape[0]
+            errand_shapes.append(jax.ShapeDtypeStruct((rows, table.shape[0]), jnp.float32))
         errand_scratch = [
             pltpu.VMEM((peers * batch_rows, table.shape[0]), table.dtype),
             pltpu.VMEM((peers, batch_rows, wide), table.dtype),
@@ -346,12 +367,12 @@
             DMA((2,)),
         ]
     outs = pl.pallas_call(
-        partial(gather_kernel, count, pairs, split, orders, bool(errand)),
+        partial(gather_kernel, count, pairs, split, orders, rows_each),
         out_shape=[jax.ShapeDtypeStruct(lead + p.shape, p.dtype) for p in parts]
         + [jax.ShapeDtypeStruct((2,) + p.shape, p.dtype) for p in pair_parts]
         + errand_shapes,
         in_specs=[VMEM] * (count + pairs + len(errand)),
-        out_specs=[space] * (count + pairs) + [VMEM] * len(errand_shapes),
+        out_specs=[space] * count + [VMEM] * pairs + [VMEM] * len(errand_shapes),
         scratch_shapes=[
             DMA((blocks * count * 4,)),
             DMA((count, 2 * nz - 1, ny, nx)),
@@ -399,7 +420,7 @@
             relays.append(copy)
 
     if relay:
-        forward(0, src_ref.at[mine], out_ref.at[me.x, mine])
+        forward(0, src_ref.at[mine if src_ref.shape[0] > 1 else 0], out_ref.at[me.x, mine])
     for p in range(1, peers):
         source, device = me.group(peers - p)
         dst = out_ref.at[section, source]
@@ -590,12 +611,8 @@
                 copy.wait_send()
         own.wait()
 
-    hooks = [begin, partial(sum_step, 0)]
-    middle = (peers + 1) // 2
-    pieces = [partial(relay, 1, middle), partial(relay, middle, peers)]
-    sums = [partial(sum_step, n) for n in range(1, len(steps) + 1)]
-    hooks += [sums[0], pieces[0], sums[1], pieces[1]] + sums[2:] + [finish]
-    return hooks
+    early = [begin] + [partial(sum_step, n) for n in range(len(steps) + 1)]
+    return early, [partial(relay, 1, peers)], [finish]
 
 
 def reduce_kernel(count, sections, sums, *refs):
@@ -664,15 +681,15 @@
             start_core(*b)
         for b in order_of(core):
             start_load(*b)
-        todo = list(hooks)
-
-        def errand(last=False):
-            while todo and (last or len(todo) > 1):
+        early, late, final = [list(part) for part in hooks] if hooks else ([], [], [])
+
+        def errand(todo, every=False):
+            while todo:
                 todo.pop(0)()
-                if not last:
+                if not every:
                     break
 
-        errand()
+        errand(early)
 
         def push(cond, src, dst, sem, device):
             copy = remote(src, dst, send_sem.at[len(sends)], sem, device)
@@ -733,54 +750,82 @@
             )
 
         each = range(count)
-        if core == 0:
-            for i in range(nx - 1, 0, -1):
-                for j in range(ny - 1, -1, -1):
-                    for k in far:
-                        for a in each:
-                            join_core(a, k, j, i)
-                            send_x(a, k, j, i)
-                        errand()
-            for j in range(ny - 1, -1, -1):
-                for k in far:
-                    for a in each:
-                        join_core(a, k, j, 0)
-            for j in range(ny - 1, 0, -1):
-                for k in far:
-                    for a in each:
-                        join_x(a, k, j)
-                        send_y(a, k, j, 0)
-            for k in far:
-                for a in each:
+
+        def x_first(arrays):
+            first, second, third = [], [], []
+
+            def cross_x(k, j, i):
+                for a in arrays:
+                    join_core(a, k, j, i)
+                    send_x(a, k, j, i)
+
+            def join_own(k, j):
+                for a in arrays:
+                    join_core(a, k, j, 0)
+
+            def cross_y(k, j):
+                for a in arrays:
+                    join_x(a, k, j)
+                    send_y(a, k, j, 0)
+
+            def along_z(k):
+                for a in arrays:
                     join_x(a, k, 0)
                     join_y(a, k, 0)
                     join_z(a, k, 0)
                     if k != 0:
                         send_z(a, k, 0)
-        else:
+
+            for i in range(nx - 1, 0, -1):
+                for j in range(ny - 1, -1, -1):
+                    first += [partial(cross_x, k, j, i) for k in far]
+            for j in range(ny - 1, -1, -1):
+                second += [partial(join_own, k, j) for k in far]
             for j in range(ny - 1, 0, -1):
-                for k in far:
-                    for i in range(nx - 1, -1, -1):
-                        for a in each:
-                            join_core(a, k, j, i)
-                            send_y(a, k, j, i)
-                        errand()
-            for k in far:
-                for i in range(nx - 1, -1, -1):
-                    for a in each:
-                        join_core(a, k, 0, i)
-            for k in far:
-                for i in range(nx - 1, -1, -1):
-                    for a in each:
-                        join_y(a, k, i)
-                        join_z(a, k, i)
-                        if k != 0:
-                            send_z(a, k, i)
-                        elif i != 0:
-                            send_x(a, 0, 0, i)
-                        else:
-                            join_x(a, 0, 0)
-        errand(last=True)
+                second += [partial(cross_y, k, j) for k in far]
+            third += [partial(along_z, k) for k in far]
+            return first, second, third
+
+        def y_first(arrays):
+            def cross_y(k, j, i):
+                for a in arrays:
+                    join_core(a, k, j, i)
+                    send_y(a, k, j, i)
+
+            def join_own(k, i):
+                for a in arrays:
+                    join_core(a, k, 0, i)
+
+            def along_z(k, i):
+                for a in arrays:
+                    join_y(a, k, i)
+                    join_z(a, k, i)
+                    if k != 0:
+                        send_z(a, k, i)
+                    elif i != 0:
+                        send_x(a, 0, 0, i)
+                    else:
+                        join_x(a, 0, 0)
+
+            slots = range(nx - 1, -1, -1)
+            first = [partial(cross_y, k, j, i) for j in range(ny - 1, 0, -1) for k in far for i in slots]
+            second = [partial(join_own, k, i) for k in far for i in slots]
+            third = [partial(along_z, k, i) for k in far for i in slots]
+            return first, second, third
+
+        plans = [x_first(list(each)) if core == 0 else y_first(list(each))]
+        for stage in range(3):
+            lists = [plan[stage] for plan in plans if plan[stage]]
+            longest = max(len(steps) for steps in lists)
+            if stage == 1:
+                errand(early, every=True)
+                errand(late, every=True)
+            for n in range(longest):
+                for steps in lists:
+                    for step in steps[len(steps) * n // longest : len(steps) * (n + 1) // longest]:
+                        step()
+                errand(early)
+        errand(final, every=True)
         finals = []
         for a in each:
             copy = remote(
@@ -887,44 +932,57 @@
     return out, extra
 
 
-def spread_kernel(columns_ref, weight_ref, target_ref, out_ref):
-    groups, entries = columns_ref.shape[0], columns_ref.shape[2]
+def spread_group(columns, values, target, high):
+    entries = columns.shape[1]
+    each = entries // 8
+    row = lax.broadcasted_iota(jnp.int32, (1, entries), 1) // each
+    key = jnp.where(columns >= 0, (columns // 128) * 8 + row, -1)
+    low_part = jnp.where(columns >= 0, lax.rem(columns, 128), -1)
+    left = jnp.where(key == lax.broadcasted_iota(jnp.int32, (high * 8, entries), 0), values, 0.0).astype(jnp.bfloat16)
+    right = jnp.where(low_part == lax.broadcasted_iota(jnp.int32, (128, entries), 0), 1.0, 0.0).astype(jnp.bfloat16)
+    placed = lax.dot_general(left, right, (((1,), (1,)), ((), ())), preferred_element_type=jnp.float32)
+    pieces = []
+    for h in range(high):
+        one = jnp.where(lax.broadcasted_iota(jnp.int32, (8, 128), 1) + 128 * h == target, 1.0, 0.0)
+        pieces.append(placed[h * 8 : (h + 1) * 8] + one)
+    return pieces
+
+
+def spread_range(first, last, shift, rows_each, columns_ref, weight_ref, target_ref, out_ref):
     high = out_ref.shape[1] // 128
-    each = entries // 8
+    per = columns_ref.shape[1]
+
+    def local_of(ids):
+        column = ids - shift
+        return jnp.where((column >= 0) & (column < rows_each), column, -1)
 
     def body(g, carry):
-        column = columns_ref[g]
-        value = weight_ref[g]
-        row = lax.broadcasted_iota(jnp.int32, (1, entries), 1) // each
-        key = jnp.where(column >= 0, (column // 128) * 8 + row, -1)
-        low_part = jnp.where(column >= 0, lax.rem(column, 128), -1)
-        left = jnp.where(
-            key == lax.broadcasted_iota(jnp.int32, (high * 8, entries), 0), value, 0.0
-        ).astype(jnp.bfloat16)
-        right = jnp.where(
-            low_part == lax.broadcasted_iota(jnp.int32, (128, entries), 0), 1.0, 0.0
-        ).astype(jnp.bfloat16)
-        dims = (((1,), (1,)), ((), ()))
-        placed = lax.dot_general(left, right, dims, preferred_element_type=jnp.float32)
+        pair, place = g // per, lax.rem(g, per)
+        target = target_ref[pair, pl.ds(pl.multiple_of(place * 8, 8), 8), :]
+        pieces = spread_group(local_of(columns_ref[pair, place]), weight_ref[pair, place], local_of(target), high)
         at = pl.ds(pl.multiple_of(g * 8, 8), 8)
-        target = target_ref[at, :]
         for h in range(high):
-            one = jnp.where(lax.broadcasted_iota(jnp.int32, (8, 128), 1) + 128 * h == target, 1.0, 0.0)
-            out_ref[at, h * 128 : (h + 1) * 128] = placed[h * 8 : (h + 1) * 8] + one
+            out_ref[at, h * 128 : (h + 1) * 128] = pieces[h]
         return carry
 
-    lax.fori_loop(0, groups, body, 0)
-
-
-def spread_entries(columns, values, targets, width):
-    rows, each = columns.shape
+    lax.fori_loop(first, last, body, 0)
+
+
+def spread_kernel(rows_each, shift_ref, columns_ref, weight_ref, target_ref, out_ref):
+    spread_range(
+        0, columns_ref.shape[0] * columns_ref.shape[1], shift_ref[0], rows_each, columns_ref, weight_ref, target_ref, out_ref
+    )
+
+
+def spread_entries(shift, columns, values, targets, rows_each, width):
+    rows = targets.shape[0] * targets.shape[1]
     return pl.pallas_call(
-        spread_kernel,
+        partial(spread_kernel, rows_each),
         out_shape=jax.ShapeDtypeStruct((rows, width), jnp.float32),
-        in_specs=[VMEM] * 3,
+        in_specs=[pl.BlockSpec(memory_space=pltpu.SMEM)] + [VMEM] * 3,
         out_specs=VMEM,
         name="spread_entries",
-    )(columns.reshape(rows // 8, 1, 8 * each), values.reshape(rows // 8, 1, 8 * each), targets[:, None])
+    )(shift, columns, values, targets)
 
 
 def ask_kernel(owners, token_row, token_col, owner_row, owner_col, row_col, hot_ref, ask_ref):
@@ -1072,15 +1130,22 @@
 
 def forward_kernel(layer, round_input, x_ref, allowed_ref, w_in, w_out, w_up, w_down, forget_ref, bias_ref, gain_ref,
                    y_ref, qkv_ref, logit_ref, lse_ref, att_ref, mid_ref, gu_ref,
-                   b_in, b_out, b_up, b_down, gu_buf, hidden, mask, sem, gu_sem):
+                   b_in, b_out, b_up, b_down, gu_buf, hidden, mask, sem, gu_sem, in_sem):
     tree_len, width = x_ref.shape
     heads = width // 64
     half = hidden.shape[1]
-    loads = [
+    loads = [None] + [
         pltpu.make_async_copy(src.at[layer], dst, sem.at[n])
-        for n, (src, dst) in enumerate(((w_in, b_in), (w_out, b_out), (w_up, b_up), (w_down, b_down)))
+        for n, (src, dst) in enumerate(((w_out, b_out), (w_up, b_up), (w_down, b_down)))
     ]
-    for copy in loads:
+
+    def first_load(n):
+        at = pl.ds(pl.multiple_of(n * 256, 256), 256)
+        return pltpu.make_async_copy(w_in.at[layer, :, at], b_in.at[:, at], in_sem.at[n])
+
+    for n in range(3 * width // 256):
+        first_load(n).start()
+    for copy in loads[1:]:
         copy.start()
     x = x_ref[...]
     if round_input:
@@ -1091,9 +1156,8 @@
     logit = product(act, forget_ref[...]) + bias_ref[...]
     logit_ref[...] = logit
     cumul = sum(product(allowed, part) for part in three_parts(log_sigmoid(logit)))
-    loads[0].wait()
-
     def project(n, carry):
+        first_load(n).wait()
         at = pl.ds(pl.multiple_of(n * 256, 256), 256)
         qkv_ref[:, at] = lower(product(act, b_in[:, at]))
         return carry
@@ -1187,6 +1251,7 @@
             pltpu.VMEM((tree_len, tree_len), f32),
             DMA((4,)),
             DMA((half // 512, 2)),
+            DMA((3 * width // 256,)),
         ],
         compiler_params=pltpu.CompilerParams(vmem_limit_bytes=56 * 2**20),
         name=f"forward_{layer}",
@@ -1202,24 +1267,21 @@
     heads = width // 64
     half = b_down.shape[0]
     chunk = 256
-    gu_loads = [
-        [
-            pltpu.make_async_copy(
-                gu_hbm.at[:, pl.ds(n * chunk + s * half, chunk)], gu.at[:, pl.ds(n * chunk + s * half, chunk)], gu_sem.at[n, s]
-            )
-            for s in range(2)
-        ]
-        for n in range(half // chunk)
+    loads = [
+        pltpu.make_async_copy(src.at[layer], dst, sem.at[n]) for n, (src, dst) in enumerate(((w_in, b_in), (w_out, b_out)))
     ]
-    loads = [
-        pltpu.make_async_copy(src.at[layer], dst, sem.at[n])
-        for n, (src, dst) in enumerate(((w_in, b_in), (w_out, b_out), (w_up, b_up), (w_down, b_down)))
-    ]
-    loads[3].start()
-    for pair_copies in gu_loads:
-        for copy in pair_copies:
+    def feed_loads(n):
+        at = pl.ds(pl.multiple_of(n * chunk, chunk), chunk)
+        at_up = pl.ds(pl.multiple_of(half + n * chunk, chunk), chunk)
+        pairs = ((gu_hbm.at[:, at], gu.at[:, at]), (gu_hbm.at[:, at_up], gu.at[:, at_up]),
+                 (w_down.at[layer, at], b_down.at[at]), (w_up.at[layer, :, at], b_up.at[:, at]),
+                 (w_up.at[layer, :, at_up], b_up.at[:, at_up]))
+        return [pltpu.make_async_copy(src, dst, gu_sem.at[n, s]) for s, (src, dst) in enumerate(pairs)]
+
+    for n in range(half // chunk):
+        for copy in feed_loads(n):
             copy.start()
-    for n in (2, 1, 0):
+    for n in (1, 0):
         loads[n].start()
     dy = dy_ref[...]
     if round_grad:
@@ -1228,13 +1290,10 @@
     normed_b, inverse_b, act_b = norm_parts(mid_ref[...], gain_ref[1:2, :])
     act_t[...] = lower((normed_b * gain_ref[1:2, :]).T)
     grad_b[...] = jnp.zeros_like(grad_b)
-    loads[3].wait()
-    for copies in gu_loads:
-        for copy in copies:
+
+    def feed(n, carry):
+        for copy in feed_loads(n):
             copy.wait()
-    loads[2].wait()
-
-    def feed(n, carry):
         at = pl.ds(pl.multiple_of(n * chunk, chunk), chunk)
         at_up = pl.ds(pl.multiple_of(half + n * chunk, chunk), chunk)
         gate, upper = gu[:, at], gu[:, at_up]
@@ -1321,10 +1380,10 @@
     grad_logit = rising / (1.0 + jnp.exp(logit))
     lane = lax.broadcasted_iota(jnp.int32, grad_logit.shape, 1)
     grad_logit = lower(jnp.where(lane < heads, grad_logit, 0.0))
-    dforget_ref[0:128, :] = dims_tn(grad_logit, act_a)
-    bias = jnp.sum(grad_logit.astype(jnp.float32), axis=0, keepdims=True)
-    dforget_ref[128:136, :] = jnp.concatenate(
-        [jnp.broadcast_to(bias, (8, 128)), jnp.zeros((8, width - 128), jnp.float32)], axis=1
+    dforget_ref[:, 0:width] = dims_tn(grad_logit, act_a)[0:16, :]
+    bias = dims_tn(grad_logit, jnp.ones((tree_len, 128), jnp.bfloat16))[0:16, :]
+    dforget_ref[:, width : width + 128] = jnp.where(
+        lax.broadcasted_iota(jnp.int32, (16, 128), 1) == 0, bias, 0.0
     )
 
     def weigh(n, carry):
@@ -1361,7 +1420,7 @@
         partial(backward_kernel, layer, round_input, round_grad),
         out_shape=[
             shape((tree_len, width), f32),
-            shape((136, width), f32),
+            shape((16, width + 128), f32),
             shape((8, width), f32),
         ]
         + [shape(w.shape[1:], b16) for w in mats],
@@ -1377,7 +1436,7 @@
             pltpu.VMEM((tree_len, 128), f32),
         ]
         + [pltpu.VMEM(w.shape[1:], b16) for w in mats]
-        + [DMA((4,)), DMA((half // 256, 2)), DMA((4,))],
+        + [DMA((4,)), DMA((half // 256, 5)), DMA((4,))],
         compiler_params=pltpu.CompilerParams(vmem_limit_bytes=60 * 2**20),
         name=f"backward_{layer}",
     )(grad, values, allowed, qkv, logit, lse, att, middle, forget_w, gains, gate_up, *mats)
@@ -1486,8 +1545,9 @@
     return carry
 
 
-def step_kernel(shapes, scalar_ref, sums_ref, forget_sum_ref, gains_sum_ref, *refs):
+def step_kernel(shapes, scalar_ref, sums_ref, *refs):
     n = len(shapes)
+    small_sums, refs = refs[:5], refs[5:]
     small_in, refs = refs[:6], refs[6:]
     grads, refs = refs[:n], refs[n:]
     weights, refs = refs[:n], refs[n:]
@@ -1531,9 +1591,9 @@
     def scalar_at(values, r, c):
         return jnp.sum(jnp.where((row == r) & (lane == c), values, 0.0))
 
-    forget_sum, gains_sum = forget_sum_ref[...], gains_sum_ref[...]
+    smalls = [ref[...] for ref in small_sums]
     norm = jnp.sqrt(
-        jnp.full((1, 1), scalar_at(sums_ref[...], 0, 0) + square_sum(forget_sum) + square_sum(gains_sum))
+        jnp.full((1, 1), scalar_at(sums_ref[...], 0, 0) + sum(square_sum(v) for v in smalls))
     )
     clip = jnp.minimum(1.0, scalar_ref[2] / norm)
     inverse_first = scalar_ref[0]
@@ -1548,25 +1608,23 @@
         ) + decay_rate * weight
         return first_new, second_new, direction
 
+    def small_step(group, part, grad):
+        w_ref, m_ref, v_ref = small_in[3 * group : 3 * group + 3]
+        weight = w_ref[part]
+        first_new, second_new, direction = adam(weight, grad, m_ref[part], v_ref[part])
+        norms = [jnp.sqrt(jnp.full((1, 1), square_sum(v))) for v in (weight, direction)]
+        small_out[3 * group][part] = weight - learn_rate * (norms[0] / norms[1]) * direction
+        small_out[3 * group + 1][part] = first_new
+        small_out[3 * group + 2][part] = second_new
+        return norms
+
+    features, heads = small_in[0].shape[1:]
     small_norms = []
-    for s, (grad, group) in enumerate(((forget_sum, scalar_heads(forget_sum)), (gains_sum, 1))):
-        w_ref, m_ref, v_ref = small_in[3 * s : 3 * s + 3]
-        weight = w_ref[...]
-        first_new, second_new, direction = adam(weight, grad, m_ref[...], v_ref[...])
-        w_norm = jnp.sum(weight * weight, axis=1, keepdims=True)
-        d_norm = jnp.sum(direction * direction, axis=1, keepdims=True)
-        rows = weight.shape[0]
-        owner = lax.broadcasted_iota(jnp.int32, (rows, 1), 0) // group
-        ratio = jnp.zeros((rows, 1), jnp.float32)
-        for t in range(-(-rows // group)):
-            ours = owner == t
-            w_total = jnp.sqrt(jnp.full((1, 1), jnp.sum(jnp.where(ours, w_norm, 0.0))))
-            d_total = jnp.sqrt(jnp.full((1, 1), jnp.sum(jnp.where(ours, d_norm, 0.0))))
-            ratio = jnp.where(ours, w_total / d_total, ratio)
-            small_norms += [w_total, d_total]
-        small_out[3 * s][...] = weight - learn_rate * ratio * direction
-        small_out[3 * s + 1][...] = first_new
-        small_out[3 * s + 2][...] = second_new
+    for layer in range(2):
+        small_norms += small_step(0, layer, smalls[layer].T[0:features, 0:heads])
+    for t in range(5):
+        grad = smalls[2 + t // 2][t % 2 : t % 2 + 1, :]
+        small_norms += small_step(1, slice(t, t + 1), grad)
     table = jnp.where((row == 0) & (lane == 0), norm, 0.0)
     for t, value in enumerate(small_norms):
         table = jnp.where((row == 1) & (lane == t), value, table)
@@ -1612,11 +1670,7 @@
             copy.wait()
 
 
-def scalar_heads(forget_sum):
-    return forget_sum.shape[0] // 2
-
-
-def optimizer_step(scalars, sums, forget_sum, gains_sum, small, grads, weights, firsts, seconds):
+def optimizer_step(scalars, sums, small_sums, small, grads, weights, firsts, seconds):
     n = len(grads)
     shapes = [w.shape for w in weights]
     flat = [jax.ShapeDtypeStruct(s, jnp.float32) for s in shapes]
@@ -1627,19 +1681,27 @@
         out_shape=flat * 3
         + [jax.ShapeDtypeStruct(s.shape, jnp.float32) for s in small]
         + [jax.ShapeDtypeStruct((8, 128), jnp.float32)] * 2,
-        in_specs=[pl.BlockSpec(memory_space=pltpu.SMEM)] + [VMEM] * 9 + [ANY] * (4 * n),
+        in_specs=[pl.BlockSpec(memory_space=pltpu.SMEM)] + [VMEM] * 12 + [ANY] * (4 * n),
         out_specs=[ANY] * (3 * n) + [VMEM] * 8,
         scratch_shapes=buffers([g.dtype for g in grads])
         + buffers([jnp.float32] * n) * 4
         + [DMA((parts, 4)), DMA((parts, 3))],
         compiler_params=pltpu.CompilerParams(vmem_limit_bytes=60 * 2**20),
         name="optimizer_step",
-    )(scalars, sums, forget_sum, gains_sum, *small, *grads, *weights, *firsts, *seconds)
+    )(scalars, sums, *small_sums, *small, *grads, *weights, *firsts, *seconds)
     return out[:n], out[n : 2 * n], out[2 * n : 3 * n], out[3 * n : 3 * n + 6], out[-2], out[-1]
 
 
-def apply_kernel(shapes, ratio_ref, *refs):
+def apply_kernel(shapes, norm_ref, *refs):
     n = len(shapes)
+    norms = jnp.sqrt(norm_ref[...])
+    lane = lax.broadcasted_iota(jnp.int32, (8, 128), 1)
+    row = lax.broadcasted_iota(jnp.int32, (8, 128), 0)
+
+    def norm_at(a, q):
+        place = q if a == 0 else 2 * lax.axis_index("section") + q
+        return jnp.full((1, 1), jnp.sum(jnp.where((row == a) & (lane == place), norms, 0.0)))
+
     weights, directions, outs = refs[:n], refs[n : 2 * n], refs[2 * n : 3 * n]
     w_buf, d_buf = refs[3 * n : 4 * n], refs[4 * n : 5 * n]
     load_sem, store_sem = refs[5 * n :]
@@ -1661,7 +1723,7 @@
         for copy in loads:
             copy.wait()
         w, d = w_buf[a].at[pl.ds(at, part)], d_buf[a].at[pl.ds(at, part)]
-        rate = ratio_ref[a]
+        rate = learn_rate * (norm_at(a, 0) / norm_at(a, 1))
 
         def tile(rows, cols, carry):
             w[rows, cols] = w[rows, cols] - rate * d[rows, cols]
@@ -1673,19 +1735,19 @@
         store.wait()
 
 
-def apply_step(rates, weights, directions):
+def apply_step(norms, weights, directions):
     n = len(weights)
     shapes = [w.shape for w in weights]
     parts = sum(len(pieces_of(s[0])) for s in shapes)
     return pl.pallas_call(
         partial(apply_kernel, shapes),
         out_shape=[jax.ShapeDtypeStruct(s, jnp.float32) for s in shapes],
-        in_specs=[pl.BlockSpec(memory_space=pltpu.SMEM)] + [ANY] * (2 * n),
+        in_specs=[VMEM] + [ANY] * (2 * n),
         out_specs=[ANY] * n,
         scratch_shapes=[pltpu.VMEM(s, jnp.float32) for s in shapes] * 2 + [DMA((parts, 2)), DMA((parts,))],
-        compiler_params=pltpu.CompilerParams(vmem_limit_bytes=40 * 2**20),
+        compiler_params=pltpu.CompilerParams(vmem_limit_bytes=62 * 2**20),
         name="apply_step",
-    )(rates, *weights, *directions)
+    )(norms, *weights, *directions)
 
 
 def lower(values):
@@ -1813,12 +1875,7 @@
         return rows.reshape(owners, batch_rows), lower(hot)
 
     def all_devices(part, ident):
-        if replicas != 2:
-            out = part
-            for axis in ("shard", "replica", "section"):
-                out = lax.all_gather(out, axis)
-            return out
-        return jnp.swapaxes(gather([part], ident, space=VMEM)[0][0], 1, 2)
+        return exchange(part[None], ident, relay=True).reshape((sections, replicas, shards) + part.shape)
 
     def wanted(batch):
         rows, hot = asked(batch)
@@ -1843,7 +1900,8 @@
         hot_more, pick = wanted(batch)
         sent = lower(product(hot_more, embed_low)).reshape(owners, batch_rows, width)
         got_more = exchange(sent, 6, relay=True).reshape(sections * owners * batch_rows, width)
-        return (batch + 1, total_rows + product_left(pick, got_more))
+        more = product_left(pick, got_more)
+        return (batch + 1, total_rows + jnp.pad(more, ((0, width_all - rows_each), (0, 0))))
 
     def halves(weight):
         return lower(weight).reshape(2, weight.shape[1] // 2, weight.shape[2])
@@ -1851,14 +1909,20 @@
     width_all = -(-rows_each // 128) * 128
     table_wide = jnp.pad(table_low, ((0, width_all - rows_each), (0, 0)))
     layer_weights = (attention_in, attention_out, feedforward_in, feedforward_out)
-    group_data = [targets, teacher_index.reshape(group_trees, -1), teacher_probability.reshape(group_trees, -1)]
+    entries = 8 * teacher_index.shape[2]
+    group_data = [
+        teacher_index.reshape(-1, 1, entries),
+        teacher_probability.reshape(-1, 1, entries),
+        targets.reshape(-1, 1),
+    ]
     pair_parts = group_data if replicas == 2 else []
     hot, asks = ask_rows(tree_tokens, token_owner, token_row, owners)
-    gathered, group_all, (asked_all, got) = gather(
-        [halves(w) for w in layer_weights], 2, pair_parts, split=True, errand=(asks, table_wide)
+    gathered, group_all, (asked_all, got, *marks) = gather(
+        [halves(w) for w in layer_weights], 2, pair_parts, split=True, errand=(asks, table_wide), rows_each=rows_each
     )
     if replicas != 2:
         group_all = [lax.all_gather(part, "replica") for part in group_data]
+        marks = [spread_entries((owner_id * rows_each)[None], *group_all, rows_each, width_all)]
     batches = (jnp.max(asked_all[:, :, 0, 127]) + batch_rows - 1) // batch_rows
     embeds = product_left(hot, got.reshape(owners * batch_rows, width))
     _, embeds = lax.while_loop(lambda s: s[0] < batches, more_rows, (jnp.int32(1), embeds))
@@ -1879,15 +1943,8 @@
     head_out, head_normed, head_inverse = rms_forward(picked, final_gain)
     head_rows = jnp.swapaxes(all_devices(lower(head_out), 3), 0, 1).reshape(pos_all, width)
 
-    target_all, index_all, prob_all = [
-        part.reshape((pos_all,) + (-1,) * (n > 0)) for n, part in enumerate(group_all)
-    ]
-
-    def owned(ids):
-        column = ids - owner_id * rows_each
-        return jnp.where((column >= 0) & (column < rows_each), column, -1)
-
-    marks = spread_entries(owned(index_all), prob_all, owned(target_all), width_all)
+    prob_all = group_all[1].reshape(pos_all, -1)
+    marks = marks[0]
     logits, stats = head_forward(rows_each, head_rows, table_wide, marks)
     if replicas == 2:
         stats_all = exchange(stats[None], 4)[0]
@@ -1914,28 +1971,12 @@
     stacked = [
         [g.reshape(shards, 2, -1, g.shape[-1]) for g in pair] for pair in zip(grads_0, grads_1)
     ]
-    def forget_form(values):
-        return jnp.pad(jnp.swapaxes(values, 1, 2).reshape(-1, values.shape[1]), ((0, 0), (0, -values.shape[1] % 128)))
-
-    def forget_terms(values):
-        bias = jnp.swapaxes(values[128:129, :heads], 0, 1)
-        return jnp.concatenate([values[:heads], jnp.pad(bias, ((0, 0), (0, -(width + 1) % 128)))], axis=1)
-
-    def forget_back(values):
-        return jnp.swapaxes(values[:, : width + 1].reshape(forget_gate.shape[0], -1, width + 1), 1, 2)
-
-    def gains_form(values):
-        return jnp.pad(values, ((0, 8 - values.shape[0]), (0, 0)))
-
     sent = lower(product(hot, embed_low)).reshape(owners, batch_rows, width)
-    small_sums = [
-        jnp.concatenate([forget_terms(forget_0), forget_terms(forget_1)], axis=0),
-        gains_form(jnp.concatenate([gains_0[:2], gains_1[:2], grad_final[None]], axis=0)),
-    ]
-    layer_grads, (forget_total, gains_total, got_grads) = reduce_parts(stacked, 8, (small_sums, sent))
+    small_sums = [forget_0, forget_1, gains_0, gains_1, grad_final[None]]
+    layer_grads, (*small_sums, got_grads) = reduce_parts(stacked, 8, (small_sums, sent))
     if replicas != 2:
         layer_grads = [lax.psum(g * jnp.bfloat16(0.5), "replica") for g in layer_grads]
-    _, head_table = lax.while_loop(lambda s: s[0] < batches, more_grads, (jnp.int32(1), head_table[:rows_each]))
+    _, head_table = lax.while_loop(lambda s: s[0] < batches, more_grads, (jnp.int32(1), head_table))
     table_grad, square = table_gradient(
         rows_each, asked_all, got_grads.reshape(-1, width), head_table, layer_grads
     )
@@ -1950,9 +1991,7 @@
             clip_factor / jnp.sqrt(jnp.float32(pos_all)),
         ]
     )
-    small = [forget_form(v) for v in (forget_gate, forget_first, forget_second)] + [
-        gains_form(v) for v in (norm_gains, gains_first, gains_second)
-    ]
+    small = [forget_gate, forget_first, forget_second, norm_gains, gains_first, gains_second]
     weights = [embed_table] + [w[0] for w in layer_weights]
     firsts = [table_first] + [
         m[0] for m in (attention_in_first, attention_out_first, feedforward_in_first, feedforward_out_first)
@@ -1961,25 +2000,22 @@
         m[0] for m in (attention_in_second, attention_out_second, feedforward_in_second, feedforward_out_second)
     ]
     firsts_new, seconds_new, directions, small_new, norms, small_norms = optimizer_step(
-        rates, scalars, forget_total, gains_total, small, [table_grad, *layer_grads], weights, firsts, seconds
+        rates, scalars, small_sums, small, [table_grad, *layer_grads], weights, firsts, seconds
     )
-    norms = jnp.sqrt(total([norms], 16)[0])
+    (norms,) = total([norms], 16)
+    weights_new = apply_step(norms, weights, directions)
+    norms = jnp.sqrt(norms)
     table_norms = norms[0, :2]
-    layer_norms = norms[1:5, : 2 * sections].reshape(4, sections, 2)
-    mine = lax.dynamic_index_in_dim(layer_norms, section_id, 1, keepdims=False)
-    both_norms = jnp.concatenate([table_norms[None], mine], axis=0)
-    weights_new = apply_step(learn_rate * both_norms[:, 0] / both_norms[:, 1], weights, directions)
+    layer_norms = norms[1:5, : 2 * sections].reshape(4 * sections, 2)
     new_table, table_first_new, table_second_new = weights_new[0], firsts_new[0], seconds_new[0]
     new_layers = [(weights_new[n][None], firsts_new[n][None], seconds_new[n][None]) for n in range(1, 5)]
-    new_forget, forget_first_new, forget_second_new = [forget_back(v) for v in small_new[:3]]
-    gain_count = norm_gains.shape[0]
-    new_gains, gains_first_new, gains_second_new = [v[:gain_count] for v in small_new[3:]]
-    layer_count = forget_gate.shape[0]
+    new_forget, forget_first_new, forget_second_new, new_gains, gains_first_new, gains_second_new = small_new
+    layer_count, gain_count = forget_gate.shape[0], norm_gains.shape[0]
     grad_norm = small_norms[0, 0]
     tensor_norms = jnp.concatenate(
         [
             table_norms[None],
-            layer_norms.reshape(4 * sections, 2),
+            layer_norms,
             small_norms[1, : 2 * (layer_count + gain_count)].reshape(-1, 2),
         ],
         axis=0,

time: 677 us -> 647 us (0.956)
  local copies, waits for them, and re-layouts: 48.7 us -> 27.4 us
    pallas_call x3 -> x1, Pallas kernels: 170 us -> 136 us  [gather(): pl.pallas_call(partial(gather_kernel, count, pairs, split, orders, rows_e...]
    pallas_call x2 -> x3, Pallas kernels: 24.5 us -> 44.8 us  [exchange(): pl.pallas_call(partial(exchange_kernel, relay), out_shape=jax.ShapeDtypeS...]
    slice x7 -> x1, local copies, waits for them, and re-layouts: 8.97 us -> 0.01 us  [local(): layer_norms = norms[1:5, :2 * sections].reshape(4 * sections, 2)]
    pallas_call x2, Pallas kernels: 83.1 us -> 75.2 us  [layer_backward(): pl.pallas_call(partial(backward_kernel, layer, round_input, round_grad),...]
where the time goes in v3:
time: 647 us; the launch traced here: 638 us
  Pallas kernels  583 us (90%)
  local copies, waits for them, and re-layouts  27.4 us (4%)
  other arithmetic  15.8 us (2%)
    pallas_call x1, Pallas kernels, reduce_shards(): pl.pallas_call(partial(reduce_kernel, count, nx, sums), out_shape=[jax.Sh...  164 us
    pallas_call x1, Pallas kernels, gather(): pl.pallas_call(partial(gather_kernel, count, pairs, split, orders, rows_e...  136 us
    pallas_call x2, Pallas kernels, layer_backward(): pl.pallas_call(partial(backward_kernel, layer, round_input, round_grad),...  75.2 us
    pallas_call x2, Pallas kernels, layer_forward(): pl.pallas_call(partial(forward_kernel, layer, round_input), out_shape=[sh...  47.2 us
    pallas_call x3, Pallas kernels, exchange(): pl.pallas_call(partial(exchange_kernel, relay), out_shape=jax.ShapeDtypeS...  44.8 us
    pallas_call x2, Pallas kernels, total(): pl.pallas_call(partial(total_kernel, count), out_shape=[jax.ShapeDtypeStr...  41.5 us
    pallas_call x1, Pallas kernels, optimizer_step(): pl.pallas_call(partial(step_kernel, shapes), out_shape=flat * 3 + [jax.Sh...  26.8 us

profile of v3, /device:TPU:0, one launch (start us, length us, event | category | flops | bytes accessed | tf_op | source)
XLA Modules:
  0.0 638.0 jit_solution(11385466850589781672)
XLA Ops:
  3.0 2.5 ask_rows.1
  5.5 3.0 convert_element_type.113
  8.6 1.8 pad.48.refs_8_.table_ref
  16.7 136.1 %gather_2.1 = (bf16[2,8,2,48,2304]{4,3,2,1,0:T(8,128)(2,1)}, bf16[2,8,2,48,768]{4,3,2,1,0:T(8,128)(2,1)}, bf16[2,8,2,48,4096]{4,3,2,1,0:T(8,128)(2,1)}, bf16[2,8...) custom-call(bf16[2,48,2304]{2,1,0:T(8,128)(2,1)} %bitcast.187, ...), custom_call_target="tpu_custom_call" | custom-call | tf_op jit(solution)/shard_map/gather_2/pallas_call | solution.py:369
  154.9 1.6 fusion.73
  162.6 23.5 %forward_0.1 = (f32[320,768]{1,0:T(8,128)}, bf16[320,2304]{1,0:T(8,128)(2,1)}, f32[320,128]{1,0:T(8,128)}, f32[320,128]{1,0:T(8,128)}, bf16[320,768]{1,0:T(8,128...) custom-call(f32[320,768]{1,0:T(8,128)S(1)} %get-tuple-element.648.x_ref, bf16[320,320]{1,0:T(8,128)(2,1)} %fusion.21.allowed_ref, ...), custom_call_target="tpu_custom_call" | custom-call | tf_op jit(solution)/shard_map/forward_0/pallas_call | solution.py:1234
  186.7 23.7 %forward_1.1 = (f32[320,768]{1,0:T(8,128)}, bf16[320,2304]{1,0:T(8,128)(2,1)}, f32[320,128]{1,0:T(8,128)}, f32[320,128]{1,0:T(8,128)}, bf16[320,768]{1,0:T(8,128...) custom-call(f32[320,768]{1,0:T(8,128)} %get-tuple-element.653.x_ref, bf16[320,320]{1,0:T(8,128)(2,1)} %fusion.21.allowed_ref, ...), custom_call_target="tpu_custom_call" | custom-call | tf_op jit(solution)/shard_map/forward_1/pallas_call | solution.py:1234
  211.2 1.8 gather_fusion
  214.6 20.3 %exchange_3.1 = bf16[2,16,16,768]{3,2,1,0:T(8,128)(2,1)} custom-call(bf16[1,16,768]{2,1,0:T(8,128)(2,1)} %fusion.37.src_ref), custom_call_target="tpu_custom_call" | custom-call | tf_op jit(solution)/shard_map/exchange_3/pallas_call | solution.py:444
  235.0 2.1 copy.97
  237.0 10.6 %head_forward.1 = (f32[512,2048]{1,0:T(8,128)}, f32[4,512]{1,0:T(4,128)}) custom-call(bf16[512,768]{1,0:T(8,128)(2,1)} %bitcast.170, bf16[2048,768]{1,0:T(8,128)(2,1)} %pad.48.refs_8_.table_ref, f32[512,2048]{1,0:T(8,128)} %get-tuple-element.655.marks_ref), custom_call_target="tpu_custom_call" | custom-call | tf_op jit(solution)/shard_map/head_forward/pallas_call | solution.py:1470
  247.7 9.6 %exchange_4.1 = f32[1,16,4,512]{3,2,1,0:T(4,128)} custom-call(f32[1,4,512]{2,1,0:T(4,128)} %bitcast.209), custom_call_target="tpu_custom_call" | custom-call | tf_op jit(solution)/shard_map/exchange_4/pallas_call | solution.py:444
  258.4 12.8 %head_backward.1 = (bf16[256,768]{1,0:T(8,128)(2,1)}, f32[2048,768]{1,0:T(8,128)}, f32[8,128]{1,0:T(8,128)}) custom-call(bf16[512,768]{1,0:T(8,128)(2,1)} %bitcast.171, bf16[2048,768]{1,0:T(8,128)(2,1)} %pad.48.refs_8_.table_ref, f32[512,2048]{1,0:T(8,128)} %get-tuple-element.655.marks_ref, f32[512,2048]{1,0:T(8,128)} %get-tuple-element.656.logits_ref, ...), custom_call_target="tpu_custom_call" | custom-call | tf_op jit(solution)/shard_map/head_backward/pallas_call | solution.py:1511
  271.3 14.8 %exchange_5.1 = bf16[1,16,16,768]{3,2,1,0:T(8,128)(2,1)} custom-call(bf16[16,16,768]{2,1,0:T(8,128)(2,1)} %bitcast.205), custom_call_target="tpu_custom_call" | custom-call | tf_op jit(solution)/shard_map/exchange_5/pallas_call | solution.py:444
  287.4 1.6 fusion.38.dy_ref
  289.0 37.6 %backward_1.1 = (f32[320,768]{1,0:T(8,128)}, f32[16,896]{1,0:T(8,128)}, f32[8,768]{1,0:T(8,128)}, bf16[768,2304]{1,0:T(8,128)(2,1)}, bf16[768,768]{1,0:T(8,128)(...) custom-call(f32[320,768]{1,0:T(8,128)} %fusion.38.dy_ref, f32[320,768]{1,0:T(8,128)} %get-tuple-element.653.x_ref, ...), custom_call_target="tpu_custom_call" | custom-call | tf_op jit(solution)/shard_map/backward_1/pallas_call | solution.py:1419
  326.6 37.6 %backward_0.1 = (f32[320,768]{1,0:T(8,128)}, f32[16,896]{1,0:T(8,128)}, f32[8,768]{1,0:T(8,128)}, bf16[768,2304]{1,0:T(8,128)(2,1)}, bf16[768,768]{1,0:T(8,128)(...) custom-call(f32[320,768]{1,0:T(8,128)} %get-tuple-element.666.dy_ref, ...), custom_call_target="tpu_custom_call" | custom-call | tf_op jit(solution)/shard_map/backward_0/pallas_call | solution.py:1419
  368.0 163.7 %reduce_8.1 = (bf16[2,48,2304]{2,1,0:T(8,128)(2,1)}, bf16[2,48,768]{2,1,0:T(8,128)(2,1)}, bf16[2,48,4096]{2,1,0:T(8,128)(2,1)}, bf16[2,128,768]{2,1,0:T(8,128)(2...) custom-call(bf16[8,2,48,2304]{3,2,1,0:T(8,128)(2,1)} %bitcast.177, ...), custom_call_target="tpu_custom_call" | custom-call | tf_op jit(solution)/shard_map/reduce_8/pallas_call | solution.py:884
  531.7 10.6 %table_gradient.1 = (f32[2000,768]{1,0:T(8,128)}, f32[8,128]{1,0:T(8,128)}) custom-call(s32[2,16,1,128]{3,2,1,0:T(1,128)} %get-tuple-element.645.asked_ref, bf16[1024,768]{1,0:T(8,128)(2,1)} %bitcast.193, f32[2048,768]{1,0:T(8,128)} %get-tuple-element.688.head_ref, bf16[2,48,2304]{2,1,0:T(8,128)(2,1)} %get-tuple-element.689.refs_0_, ...), custom_call_target="tpu_custom_call" | custom-call | tf_op jit(solution)/shard_map/table_gradient/pallas_call | solution.py:1074
  542.3 27.6 %total_15.1.sums_ref = f32[8,128]{1,0:T(8,128)} custom-call(f32[8,128]{1,0:T(8,128)} %get-tuple-element.693.refs_0_), custom_call_target="tpu_custom_call" | custom-call | tf_op jit(solution)/shard_map/total_15/pallas_call | solution.py:507
  575.0 26.8 %optimizer_step.1 = (f32[2000,768]{1,0:T(8,128)}, f32[96,2304]{1,0:T(8,128)}, f32[96,768]{1,0:T(8,128)}, f32[96,4096]{1,0:T(8,128)}, f32[256,768]{1,0:T(8,128)},...) custom-call(f32[3]{0:T(128)} %pad_maximum_fusion.1.scalar_ref, ...), custom_call_target="tpu_custom_call" | custom-call | tf_op jit(solution)/shard_map/optimizer_step/pallas_call | solution.py:1679
  601.8 13.9 %total_16.1.norm_ref = f32[8,128]{1,0:T(8,128)} custom-call(f32[8,128]{1,0:T(8,128)} %get-tuple-element.700.refs_0_), custom_call_target="tpu_custom_call" | custom-call | tf_op jit(solution)/shard_map/total_16/pallas_call | solution.py:507
  618.2 11.5 %apply_step.1 = (f32[2000,768]{1,0:T(8,128)}, f32[96,2304]{1,0:T(8,128)}, f32[96,768]{1,0:T(8,128)}, f32[96,4096]{1,0:T(8,128)}, f32[256,768]{1,0:T(8,128)}) custom-call(f32[8,128]{1,0:T(8,128)} %total_16.1.norm_ref, f32[2000,768]{1,0:T(8,128)} %refs_0_.1, f32[96,2304]{1,0:T(8,128)} %bitcast.167, f32[96,768]{1,0:T(8,128)} %bitcast.185, ...), custom_call_target="tpu_custom_call" | custom-call | tf_op jit(solution)/shard_map/apply_step/pallas_call | solution.py:1742
  629.7 2.1 copy.104
  (103 shorter events, 36.0 us)
Async XLA Ops:
  1.4 1.6 copy-start.17
  1.6 1.5 copy-start.6
  8.5 3.6 copy-start.1
  8.6 2.6 copy-start
  8.6 3.5 copy-start.2
  8.6 4.3 copy-start.3
  8.6 5.1 copy-start.4
  11.1 3.3 copy-start.18
  11.1 4.0 copy-start.11
  11.1 4.8 copy-start.12
  12.1 142.8 %copy-start.5 = (bf16[512,320]{1,0:T(8,128)(2,1)S(1)}, bf16[512,320]{1,0:T(8,128)(2,1)}, u32[]{:S(2)}) copy-start(bf16[512,320]{1,0:T(8,128)(2,1)} %get-tuple-element.646) | copy-start | bytes 983044
  156.8 2.6 copy-start.9
  156.8 3.7 copy-start.16
  156.8 4.3 slice-start
  237.0 20.3 %copy-start.13 = (f32[2,32,1,512]{3,2,1,0:T(1,128)S(1)}, f32[2,32,1,512]{3,2,1,0:T(1,128)}, u32[]{:S(2)}) copy-start(f32[2,32,1,512]{3,2,1,0:T(1,128)} %get-tuple-element.658) | copy-start | bytes 393220
  531.7 39.7 %copy-start.14 = (f32[2,769,12]{1,0,2:T(2,128)S(1)}, f32[2,769,12]{1,0,2:T(2,128)}, u32[]{:S(2)}) copy-start(f32[2,769,12]{1,0,2:T(2,128)} %param.56) | copy-start | bytes 221476
  531.7 40.9 %copy-start.10 = (f32[2,769,12]{1,0,2:T(2,128)S(1)}, f32[2,769,12]{1,0,2:T(2,128)}, u32[]{:S(2)}) copy-start(f32[2,769,12]{1,0,2:T(2,128)} %param.54) | copy-start | bytes 221476
  531.7 42.1 %copy-start.15 = (f32[2,769,12]{1,0,2:T(2,128)S(1)}, f32[2,769,12]{1,0,2:T(2,128)}, u32[]{:S(2)}) copy-start(f32[2,769,12]{1,0,2:T(2,128)} %param.55) | copy-start | bytes 221476
  618.2 13.6 %copy-start.8 = (f32[2,769,12]{2,1,0:T(8,128)S(1)}, f32[2,769,12]{2,1,0:T(8,128)}, u32[]{:S(2)}) copy-start(f32[2,769,12]{2,1,0:T(8,128)} %get-tuple-element.861) | copy-start | bytes 221476
  618.2 14.5 %copy-start.7 = (f32[2,769,12]{2,1,0:T(8,128)S(1)}, f32[2,769,12]{2,1,0:T(8,128)}, u32[]{:S(2)}) copy-start(f32[2,769,12]{2,1,0:T(8,128)} %get-tuple-element.862) | copy-start | bytes 221476

commit v4 on v3

--- a/solution.py
+++ b/solution.py
@@ -492,7 +492,7 @@
         copies += step_copies
         for a in range(count):
             step_copies[a].wait_recv()
-            summed = held[a][2 * n] + held[a][2 * n + 1]
+            summed = (held[a][2 * n].astype(jnp.float32) + held[a][2 * n + 1].astype(jnp.float32)).astype(held[a].dtype)
             if n + 1 < len(steps):
                 held[a][2 * n + 2] = summed
             else:
@@ -611,19 +611,18 @@
                 copy.wait_send()
         own.wait()
 
-    early = [begin] + [partial(sum_step, n) for n in range(len(steps) + 1)]
+    early = [begin] + [partial(sum_step, n) for n in range(len(steps) + 1) if n_sums]
     return early, [partial(relay, 1, peers)], [finish]
 
 
-def reduce_kernel(count, sections, sums, *refs):
+def reduce_kernel(count, sections, sums, extra, *refs):
     ins, refs = [refs[a * sections : (a + 1) * sections] for a in range(count)], refs[count * sections :]
     sum_in, refs = refs[:sums], refs[sums:]
-    sent = None
-    if sums:
+    if extra:
         sent, refs = refs[0], refs[1:]
     outs, refs = refs[:count], refs[count:]
     sum_out, refs = refs[:sums], refs[sums:]
-    if sums:
+    if extra:
         got, refs = refs[0], refs[1:]
     acc, refs = refs[:count], refs[count:]
     from_core, refs = refs[:count], refs[count:]
@@ -634,7 +633,7 @@
     me = Place()
     nz, ny, nx = me.nz, me.ny, me.sections
     hooks = []
-    if sums:
+    if extra:
         me.greet_group()
         hooks = grads_errand(me, sent, got, sum_in, sum_out, *refs[8 : 8 + sums], *refs[8 + sums :])
     else:
@@ -879,13 +878,13 @@
             DMA((2, peers)),
             DMA((2, peers, nx)),
             DMA((1,)),
-            DMA((2, steps, sums)),
+            DMA((2, steps, max(sums, 1))),
         ]
     return pl.pallas_call(
-        partial(reduce_kernel, count, nx, sums),
+        partial(reduce_kernel, count, nx, sums, bool(errand)),
         out_shape=[jax.ShapeDtypeStruct(g[0].shape[1:], g[0].dtype) for g in grads] + extra_shapes,
-        in_specs=[ANY] * (count * nx) + [VMEM] * sums + [ANY] * bool(sums),
-        out_specs=[VMEM] * (count + sums) + [ANY] * bool(sums),
+        in_specs=[ANY] * (count * nx) + [VMEM] * sums + [ANY] * bool(errand),
+        out_specs=[VMEM] * (count + sums) + [ANY] * bool(errand),
         scratch_shapes=scratch((nx, shards))
         + scratch((nx, shards))
         + scratch((max(nx - 1, 1), shards))
@@ -1380,11 +1379,10 @@
     grad_logit = rising / (1.0 + jnp.exp(logit))
     lane = lax.broadcasted_iota(jnp.int32, grad_logit.shape, 1)
     grad_logit = lower(jnp.where(lane < heads, grad_logit, 0.0))
-    dforget_ref[:, 0:width] = dims_tn(grad_logit, act_a)[0:16, :]
+    dforget_ref[:, 0:width] = lower(dims_tn(grad_logit, act_a)[0:16, :])
     bias = dims_tn(grad_logit, jnp.ones((tree_len, 128), jnp.bfloat16))[0:16, :]
-    dforget_ref[:, width : width + 128] = jnp.where(
-        lax.broadcasted_iota(jnp.int32, (16, 128), 1) == 0, bias, 0.0
-    )
+    bias = jnp.where(lax.broadcasted_iota(jnp.int32, (16, 128), 1) == 0, bias, 0.0)
+    dforget_ref[:, width : width + 128] = lower(bias)
 
     def weigh(n, carry):
         at = pl.ds(pl.multiple_of(n * 256, 256), 256)
@@ -1404,7 +1402,7 @@
     lax.fori_loop(0, 3 * width // 256, gather_back, 0)
     back_a, dgain_a = norm_backward(grad_b[...], normed_a, inverse_a, gain_ref[0:1, :])
     dx_ref[...] = grad_mid + back_a
-    dgain_ref[...] = jnp.concatenate([dgain_a, dgain_b, jnp.zeros((6, width), jnp.float32)], axis=0)
+    dgain_ref[...] = jnp.concatenate([dgain_a, dgain_b], axis=0)
     for copy in stores:
         copy.wait()
 
@@ -1420,8 +1418,8 @@
         partial(backward_kernel, layer, round_input, round_grad),
         out_shape=[
             shape((tree_len, width), f32),
-            shape((16, width + 128), f32),
-            shape((8, width), f32),
+            shape((16, width + 128), b16),
+            shape((2, width), f32),
         ]
         + [shape(w.shape[1:], b16) for w in mats],
         in_specs=[VMEM] * 10 + [ANY] * 5,
@@ -1582,7 +1580,7 @@
                 )
             ]
             work.append((a, at, part, loads, stores))
-    for _, _, _, loads, _ in work:
+    for _, _, _, loads, _ in work[:3]:
         for copy in loads:
             copy.start()
     lane = lax.broadcasted_iota(jnp.int32, (8, 128), 1)
@@ -1591,7 +1589,7 @@
     def scalar_at(values, r, c):
         return jnp.sum(jnp.where((row == r) & (lane == c), values, 0.0))
 
-    smalls = [ref[...] for ref in small_sums]
+    smalls = [ref[...].astype(jnp.float32) for ref in small_sums]
     norm = jnp.sqrt(
         jnp.full((1, 1), scalar_at(sums_ref[...], 0, 0) + sum(square_sum(v) for v in smalls))
     )
@@ -1631,9 +1629,12 @@
     small_norm_ref[...] = table
 
     sums = [[jnp.float32(0), jnp.float32(0)] for _ in range(n)]
-    for a, at, part, loads, stores in work:
+    for p, (a, at, part, loads, stores) in enumerate(work):
         for copy in loads:
             copy.wait()
+        if p + 3 < len(work):
+            for copy in work[p + 3][3]:
+                copy.start()
         g, w, m, v, d = (buf[a].at[pl.ds(at, part)] for buf in (g_buf, w_buf, m_buf, v_buf, d_buf))
         columns = shapes[a][1]
         wide = 256 if columns % 256 == 0 else columns
@@ -1716,12 +1717,15 @@
             ]
             store = pltpu.make_async_copy(w_buf[a].at[rows], outs[a].at[rows], store_sem.at[p])
             work.append((a, at, part, loads, store))
-    for _, _, _, loads, _ in work:
+    for _, _, _, loads, _ in work[:3]:
         for copy in loads:
             copy.start()
-    for a, at, part, loads, store in work:
+    for p, (a, at, part, loads, store) in enumerate(work):
         for copy in loads:
             copy.wait()
+        if p + 3 < len(work):
+            for copy in work[p + 3][3]:
+                copy.start()
         w, d = w_buf[a].at[pl.ds(at, part)], d_buf[a].at[pl.ds(at, part)]
         rate = learn_rate * (norm_at(a, 0) / norm_at(a, 1))
 
@@ -1973,7 +1977,7 @@
     ]
     sent = lower(product(hot, embed_low)).reshape(owners, batch_rows, width)
     small_sums = [forget_0, forget_1, gains_0, gains_1, grad_final[None]]
-    layer_grads, (*small_sums, got_grads) = reduce_parts(stacked, 8, (small_sums, sent))
+    layer_grads, (got_grads,) = reduce_parts(stacked, 8, ([], sent))
     if replicas != 2:
         layer_grads = [lax.psum(g * jnp.bfloat16(0.5), "replica") for g in layer_grads]
     _, head_table = lax.while_loop(lambda s: s[0] < batches, more_grads, (jnp.int32(1), head_table))
@@ -1981,7 +1985,7 @@
         rows_each, asked_all, got_grads.reshape(-1, width), head_table, layer_grads
     )
     layer_grads = [g.reshape(w.shape[1:]) for g, w in zip(layer_grads, layer_weights)]
-    (scalars,) = total([square], 15)
+    scalars, *small_sums = total([square, *small_sums], 15)
     loss_total = loss_sum[0, 0] / pos_all
     count_float = step_count.astype(jnp.float32)
     rates = jnp.stack(

time: 647 us -> 618 us (0.955)
  Pallas kernels: 583 us -> 555 us
    pallas_call x1, Pallas kernels: 164 us -> 144 us  [reduce_shards(): pl.pallas_call(partial(reduce_kernel, count, nx, sums, bool(errand)), out...]
    pallas_call x2, Pallas kernels: 41.5 us -> 32.6 us  [total(): pl.pallas_call(partial(total_kernel, count), out_shape=[jax.ShapeDtypeStr...]
where the time goes in v4:
time: 618 us; the launch traced here: 610 us
  Pallas kernels  555 us (90%)
  local copies, waits for them, and re-layouts  27.4 us (4%)
  other arithmetic  16.3 us (3%)
  matrix products  6.43 us (1%)
    pallas_call x1, Pallas kernels, reduce_shards(): pl.pallas_call(partial(reduce_kernel, count, nx, sums, bool(errand)), out...  144 us
    pallas_call x1, Pallas kernels, gather(): pl.pallas_call(partial(gather_kernel, count, pairs, split, orders, rows_e...  136 us
    pallas_call x2, Pallas kernels, layer_backward(): pl.pallas_call(partial(backward_kernel, layer, round_input, round_grad),...  75.4 us
    pallas_call x2, Pallas kernels, layer_forward(): pl.pallas_call(partial(forward_kernel, layer, round_input), out_shape=[sh...  47.2 us
    pallas_call x3, Pallas kernels, exchange(): pl.pallas_call(partial(exchange_kernel, relay), out_shape=jax.ShapeDtypeS...  44.8 us
    pallas_call x2, Pallas kernels, total(): pl.pallas_call(partial(total_kernel, count), out_shape=[jax.ShapeDtypeStr...  32.6 us
    pallas_call x1, Pallas kernels, optimizer_step(): pl.pallas_call(partial(step_kernel, shapes), out_shape=flat * 3 + [jax.Sh...  26.9 us
    pallas_call x1, Pallas kernels, head_backward(): pl.pallas_call(partial(head_backward_kernel, sections, span, pos_all), ou...  13.1 us

profile of v4, /device:TPU:0, one launch (start us, length us, event | category | flops | bytes accessed | tf_op | source)
XLA Modules:
  0.0 609.7 jit_solution(6327317615327380368)
XLA Ops:
  3.0 2.5 ask_rows.1
  5.5 3.0 convert_element_type.113
  8.6 1.8 pad.48.refs_8_.table_ref
  16.7 136.1 %gather_2.1 = (bf16[2,8,2,48,2304]{4,3,2,1,0:T(8,128)(2,1)}, bf16[2,8,2,48,768]{4,3,2,1,0:T(8,128)(2,1)}, bf16[2,8,2,48,4096]{4,3,2,1,0:T(8,128)(2,1)}, bf16[2,8...) custom-call(bf16[2,48,2304]{2,1,0:T(8,128)(2,1)} %bitcast.187, ...), custom_call_target="tpu_custom_call" | custom-call | tf_op jit(solution)/shard_map/gather_2/pallas_call | solution.py:369
  154.9 1.6 fusion.73
  162.6 23.5 %forward_0.1 = (f32[320,768]{1,0:T(8,128)}, bf16[320,2304]{1,0:T(8,128)(2,1)}, f32[320,128]{1,0:T(8,128)}, f32[320,128]{1,0:T(8,128)}, bf16[320,768]{1,0:T(8,128...) custom-call(f32[320,768]{1,0:T(8,128)S(1)} %get-tuple-element.649.x_ref, bf16[320,320]{1,0:T(8,128)(2,1)} %fusion.21.allowed_ref, ...), custom_call_target="tpu_custom_call" | custom-call | tf_op jit(solution)/shard_map/forward_0/pallas_call | solution.py:1233
  186.7 23.7 %forward_1.1 = (f32[320,768]{1,0:T(8,128)}, bf16[320,2304]{1,0:T(8,128)(2,1)}, f32[320,128]{1,0:T(8,128)}, f32[320,128]{1,0:T(8,128)}, bf16[320,768]{1,0:T(8,128...) custom-call(f32[320,768]{1,0:T(8,128)} %get-tuple-element.654.x_ref, bf16[320,320]{1,0:T(8,128)(2,1)} %fusion.21.allowed_ref, ...), custom_call_target="tpu_custom_call" | custom-call | tf_op jit(solution)/shard_map/forward_1/pallas_call | solution.py:1233
  211.2 1.8 gather_fusion
  214.6 20.3 %exchange_3.1 = bf16[2,16,16,768]{3,2,1,0:T(8,128)(2,1)} custom-call(bf16[1,16,768]{2,1,0:T(8,128)(2,1)} %fusion.37.src_ref), custom_call_target="tpu_custom_call" | custom-call | tf_op jit(solution)/shard_map/exchange_3/pallas_call | solution.py:444
  234.9 2.1 copy.97
  237.0 10.6 %head_forward.1 = (f32[512,2048]{1,0:T(8,128)}, f32[4,512]{1,0:T(4,128)}) custom-call(bf16[512,768]{1,0:T(8,128)(2,1)} %bitcast.170, bf16[2048,768]{1,0:T(8,128)(2,1)} %pad.48.refs_8_.table_ref, f32[512,2048]{1,0:T(8,128)} %get-tuple-element.656.marks_ref), custom_call_target="tpu_custom_call" | custom-call | tf_op jit(solution)/shard_map/head_forward/pallas_call | solution.py:1468
  247.6 9.6 %exchange_4.1 = f32[1,16,4,512]{3,2,1,0:T(4,128)} custom-call(f32[1,4,512]{2,1,0:T(4,128)} %bitcast.209), custom_call_target="tpu_custom_call" | custom-call | tf_op jit(solution)/shard_map/exchange_4/pallas_call | solution.py:444
  258.4 13.1 %head_backward.1 = (bf16[256,768]{1,0:T(8,128)(2,1)}, f32[2048,768]{1,0:T(8,128)}, f32[8,128]{1,0:T(8,128)}) custom-call(bf16[512,768]{1,0:T(8,128)(2,1)} %bitcast.171, bf16[2048,768]{1,0:T(8,128)(2,1)} %pad.48.refs_8_.table_ref, f32[512,2048]{1,0:T(8,128)} %get-tuple-element.656.marks_ref, f32[512,2048]{1,0:T(8,128)} %get-tuple-element.657.logits_ref, ...), custom_call_target="tpu_custom_call" | custom-call | tf_op jit(solution)/shard_map/head_backward/pallas_call | solution.py:1509
  271.5 14.8 %exchange_5.1 = bf16[1,16,16,768]{3,2,1,0:T(8,128)(2,1)} custom-call(bf16[16,16,768]{2,1,0:T(8,128)(2,1)} %bitcast.205), custom_call_target="tpu_custom_call" | custom-call | tf_op jit(solution)/shard_map/exchange_5/pallas_call | solution.py:444
  288.1 1.6 fusion.38.dy_ref
  289.7 37.7 %backward_1.1 = (f32[320,768]{1,0:T(8,128)}, bf16[16,896]{1,0:T(8,128)(2,1)}, f32[2,768]{1,0:T(2,128)}, bf16[768,2304]{1,0:T(8,128)(2,1)}, bf16[768,768]{1,0:T(8...) custom-call(f32[320,768]{1,0:T(8,128)} %fusion.38.dy_ref, f32[320,768]{1,0:T(8,128)} %get-tuple-element.654.x_ref, ...), custom_call_target="tpu_custom_call" | custom-call | tf_op jit(solution)/shard_map/backward_1/pallas_call | solution.py:1417
  327.4 37.7 %backward_0.1 = (f32[320,768]{1,0:T(8,128)}, bf16[16,896]{1,0:T(8,128)(2,1)}, f32[2,768]{1,0:T(2,128)}, bf16[768,2304]{1,0:T(8,128)(2,1)}, bf16[768,768]{1,0:T(8...) custom-call(f32[320,768]{1,0:T(8,128)} %get-tuple-element.667.dy_ref, ...), custom_call_target="tpu_custom_call" | custom-call | tf_op jit(solution)/shard_map/backward_0/pallas_call | solution.py:1417
  368.1 143.5 %reduce_8.1 = (bf16[2,48,2304]{2,1,0:T(8,128)(2,1)}, bf16[2,48,768]{2,1,0:T(8,128)(2,1)}, bf16[2,48,4096]{2,1,0:T(8,128)(2,1)}, bf16[2,128,768]{2,1,0:T(8,128)(2,1)}, bf16[2,16,32,768]{3,2,1,0:T(8,128)(2,1)}) custom-call(bf16[8,2,48,2304]{3,2,1,0:T(8,128)(2,1)} %bitcast.177, bf16[8,2,48,2304]{3,2,1,0:T(8,128)(2,1)} %bitcast.176, ...), custom_call_target="tpu_custom_call" | custom-call | tf_op jit(solution)/shard_map/reduce_8/pallas_call | solution.py:883
  511.6 10.6 %table_gradient.1 = (f32[2000,768]{1,0:T(8,128)}, f32[8,128]{1,0:T(8,128)}) custom-call(s32[2,16,1,128]{3,2,1,0:T(1,128)} %get-tuple-element.646.asked_ref, bf16[1024,768]{1,0:T(8,128)(2,1)} %bitcast.193, f32[2048,768]{1,0:T(8,128)} %get-tuple-element.685.head_ref, bf16[2,48,2304]{2,1,0:T(8,128)(2,1)} %get-tuple-element.686.refs_0_, ...), custom_call_target="tpu_custom_call" | custom-call | tf_op jit(solution)/shard_map/table_gradient/pallas_call | solution.py:1073
  522.8 19.9 %total_15.1 = (f32[8,128]{1,0:T(8,128)}, bf16[16,896]{1,0:T(8,128)(2,1)}, bf16[16,896]{1,0:T(8,128)(2,1)}, f32[2,768]{1,0:T(2,128)}, f32[2,768]{1,0:T(2,128)}, /*index=5*/f32[1,768]{1,0:T(1,128)}) custom-call(f32[8,128]{1,0:T(8,128)} %get-tuple-element.690.refs_0_, bf16[16,896]{1,0:T(8,128)(2,1)} %get-tuple-element.691.refs_1_, ...), custom_call_target="tpu_custom_call" | custom-call | tf_op jit(solution)/shard_map/total_15/pallas_call | solution.py:507
  547.8 26.9 %optimizer_step.1 = (f32[2000,768]{1,0:T(8,128)}, f32[96,2304]{1,0:T(8,128)}, f32[96,768]{1,0:T(8,128)}, f32[96,4096]{1,0:T(8,128)}, f32[256,768]{1,0:T(8,128)},...) custom-call(f32[3]{0:T(128)} %pad_maximum_fusion.1.scalar_ref, ...), custom_call_target="tpu_custom_call" | custom-call | tf_op jit(solution)/shard_map/optimizer_step/pallas_call | solution.py:1680
  574.7 12.6 %total_16.1.norm_ref = f32[8,128]{1,0:T(8,128)} custom-call(f32[8,128]{1,0:T(8,128)} %get-tuple-element.702.refs_0_), custom_call_target="tpu_custom_call" | custom-call | tf_op jit(solution)/shard_map/total_16/pallas_call | solution.py:507
  589.8 11.7 %apply_step.1 = (f32[2000,768]{1,0:T(8,128)}, f32[96,2304]{1,0:T(8,128)}, f32[96,768]{1,0:T(8,128)}, f32[96,4096]{1,0:T(8,128)}, f32[256,768]{1,0:T(8,128)}) custom-call(f32[8,128]{1,0:T(8,128)} %total_16.1.norm_ref, f32[2000,768]{1,0:T(8,128)} %refs_0_.1, f32[96,2304]{1,0:T(8,128)} %bitcast.167, f32[96,768]{1,0:T(8,128)} %bitcast.185, ...), custom_call_target="tpu_custom_call" | custom-call | tf_op jit(solution)/shard_map/apply_step/pallas_call | solution.py:1746
  601.4 2.1 copy.104
  (105 shorter events, 36.3 us)
Async XLA Ops:
  1.4 1.6 copy-start.17
  1.6 1.5 copy-start.6
  8.5 3.6 copy-start.1
  8.6 2.6 copy-start
  8.6 3.5 copy-start.2
  8.6 4.3 copy-start.3
  8.6 5.1 copy-start.4
  11.1 3.3 copy-start.19
  11.1 4.0 copy-start.11
  11.1 4.8 copy-start.12
  12.1 142.8 %copy-start.5 = (bf16[512,320]{1,0:T(8,128)(2,1)S(1)}, bf16[512,320]{1,0:T(8,128)(2,1)}, u32[]{:S(2)}) copy-start(bf16[512,320]{1,0:T(8,128)(2,1)} %get-tuple-element.647) | copy-start | bytes 983044
  156.7 2.6 copy-start.9
  156.7 3.7 copy-start.16
  156.7 4.3 slice-start
  237.0 20.3 %copy-start.13 = (f32[2,32,1,512]{3,2,1,0:T(1,128)S(1)}, f32[2,32,1,512]{3,2,1,0:T(1,128)}, u32[]{:S(2)}) copy-start(f32[2,32,1,512]{3,2,1,0:T(1,128)} %get-tuple-element.659) | copy-start | bytes 393220
  511.6 10.7 %copy-start.18 = (f32[768]{0:T(1024)S(1)}, f32[768]{0:T(1024)}, u32[]{:S(2)}) copy-start(f32[768]{0:T(1024)} %get-tuple-element.871) | copy-start | bytes 9220
  511.6 32.6 %copy-start.14 = (f32[2,769,12]{1,0,2:T(2,128)S(1)}, f32[2,769,12]{1,0,2:T(2,128)}, u32[]{:S(2)}) copy-start(f32[2,769,12]{1,0,2:T(2,128)} %param.56) | copy-start | bytes 221476
  511.6 33.8 %copy-start.10 = (f32[2,769,12]{1,0,2:T(2,128)S(1)}, f32[2,769,12]{1,0,2:T(2,128)}, u32[]{:S(2)}) copy-start(f32[2,769,12]{1,0,2:T(2,128)} %param.54) | copy-start | bytes 221476
  511.6 35.0 %copy-start.15 = (f32[2,769,12]{1,0,2:T(2,128)S(1)}, f32[2,769,12]{1,0,2:T(2,128)}, u32[]{:S(2)}) copy-start(f32[2,769,12]{1,0,2:T(2,128)} %param.55) | copy-start | bytes 221476
  589.8 13.7 %copy-start.8 = (f32[2,769,12]{2,1,0:T(8,128)S(1)}, f32[2,769,12]{2,1,0:T(8,128)}, u32[]{:S(2)}) copy-start(f32[2,769,12]{2,1,0:T(8,128)} %get-tuple-element.863) | copy-start | bytes 221476
  589.8 14.7 %copy-start.7 = (f32[2,769,12]{2,1,0:T(8,128)S(1)}, f32[2,769,12]{2,1,0:T(8,128)}, u32[]{:S(2)}) copy-start(f32[2,769,12]{2,1,0:T(8,128)} %get-tuple-element.864) | copy-start | bytes 221476

commit v5 on v4

--- a/solution.py
+++ b/solution.py
@@ -1182,7 +1182,7 @@
         att_ref[:, pl.ds(base, 128)] = lower(jnp.where(pair.lane < 64, outs[0], outs[1]))
         return carry
 
-    lax.fori_loop(0, heads // 2, attend, 0)
+    lax.fori_loop(0, heads // 2, attend, 0, unroll=2)
     loads[1].wait()
     middle = x + product(att_ref[...], b_out[...])
     mid_ref[...] = middle
@@ -1853,7 +1853,6 @@
     owners = replicas * shards
     owner_id = replica_id * shards + shard_id
     own_tree = section_id * shards + shard_id
-    table_low = lower(embed_table)
 
     def own_row(values):
         return lax.dynamic_index_in_dim(values, own_tree, 0, keepdims=False)
@@ -1895,7 +1894,7 @@
         own_pick = lax.dynamic_index_in_dim(
             pick.reshape(sections, owners * batch_rows, rows_each), section_id, 0, keepdims=False
         )
-        sent = lower(product(own_pick, table_low)).reshape(owners, batch_rows, width)
+        sent = lower(product(own_pick, table_wide[:rows_each])).reshape(owners, batch_rows, width)
         got_more = exchange(sent, 1)[0].reshape(owners * batch_rows, width)
         return (batch + 1, total_rows + product_left(hot_more, got_more))
 
@@ -1911,7 +1910,7 @@
         return lower(weight).reshape(2, weight.shape[1] // 2, weight.shape[2])
 
     width_all = -(-rows_each // 128) * 128
-    table_wide = jnp.pad(table_low, ((0, width_all - rows_each), (0, 0)))
+    table_wide = lower(jnp.pad(embed_table, ((0, width_all - rows_each), (0, 0))))
     layer_weights = (attention_in, attention_out, feedforward_in, feedforward_out)
     entries = 8 * teacher_index.shape[2]
     group_data = [

time: 618 us -> 616 us (level)
  no operation moved by 1% of the time
where the time goes in v5:
time: 616 us; the launch traced here: 608 us
  Pallas kernels  552 us (90%)
  local copies, waits for them, and re-layouts  28 us (5%)
  other arithmetic  16.4 us (3%)
  matrix products  6.43 us (1%)
    pallas_call x1, Pallas kernels, reduce_shards(): pl.pallas_call(partial(reduce_kernel, count, nx, sums, bool(errand)), out...  144 us
    pallas_call x1, Pallas kernels, gather(): pl.pallas_call(partial(gather_kernel, count, pairs, split, orders, rows_e...  135 us
    pallas_call x2, Pallas kernels, layer_backward(): pl.pallas_call(partial(backward_kernel, layer, round_input, round_grad),...  75.3 us
    pallas_call x2, Pallas kernels, layer_forward(): pl.pallas_call(partial(forward_kernel, layer, round_input), out_shape=[sh...  45.7 us
    pallas_call x3, Pallas kernels, exchange(): pl.pallas_call(partial(exchange_kernel, relay), out_shape=jax.ShapeDtypeS...  44.8 us
    pallas_call x2, Pallas kernels, total(): pl.pallas_call(partial(total_kernel, count), out_shape=[jax.ShapeDtypeStr...  32.6 us
    pallas_call x1, Pallas kernels, optimizer_step(): pl.pallas_call(partial(step_kernel, shapes), out_shape=flat * 3 + [jax.Sh...  26.9 us
    pallas_call x1, Pallas kernels, head_backward(): pl.pallas_call(partial(head_backward_kernel, sections, span, pos_all), ou...  12.7 us

profile of v5, /device:TPU:0, one launch (start us, length us, event | category | flops | bytes accessed | tf_op | source)
XLA Modules:
  0.0 607.7 jit_solution(16511707202152822327)
XLA Ops:
  3.0 2.5 ask_rows.1
  5.5 3.0 convert.7
  14.1 1.7 reshape.520.refs_4_
  15.7 1.7 reshape.521.refs_5_
  17.4 135.4 %gather_2.1 = (bf16[2,8,2,48,2304]{4,3,2,1,0:T(8,128)(2,1)}, bf16[2,8,2,48,768]{4,3,2,1,0:T(8,128)(2,1)}, bf16[2,8,2,48,4096]{4,3,2,1,0:T(8,128)(2,1)}, bf16[2,8...) custom-call(bf16[2,48,2304]{2,1,0:T(8,128)(2,1)} %bitcast.184, ...), custom_call_target="tpu_custom_call" | custom-call | tf_op jit(solution)/shard_map/gather_2/pallas_call | solution.py:369
  162.6 22.7 %forward_0.1 = (f32[320,768]{1,0:T(8,128)}, bf16[320,2304]{1,0:T(8,128)(2,1)}, f32[320,128]{1,0:T(8,128)}, f32[320,128]{1,0:T(8,128)}, bf16[320,768]{1,0:T(8,128...) custom-call(f32[320,768]{1,0:T(8,128)S(1)} %get-tuple-element.649.x_ref, bf16[320,320]{1,0:T(8,128)(2,1)} %fusion.24.allowed_ref, ...), custom_call_target="tpu_custom_call" | custom-call | tf_op jit(solution)/shard_map/forward_0/pallas_call | solution.py:1233
  186.0 22.9 %forward_1.1 = (f32[320,768]{1,0:T(8,128)}, bf16[320,2304]{1,0:T(8,128)(2,1)}, f32[320,128]{1,0:T(8,128)}, f32[320,128]{1,0:T(8,128)}, bf16[320,768]{1,0:T(8,128...) custom-call(f32[320,768]{1,0:T(8,128)} %get-tuple-element.654.x_ref, bf16[320,320]{1,0:T(8,128)(2,1)} %fusion.24.allowed_ref, ...), custom_call_target="tpu_custom_call" | custom-call | tf_op jit(solution)/shard_map/forward_1/pallas_call | solution.py:1233
  209.7 1.8 gather_fusion
  213.1 20.3 %exchange_3.1 = bf16[2,16,16,768]{3,2,1,0:T(8,128)(2,1)} custom-call(bf16[1,16,768]{2,1,0:T(8,128)(2,1)} %fusion.40.src_ref), custom_call_target="tpu_custom_call" | custom-call | tf_op jit(solution)/shard_map/exchange_3/pallas_call | solution.py:444
  233.4 2.1 copy.97
  235.5 10.6 %head_forward.1 = (f32[512,2048]{1,0:T(8,128)}, f32[4,512]{1,0:T(4,128)}) custom-call(bf16[512,768]{1,0:T(8,128)(2,1)} %bitcast.167, bf16[2048,768]{1,0:T(8,128)(2,1)} %get-tuple-element.1124, f32[512,2048]{1,0:T(8,128)} %get-tuple-element.656.marks_ref), custom_call_target="tpu_custom_call" | custom-call | tf_op jit(solution)/shard_map/head_forward/pallas_call | solution.py:1468
  246.1 9.6 %exchange_4.1 = f32[1,16,4,512]{3,2,1,0:T(4,128)} custom-call(f32[1,4,512]{2,1,0:T(4,128)} %bitcast.206), custom_call_target="tpu_custom_call" | custom-call | tf_op jit(solution)/shard_map/exchange_4/pallas_call | solution.py:444
  256.9 12.7 %head_backward.1 = (bf16[256,768]{1,0:T(8,128)(2,1)}, f32[2048,768]{1,0:T(8,128)}, f32[8,128]{1,0:T(8,128)}) custom-call(bf16[512,768]{1,0:T(8,128)(2,1)} %bitcast.168, bf16[2048,768]{1,0:T(8,128)(2,1)} %get-tuple-element.1124, f32[512,2048]{1,0:T(8,128)} %get-tuple-element.656.marks_ref, f32[512,2048]{1,0:T(8,128)} %get-tuple-element.657.logits_ref, ...), custom_call_target="tpu_custom_call" | custom-call | tf_op jit(solution)/shard_map/head_backward/pallas_call | solution.py:1509
  269.5 14.8 %exchange_5.1 = bf16[1,16,16,768]{3,2,1,0:T(8,128)(2,1)} custom-call(bf16[16,16,768]{2,1,0:T(8,128)(2,1)} %bitcast.202), custom_call_target="tpu_custom_call" | custom-call | tf_op jit(solution)/shard_map/exchange_5/pallas_call | solution.py:444
  286.1 1.6 fusion.41.dy_ref
  287.8 37.7 %backward_1.1 = (f32[320,768]{1,0:T(8,128)}, bf16[16,896]{1,0:T(8,128)(2,1)}, f32[2,768]{1,0:T(2,128)}, bf16[768,2304]{1,0:T(8,128)(2,1)}, bf16[768,768]{1,0:T(8...) custom-call(f32[320,768]{1,0:T(8,128)} %fusion.41.dy_ref, f32[320,768]{1,0:T(8,128)} %get-tuple-element.654.x_ref, ...), custom_call_target="tpu_custom_call" | custom-call | tf_op jit(solution)/shard_map/backward_1/pallas_call | solution.py:1417
  325.5 37.5 %backward_0.1 = (f32[320,768]{1,0:T(8,128)}, bf16[16,896]{1,0:T(8,128)(2,1)}, f32[2,768]{1,0:T(2,128)}, bf16[768,2304]{1,0:T(8,128)(2,1)}, bf16[768,768]{1,0:T(8...) custom-call(f32[320,768]{1,0:T(8,128)} %get-tuple-element.667.dy_ref, ...), custom_call_target="tpu_custom_call" | custom-call | tf_op jit(solution)/shard_map/backward_0/pallas_call | solution.py:1417
  366.0 143.5 %reduce_8.1 = (bf16[2,48,2304]{2,1,0:T(8,128)(2,1)}, bf16[2,48,768]{2,1,0:T(8,128)(2,1)}, bf16[2,48,4096]{2,1,0:T(8,128)(2,1)}, bf16[2,128,768]{2,1,0:T(8,128)(2,1)}, bf16[2,16,32,768]{3,2,1,0:T(8,128)(2,1)}) custom-call(bf16[8,2,48,2304]{3,2,1,0:T(8,128)(2,1)} %bitcast.174, bf16[8,2,48,2304]{3,2,1,0:T(8,128)(2,1)} %bitcast.173, ...), custom_call_target="tpu_custom_call" | custom-call | tf_op jit(solution)/shard_map/reduce_8/pallas_call | solution.py:883
  509.5 10.6 %table_gradient.1 = (f32[2000,768]{1,0:T(8,128)}, f32[8,128]{1,0:T(8,128)}) custom-call(s32[2,16,1,128]{3,2,1,0:T(1,128)} %get-tuple-element.646.asked_ref, bf16[1024,768]{1,0:T(8,128)(2,1)} %bitcast.190, f32[2048,768]{1,0:T(8,128)} %get-tuple-element.685.head_ref, bf16[2,48,2304]{2,1,0:T(8,128)(2,1)} %get-tuple-element.686.refs_0_, ...), custom_call_target="tpu_custom_call" | custom-call | tf_op jit(solution)/shard_map/table_gradient/pallas_call | solution.py:1073
  520.7 19.9 %total_15.1 = (f32[8,128]{1,0:T(8,128)}, bf16[16,896]{1,0:T(8,128)(2,1)}, bf16[16,896]{1,0:T(8,128)(2,1)}, f32[2,768]{1,0:T(2,128)}, f32[2,768]{1,0:T(2,128)}, /*index=5*/f32[1,768]{1,0:T(1,128)}) custom-call(f32[8,128]{1,0:T(8,128)} %get-tuple-element.690.refs_0_, bf16[16,896]{1,0:T(8,128)(2,1)} %get-tuple-element.691.refs_1_, ...), custom_call_target="tpu_custom_call" | custom-call | tf_op jit(solution)/shard_map/total_15/pallas_call | solution.py:507
  545.7 26.9 %optimizer_step.1 = (f32[2000,768]{1,0:T(8,128)}, f32[96,2304]{1,0:T(8,128)}, f32[96,768]{1,0:T(8,128)}, f32[96,4096]{1,0:T(8,128)}, f32[256,768]{1,0:T(8,128)},...) custom-call(f32[3]{0:T(128)} %pad_maximum_fusion.1.scalar_ref, ...), custom_call_target="tpu_custom_call" | custom-call | tf_op jit(solution)/shard_map/optimizer_step/pallas_call | solution.py:1680
  572.6 12.7 %total_16.1.norm_ref = f32[8,128]{1,0:T(8,128)} custom-call(f32[8,128]{1,0:T(8,128)} %get-tuple-element.702.refs_0_), custom_call_target="tpu_custom_call" | custom-call | tf_op jit(solution)/shard_map/total_16/pallas_call | solution.py:507
  587.7 11.7 %apply_step.1 = (f32[2000,768]{1,0:T(8,128)}, f32[96,2304]{1,0:T(8,128)}, f32[96,768]{1,0:T(8,128)}, f32[96,4096]{1,0:T(8,128)}, f32[256,768]{1,0:T(8,128)}) custom-call(f32[8,128]{1,0:T(8,128)} %total_16.1.norm_ref, f32[2000,768]{1,0:T(8,128)} %refs_0_.1, f32[96,2304]{1,0:T(8,128)} %bitcast.164, f32[96,768]{1,0:T(8,128)} %bitcast.182, ...), custom_call_target="tpu_custom_call" | custom-call | tf_op jit(solution)/shard_map/apply_step/pallas_call | solution.py:1746
  599.4 2.1 copy.104
  (101 shorter events, 37.2 us)
Async XLA Ops:
  1.4 1.6 copy-start.15
  1.6 1.5 copy-start.6
  8.5 1.4 copy-start.1
  8.6 2.5 copy-start.2
  8.6 3.3 copy-start.3
  8.6 4.0 copy-start.4
  9.9 142.8 %copy-start = (bf16[2048,768]{1,0:T(8,128)(2,1)}, bf16[2048,768]{1,0:T(8,128)(2,1)S(1)}, u32[]{:S(2)}) copy-start(bf16[2048,768]{1,0:T(8,128)(2,1)S(1)} %pad.49.refs_8_.table_ref) | copy-start | bytes 9437188
  10.0 3.3 copy-start.17
  11.0 143.9 %copy-start.5 = (bf16[512,320]{1,0:T(8,128)(2,1)S(1)}, bf16[512,320]{1,0:T(8,128)(2,1)}, u32[]{:S(2)}) copy-start(bf16[512,320]{1,0:T(8,128)(2,1)} %get-tuple-element.647) | copy-start | bytes 983044
  156.8 2.6 copy-start.9
  156.8 3.7 copy-start.14
  156.8 4.3 slice-start
  235.5 20.3 %copy-start.11 = (f32[2,32,1,512]{3,2,1,0:T(1,128)S(1)}, f32[2,32,1,512]{3,2,1,0:T(1,128)}, u32[]{:S(2)}) copy-start(f32[2,32,1,512]{3,2,1,0:T(1,128)} %get-tuple-element.659) | copy-start | bytes 393220
  509.5 10.7 %copy-start.16 = (f32[768]{0:T(1024)S(1)}, f32[768]{0:T(1024)}, u32[]{:S(2)}) copy-start(f32[768]{0:T(1024)} %get-tuple-element.871) | copy-start | bytes 9220
  509.5 32.6 %copy-start.12 = (f32[2,769,12]{1,0,2:T(2,128)S(1)}, f32[2,769,12]{1,0,2:T(2,128)}, u32[]{:S(2)}) copy-start(f32[2,769,12]{1,0,2:T(2,128)} %param.56) | copy-start | bytes 221476
  509.5 33.8 %copy-start.10 = (f32[2,769,12]{1,0,2:T(2,128)S(1)}, f32[2,769,12]{1,0,2:T(2,128)}, u32[]{:S(2)}) copy-start(f32[2,769,12]{1,0,2:T(2,128)} %param.54) | copy-start | bytes 221476
  509.5 35.0 %copy-start.13 = (f32[2,769,12]{1,0,2:T(2,128)S(1)}, f32[2,769,12]{1,0,2:T(2,128)}, u32[]{:S(2)}) copy-start(f32[2,769,12]{1,0,2:T(2,128)} %param.55) | copy-start | bytes 221476
  587.7 13.7 %copy-start.8 = (f32[2,769,12]{2,1,0:T(8,128)S(1)}, f32[2,769,12]{2,1,0:T(8,128)}, u32[]{:S(2)}) copy-start(f32[2,769,12]{2,1,0:T(8,128)} %get-tuple-element.863) | copy-start | bytes 221476
  587.7 14.7 %copy-start.7 = (f32[2,769,12]{2,1,0:T(8,128)S(1)}, f32[2,769,12]{2,1,0:T(8,128)}, u32[]{:S(2)}) copy-start(f32[2,769,12]{2,1,0:T(8,128)} %get-tuple-element.864) | copy-start | bytes 221476
